TPU v7x, 32 devices: a whole 2x2x4 slice. The times are simulated.
32 devices in a mesh: dp: 8 (over z, x), fsdp: 4 (over y, core).
Axes of the slice: x: 2, y: 2, z: 4, core: 2. Of those that a mesh axis runs over, the one named last changes fastest.
Arguments:
- hidden: bfloat16 [16384, 1536], P(('dp', 'fsdp')), may hold values from -6 to 6
- cotangent: bfloat16 [16384, 1536], P(('dp', 'fsdp')), may hold values from -6 to 6
- lengths: int32 [32], P(('dp', 'fsdp')), may hold values from 1 to 512, 12288 in all
- norm_gain: bfloat16 [1536], P(('dp', 'fsdp')), may hold values from 0.5 to 1.5
- in_proj: bfloat16 [1536, 6400], P(('dp', 'fsdp')), may hold values from -0.15625 to 0.15625
- dt_proj: bfloat16 [1536, 48], P(('dp', 'fsdp')), may hold values from -0.15625 to 0.15625
- conv_weight: bfloat16 [4, 3328], P(None, ('dp', 'fsdp')), may hold values from -3 to 3
- conv_bias: bfloat16 [3328], P(('dp', 'fsdp')), may hold values from -3 to 3
- dt_bias: bfloat16 [48], replicated, may hold values from -6 to -3
- a_log: bfloat16 [48], replicated, may hold values from 0 to 2.5
- skip_gain: bfloat16 [48], replicated, may hold values from 0.5 to 1.5
- gate_gain: bfloat16 [3072], P(('dp', 'fsdp')), may hold values from 0.5 to 1.5
- out_proj: bfloat16 [3072, 1536], P(('dp', 'fsdp')), may hold values from -0.109375 to 0.109375
Outputs:
- output: bfloat16 [16384, 1536], P(('dp', 'fsdp'))
- input_grad: float32 [16384, 1536], P(('dp', 'fsdp'))
- grad_norm_gain: float32 [1536], P(('dp', 'fsdp'))
- grad_in_proj: float32 [1536, 6400], P(('dp', 'fsdp'))
- grad_dt_proj: float32 [1536, 48], P(('dp', 'fsdp'))
- grad_conv_weight: float32 [4, 3328], P(None, ('dp', 'fsdp'))
- grad_conv_bias: float32 [3328], P(('dp', 'fsdp'))
- grad_dt_bias: float32 [48], replicated
- grad_a_log: float32 [48], replicated
- grad_skip_gain: float32 [48], replicated
- grad_gate_gain: float32 [3072], P(('dp', 'fsdp'))
- grad_out_proj: float32 [3072, 1536], P(('dp', 'fsdp'))
Inputs may be any that keep to these rules, and one draw needn't show every extreme that they name: `lengths`: each slot has 1 to 512 live tokens, the longest slot is full, and all slots hold 12288 live tokens together.
All inputs are finite; a program needn't handle non-finite values. No bound on the sum of `lengths` on one device may be relied on, other than what follows from the above.
Results may differ from a plain program's by a relative error of at most 0.0078.
Values may be sent and summed in bfloat16 or wider, within the bound.
A program may use at most 320 MiB of HBM per device.

v0:
```python
from functools import partial

import jax
import jax.numpy as jnp
from jax import lax
from jax.sharding import PartitionSpec as P

SPAN = 256


highest = lax.Precision.HIGHEST
epsilon = 1e-05


def pre_norm(row_values, gain_values):
    inverse = lax.rsqrt(jnp.mean(row_values * row_values, axis=1, keepdims=True) + epsilon)
    return row_values * inverse * gain_values[None, :]


def state_space(values, step_size, log_decay, input_keys, read_keys, span_len):
    length, head_count, head_dim = values.shape
    blocks = length // span_len
    scaled = (values * step_size[:, :, None]).reshape(blocks, span_len, head_count, head_dim)
    scaled = jnp.transpose(scaled, (0, 2, 1, 3))
    decays = jnp.transpose(log_decay.reshape(blocks, span_len, head_count), (0, 2, 1))
    summed = jnp.cumsum(decays, axis=2)
    in_keys = input_keys.reshape(blocks, span_len, -1)
    out_keys = read_keys.reshape(blocks, span_len, -1)
    scores = jnp.einsum("kin,kjn->kij", out_keys, in_keys, precision=highest)
    causal = jnp.arange(span_len)[:, None] >= jnp.arange(span_len)[None, :]
    spread = summed[:, :, :, None] - summed[:, :, None, :]
    decay_matrix = jnp.where(causal, jnp.exp(jnp.where(causal, spread, 0.0)), 0.0)
    mixing = decay_matrix * scores[:, None, :, :]
    inner_part = jnp.einsum("khij,khjp->khip", mixing, scaled, precision=highest)
    ending = summed[:, :, -1]
    tail_decay = jnp.exp(ending[:, :, None] - summed)
    states = jnp.einsum(
        "kjn,khjp->khpn", in_keys, scaled * tail_decay[:, :, :, None], precision=highest
    )

    def advance(carried, inputs):
        block_state, block_end = inputs
        return (jnp.exp(block_end)[:, None, None] * carried + block_state, carried)

    _, entering = lax.scan(advance, jnp.zeros(states.shape[1:], states.dtype), (states, ending))
    outer_part = (
        jnp.einsum("kin,khpn->khip", out_keys, entering, precision=highest)
        * jnp.exp(summed)[:, :, :, None]
    )
    result = jnp.transpose(inner_part + outer_part, (0, 2, 1, 3))
    return result.reshape(length, head_count, head_dim)


def mixer_block(projected, dt_raw, conv_w, conv_b, dt_shift, a_log, skip_gain, gate_gain, span_len):
    length = projected.shape[0]
    inner_width = gate_gain.shape[0]
    head_count = dt_shift.shape[0]
    state_dim = (projected.shape[1] - 2 * inner_width) // 2
    gate_part = projected[:, :inner_width]
    raw_part = projected[:, inner_width:]
    kernel = conv_w.shape[0]
    padded = jnp.pad(raw_part, ((kernel - 1, 0), (0, 0)))
    conv_out = conv_b[None, :] + conv_w[kernel - 1][None, :] * raw_part
    for offset in range(kernel - 1):
        conv_out = conv_out + conv_w[offset][None, :] * padded[offset : offset + length]
    active = jax.nn.silu(conv_out)
    values = active[:, :inner_width].reshape(length, head_count, inner_width // head_count)
    input_keys = active[:, inner_width : inner_width + state_dim]
    read_keys = active[:, inner_width + state_dim :]
    step_size = jax.nn.softplus(dt_raw + dt_shift[None, :])
    log_decay = -step_size * jnp.exp(a_log)[None, :]
    mixed_out = (
        state_space(values, step_size, log_decay, input_keys, read_keys, span_len)
        + skip_gain[None, :, None] * values
    )
    product = mixed_out.reshape(length, inner_width) * jax.nn.silu(gate_part)
    return pre_norm(product, gate_gain)


def row_dot(left, right):
    return lax.dot_general(
        left, right, (((0,), (0,)), ((), ())), preferred_element_type=jnp.float32
    )


def back_dot(left, weight):
    return lax.dot_general(
        left, weight, (((1,), (1,)), ((), ())), preferred_element_type=jnp.float32
    )


def shards(
    hidden,
    cotangent,
    lengths,
    norm_gain,
    in_proj,
    dt_proj,
    conv_weight,
    conv_bias,
    dt_bias,
    a_log,
    skip_gain,
    gate_gain,
    out_proj,
):
    gathered = (
        lax.all_gather(norm_gain, ("dp", "fsdp"), axis=0, tiled=True),
        lax.all_gather(in_proj, ("dp", "fsdp"), axis=0, tiled=True),
        lax.all_gather(dt_proj, ("dp", "fsdp"), axis=0, tiled=True),
        lax.all_gather(conv_weight, ("dp", "fsdp"), axis=1, tiled=True),
        lax.all_gather(conv_bias, ("dp", "fsdp"), axis=0, tiled=True),
        lax.all_gather(gate_gain, ("dp", "fsdp"), axis=0, tiled=True),
        lax.all_gather(out_proj, ("dp", "fsdp"), axis=0, tiled=True),
    )
    seq_count = lengths.shape[0]
    width = hidden.shape[1]
    slot_len = hidden.shape[0] // seq_count
    dt_shift = dt_bias.astype(jnp.float32)
    rates_log = a_log.astype(jnp.float32)
    skip_vals = skip_gain.astype(jnp.float32)
    mixer_fn = partial(mixer_block, span_len=SPAN)
    row_blocks = hidden.reshape(seq_count, slot_len, width)
    cot_blocks = cotangent.reshape(seq_count, slot_len, width)

    def forward(item):
        row_values, seq_len = item
        rows_wide = row_values.astype(jnp.float32)
        live = (jnp.arange(slot_len) < seq_len).astype(jnp.float32)
        normed = pre_norm(rows_wide, gathered[0].astype(jnp.float32)).astype(jnp.bfloat16)
        projected = jnp.dot(normed, gathered[1], preferred_element_type=jnp.float32)
        dt_raw = jnp.dot(normed, gathered[2], preferred_element_type=jnp.float32)
        gated = mixer_fn(
            projected,
            dt_raw,
            gathered[3].astype(jnp.float32),
            gathered[4].astype(jnp.float32),
            dt_shift,
            rates_log,
            skip_vals,
            gathered[5].astype(jnp.float32),
        ).astype(jnp.bfloat16)
        branch = jnp.dot(gated, gathered[6], preferred_element_type=jnp.float32)
        output = (rows_wide + live[:, None] * branch).astype(jnp.bfloat16)
        return (output, normed, projected, dt_raw, gated)

    outputs, normed_all, projected_all, dtraw_all, gated_all = lax.map(
        forward, (row_blocks, lengths)
    )
    weights = (
        lax.all_gather(norm_gain, ("dp", "fsdp"), axis=0, tiled=True),
        lax.all_gather(in_proj, ("dp", "fsdp"), axis=0, tiled=True),
        lax.all_gather(dt_proj, ("dp", "fsdp"), axis=0, tiled=True),
        lax.all_gather(conv_weight, ("dp", "fsdp"), axis=1, tiled=True),
        lax.all_gather(conv_bias, ("dp", "fsdp"), axis=0, tiled=True),
        lax.all_gather(gate_gain, ("dp", "fsdp"), axis=0, tiled=True),
        lax.all_gather(out_proj, ("dp", "fsdp"), axis=0, tiled=True),
    )
    gain_one = weights[0].astype(jnp.float32)
    conv_taps = weights[3].astype(jnp.float32)
    conv_shift = weights[4].astype(jnp.float32)
    gain_two = weights[5].astype(jnp.float32)

    def backward(totals, item):
        row_values, cot_values, seq_len, normed, projected, dt_raw, gated = item
        rows_wide = row_values.astype(jnp.float32)
        live = (jnp.arange(slot_len) < seq_len).astype(jnp.float32)
        _, norm_back = jax.vjp(pre_norm, rows_wide, gain_one)
        _, mixer_back = jax.vjp(
            mixer_fn,
            projected,
            dt_raw,
            conv_taps,
            conv_shift,
            dt_shift,
            rates_log,
            skip_vals,
            gain_two,
        )
        upstream = (cot_values.astype(jnp.float32) * live[:, None]).astype(jnp.bfloat16)
        grad_out = row_dot(gated, upstream)
        grad_gated = back_dot(upstream, weights[6])
        g_proj, g_dtraw, g_conv, g_convb, g_dtb, g_alog, g_skip, g_ggain = mixer_back(grad_gated)
        proj_low = g_proj.astype(jnp.bfloat16)
        dtraw_low = g_dtraw.astype(jnp.bfloat16)
        grad_in = row_dot(normed, proj_low)
        grad_dt = row_dot(normed, dtraw_low)
        grad_normed = back_dot(proj_low, weights[1]) + back_dot(dtraw_low, weights[2])
        grad_rows, grad_gain = norm_back(grad_normed)
        input_grad = cot_values.astype(jnp.float32) + grad_rows
        terms = (
            grad_gain,
            grad_in,
            grad_dt,
            g_conv,
            g_convb,
            g_ggain,
            grad_out,
            g_dtb,
            g_alog,
            g_skip,
        )
        totals = tuple((left + right for left, right in zip(totals, terms)))
        return (totals, input_grad)

    shaped = (
        weights[0],
        weights[1],
        weights[2],
        weights[3],
        weights[4],
        weights[5],
        weights[6],
        dt_bias,
        a_log,
        skip_gain,
    )
    start = tuple((jnp.zeros(entry.shape, jnp.float32) for entry in shaped))
    totals, in_grads = lax.scan(
        backward,
        start,
        (row_blocks, cot_blocks, lengths, normed_all, projected_all, dtraw_all, gated_all),
    )
    shares = (
        lax.psum_scatter(totals[0], ("dp", "fsdp"), scatter_dimension=0, tiled=True),
        lax.psum_scatter(totals[1], ("dp", "fsdp"), scatter_dimension=0, tiled=True),
        lax.psum_scatter(totals[2], ("dp", "fsdp"), scatter_dimension=0, tiled=True),
        lax.psum_scatter(totals[3], ("dp", "fsdp"), scatter_dimension=1, tiled=True),
        lax.psum_scatter(totals[4], ("dp", "fsdp"), scatter_dimension=0, tiled=True),
        lax.psum_scatter(totals[5], ("dp", "fsdp"), scatter_dimension=0, tiled=True),
        lax.psum_scatter(totals[6], ("dp", "fsdp"), scatter_dimension=0, tiled=True),
    )
    head_sums = lax.psum((totals[7], totals[8], totals[9]), ("dp", "fsdp"))
    return (
        outputs.reshape(seq_count * slot_len, width),
        in_grads.reshape(seq_count * slot_len, width),
        shares[0],
        shares[1],
        shares[2],
        shares[3],
        shares[4],
        head_sums[0],
        head_sums[1],
        head_sums[2],
        shares[5],
        shares[6],
    )


def solution(mesh):
    return jax.shard_map(
        shards,
        mesh=mesh,
        in_specs=(
            P(("dp", "fsdp"), None),
            P(("dp", "fsdp"), None),
            P(("dp", "fsdp")),
            P(("dp", "fsdp")),
            P(("dp", "fsdp"), None),
            P(("dp", "fsdp"), None),
            P(None, ("dp", "fsdp")),
            P(("dp", "fsdp")),
            P(),
            P(),
            P(),
            P(("dp", "fsdp")),
            P(("dp", "fsdp"), None),
        ),
        out_specs=(
            P(("dp", "fsdp"), None),
            P(("dp", "fsdp"), None),
            P(("dp", "fsdp")),
            P(("dp", "fsdp"), None),
            P(("dp", "fsdp"), None),
            P(None, ("dp", "fsdp")),
            P(("dp", "fsdp")),
            P(),
            P(),
            P(),
            P(("dp", "fsdp")),
            P(("dp", "fsdp"), None),
        ),
        check_vma=False,
    )
```

profile of v0, /device:TPU:0, one launch (start us, length us, event | category | flops | bytes accessed | tf_op | source)
XLA Modules:
  0.0 1517.4 jit_solution(16952419418065902820)
XLA Ops:
  12.0 44.2 %all-reduce.22 = (bf16[1536]{0:T(1024)(128)(2,1)S(1)}, bf16[3328]{0:T(1024)(128)(2,1)S(1)}, bf16[3072]{0:T(1024)(128)(2,1)S(1)}) all-reduce(bf16[1536]{0:T(1024)(128)(2,1)S(1)} %dynamic-update-slice, bf16[3328]{0:T(1024)(128)(2,1)S(1)} %dynamic-update-slice.1, ...), channel_id=1, replica_groups=mesh['dp'=8,'fsdp'=4] {'dp','fsdp'}, use_global_device_ids=true, to_apply=%add.14 | all-reduce | flops 7936 | bytes 31744
  56.9 43.5 %all_gather.29 = bf16[1536,48]{1,0:T(8,128)(2,1)S(1)} all-gather(bf16[48,48]{1,0:T(8,128)(2,1)} %param.24), channel_id=1, replica_groups=mesh['dp'=8,'fsdp'=4] {'dp','fsdp'}, dimensions={0}, use_global_device_ids=true | all-gather | bytes 152064 | tf_op jit(solution)/shard_map/all_gather | solution.py:110
  108.0 37.8 %all-gather = bf16[32,104,4]{1,2,0:T(4,128)(2,1)S(1)} all-gather(bf16[1,104,4]{1,2,0:T(4,128)(2,1)S(1)} %bitcast.298), channel_id=1, replica_groups=mesh['dp'=8,'fsdp'=4] {'dp','fsdp'}, dimensions={0}, use_global_device_ids=true | all-gather | bytes 27456 | tf_op jit(solution)/shard_map/all_gather | solution.py:111
  168.6 13.9 fusion.126
  189.3 15.2 %fusion.38 = (f32[512,3328]{1,0:T(8,128)S(1)}, f32[512,3328]{1,0:T(8,128)}) fusion(f32[3328]{0:T(1024)S(1)} %get-tuple-element.471, f32[3328]{0:T(1024)S(1)} %copy-done.41, f32[512,3328]{1,0:T(8,128)} %slice.122, f32[3328]{0:T(1024)S(1)} %copy-done.43, f32[3328]{0:T(1024)S(1)} %get-tuple-element.470, f32[3328]{0:T(1024)S(1)} %copy-done.51), kind=kLoop, calls=%fused_computation.62 | loop fusion | flops 20447232 | bytes 20513792 | tf_op jit(solution)/shard_map/while/body/eval_jaxpr/jit(silu)/mul | solution.py:66
  228.0 11.0 copy.171
  270.0 33.2 %fusion.46 = f32[2,256,48,64]{1,3,2,0:T(8,128)} fusion(f32[2,48,64,256]{3,2,1,0:T(8,128)S(1)} %fusion.140, f32[2,256,48]{1,2,0:T(8,128)S(1)} %copy-done.46, f32[2,256,48,64]{1,3,2,0:T(8,128)} %copy.171, f32[2,256,48]{1,2,0:T(8,128)S(1)} %bitcast.282, f32[2,48,256]{2,1,0:T(8,128)S(1)} %copy-done.33, f32[2,256,256]{2,1,0:T(8,128)S(1)} %copy-done.26, ...), kind=kOutput, calls=%fused_computation.79 | convolution fusion | flops 4861722624 | bytes 19759104 | tf_op jit(solution)/shard_map/while/body/eval_jaxpr/jvp(khij,khjp->khip)/dot_general | solution.py:34
  303.3 11.3 copy.201
  314.6 10.6 reshape.513
  349.3 33.6 %bitcast_add_fusion.4 = f32[2,256,48,64]{1,3,2,0:T(8,128)} fusion(f32[2,256,48,64]{1,3,2,0:T(8,128)S(1)} %fusion.139, f32[2,256,48]{1,2,0:T(8,128)S(1)} %copy-done.45, f32[2,256,48,64]{1,3,2,0:T(8,128)} %copy.171, f32[2,256,48]{1,2,0:T(8,128)S(1)} %bitcast.284, f32[2,256,256]{2,1,0:T(8,128)S(1)} %copy-done.26, f32[2,48,256]{2,1,0:T(8,128)S(1)} %copy-done.36, ...), kind=kOutput, calls=%fused_computation.80 | convolution fusion | flops 4861722624 | bytes 19759104 | tf_op jit(solution)/shard_map/while/body/eval_jaxpr/khij,khjp->khip/dot_general | solution.py:34
  382.9 11.3 copy.200
  394.2 10.6 reshape.512
  404.9 15.0 multiply_reduce_fusion.9
  419.9 12.8 multiply_reduce_fusion.5
  432.7 13.7 multiply_reduce_fusion.6
  456.3 11.2 copy.180
  467.6 39.1 %fusion.19 = (f32[2,48,256]{2,1,0:T(8,128)}, f32[2,48,256]{2,1,0:T(8,128)}, f32[2,256,256]{2,1,0:T(8,128)S(1)}) fusion(f32[2,48,256]{2,1,0:T(8,128)S(1)} %copy-done.33, f32[2,256,256]{2,1,0:T(8,128)} %fusion.138, pred[256,256]{1,0:T(8,128)(4,1)S(1)} %copy-done.49, f32[2,256,48,64]{1,3,2,0:T(8,128)} %copy.171, f32[2,256,48]{1,2,0:T(8,128)S(1)} %bitcast.285, ...), kind=kOutput, calls=%fused_computation.32 | convolution fusion | flops 4902436864 | bytes 14090240 | tf_op jit(solution)/shard_map/while/body/eval_jaxpr/transpose(jvp(khij,khjp->khip))/dot_general | solution.py:34
  535.4 12.7 fusion.96
  548.2 12.2 fusion.95
  566.5 25.5 %bitcast_add_fusion.3 = f32[2,256,48,64]{1,3,2,0:T(8,128)} fusion(f32[2,48,64,256]{3,2,1,0:T(8,128)} %get-tuple-element.557, f32[2,256,48]{1,2,0:T(8,128)S(1)} %bitcast.288, f32[2,256,48,64]{1,3,2,0:T(8,128)} %copy.180, f32[2,48,256]{2,1,0:T(8,128)S(1)} %copy-done.34, f32[2,256,256]{2,1,0:T(8,128)S(1)} %copy-done.27, pred[256,256]{1,0:T(8,128)(4,1)S(1)} %copy-done.50), kind=kOutput, calls=%fused_computation.72 | convolution fusion | flops 4860149760 | bytes 19660800 | tf_op jit(solution)/shard_map/while/body/eval_jaxpr/transpose(jvp(khij,khjp->khip))/dot_general | solution.py:34
  592.0 11.3 copy.202
  616.5 10.6 reshape.514
  638.7 19.5 %fusion.130 = (f32[3328]{0:T(1024)}, f32[3328]{0:T(1024)S(1)}, f32[3328]{0:T(1024)S(1)}, f32[3328]{0:T(1024)S(1)}, f32[3328]{0:T(1024)S(1)}, /*index=5*/f32[512,3328]{1,0:T(8,128)}) fusion(f32[512,6400]{1,0:T(8,128)} %copy-done.4, f32[512,3328]{1,0:T(8,128)} %slice.122, f32[512,3328]{1,0:T(8,128)} %get-tuple-element.536, ...), kind=kLoop, calls=%fused_computation.219 | loop fusion | flops 34062080 | bytes 34145280 | tf_op jit(solution)/shard_map/while/body/eval_jaxpr/transpose(jvp())/reduce_sum | solution.py:63
  669.8 13.0 fusion.37
  683.6 20.0 %fusion.65 = (f32[1536]{0:T(1024)}, f32[512]{0:T(512)S(1)}, f32[512,1536]{1,0:T(8,128)}) fusion(bf16[512,1536]{1,0:T(8,128)(2,1)S(1)} %copy-done.9, f32[512]{0:T(512)S(1)} %copy-done.29, f32[1536]{0:T(1024)S(1)} %copy-done.25, f32[512,1536]{1,0:T(8,128)} %fusion.111, bf16[1536,6400]{1,0:T(8,128)(2,1)} %all-gather.4.cloned.1.call-done, ...), kind=kOutput, calls=%fused_computation.125 | convolution fusion | flops 10079172608 | bytes 40648704 | tf_op jit(solution)/shard_map/while/body/eval_jaxpr/dot_general | solution.py:87
  704.2 12.5 fusion.98
  716.8 21.9 %fusion.97 = f32[1536,6400]{1,0:T(8,128)} fusion(f32[512,3072]{1,0:T(8,128)} %get-tuple-element.539, f32[512,3328]{1,0:T(8,128)} %fusion.37, bf16[512,1536]{1,0:T(8,128)(2,1)S(1)} %copy-done.9, f32[1536]{0:T(1024)S(1)} %copy-done.25, f32[512]{0:T(512)S(1)} %copy-done.29), kind=kOutput, calls=%fused_computation.147 | convolution fusion | flops 10076028928 | bytes 54009856 | tf_op jit(solution)/shard_map/while/body/eval_jaxpr/dot_general | solution.py:81
  743.8 11.0 fusion.68
  754.8 71.7 %all-reduce.25.cloned.1.call-done = (f32[1536]{0:T(1024)}, f32[4,3328]{1,0:T(4,128)}, f32[3328]{0:T(1024)}, f32[48]{0:T(128)}, f32[48]{0:T(128)}, /*index=5*/f32[48]{0:T(128)}, f32[3072]{0:T(1024)}) async-done(((f32[1536]{0:T(1024)}, f32[4,3328]{1,0:T(4,128)}, f32[3328]{0:T(1024)}, f32[48]{0:T(128)}, f32[48]{0:T(128)}, /*index=5*/f32[48]{0:T(128)}, f32[3072]{0:T(1024)}), (f32[1536]{0:T(1024)}, ...) | async-done | bytes 85584
  831.7 97.6 %reduce-scatter.7.cloned.1.call-done = f32[48,48]{1,0:T(8,128)} async-done(((f32[1536,48]{1,0:T(8,128)}), f32[48,48]{1,0:T(8,128)}) %reduce-scatter.7.cloned.1.call-update) | async-done | bytes 9232 | tf_op jit(solution)/shard_map/reduce_scatter | solution.py:227
  929.3 212.7 %reduce-scatter.9.cloned.1.call-done = f32[96,1536]{1,0:T(8,128)} async-done(((f32[3072,1536]{1,0:T(8,128)}), f32[96,1536]{1,0:T(8,128)}) %reduce-scatter.9.cloned.1.call-update) | async-done | bytes 589840 | tf_op jit(solution)/shard_map/reduce_scatter | solution.py:231
  1142.0 364.9 %reduce-scatter.5.cloned.1.call-done = f32[48,6400]{1,0:T(8,128)} async-done(((f32[1536,6400]{1,0:T(8,128)}), f32[48,6400]{1,0:T(8,128)}) %reduce-scatter.5.cloned.1.call-update) | async-done | bytes 1228816 | tf_op jit(solution)/shard_map/reduce_scatter | solution.py:226
  (303 shorter events, 236.3 us)
Async XLA Ops:
  7.2 100.8 %copy-start.73 = (bf16[4,104]{1,0:T(4,128)(2,1)S(1)}, bf16[4,104]{1,0:T(4,128)(2,1)}, u32[]{:S(2)}) copy-start(bf16[4,104]{1,0:T(4,128)(2,1)} %param.25) | copy-start | bytes 2500
  7.2 140.3 %copy-start.74 = (bf16[48]{0:T(256)(128)(2,1)S(1)}, bf16[48]{0:T(256)(128)(2,1)}, u32[]{:S(2)}) copy-start(bf16[48]{0:T(256)(128)(2,1)} %param.29) | copy-start | bytes 292
  7.2 161.4 %all-gather.4.cloned.1.call-start = ((), (), s32[]{:S(2)}) async-start(), calls=%async_computation.3 | async-start | bytes 20275200 | tf_op jit(solution)/shard_map/all_gather | solution.py:109
  7.9 411.9 %all-gather.6.cloned.1.call-start = ((), (), s32[]{:S(2)}) async-start(), calls=%async_computation.4 | async-start | bytes 9732096 | tf_op jit(solution)/shard_map/all_gather | solution.py:114
  8.7 817.8 %all-reduce.25.cloned.1.call-start = ((), (), s32[]{:S(2)}) async-start(), calls=%async_computation.8 | async-start | bytes 183296
  56.2 112.4 %copy-start.24 = (f32[1536]{0:T(1024)}, f32[1536]{0:T(1024)S(1)}, u32[]{:S(2)}) copy-start(f32[1536]{0:T(1024)S(1)} %convert_element_type.88) | copy-start | bytes 18436
  56.9 49.7 %copy-start.65 = (f32[48]{0:T(128)}, f32[48]{0:T(128)S(1)}, u32[]{:S(2)}) copy-start(f32[48]{0:T(128)S(1)} %convert_element_type.90) | copy-start | bytes 580
  103.0 42.9 %copy-start.69 = (f32[48]{0:T(128)}, f32[48]{0:T(128)S(1)}, u32[]{:S(2)}) copy-start(f32[48]{0:T(128)S(1)} %convert_exponential_fusion) | copy-start | bytes 580
  103.0 65.6 %copy-start.28 = (f32[512]{0:T(512)}, f32[512]{0:T(512)S(1)}, u32[]{:S(2)}) copy-start(f32[512]{0:T(512)S(1)} %fusion.114) | copy-start | bytes 6148
  107.7 60.0 %copy-start.12 = (f32[2,48,2,128]{3,1,2,0:T(8,128)}, f32[2,48,2,128]{3,1,2,0:T(8,128)S(1)}, u32[]{:S(2)}) copy-start(f32[2,48,2,128]{3,1,2,0:T(8,128)S(1)} %reduce-window.24) | copy-start | bytes 294916
  108.0 59.7 %copy-start.52 = (f32[2,48,2]{1,2,0:T(2,128)}, f32[2,48,2]{1,2,0:T(2,128)S(1)}, u32[]{:S(2)}) copy-start(f32[2,48,2]{1,2,0:T(2,128)S(1)} %slice.132) | copy-start | bytes 2308
  166.3 23.0 %copy-start.37 = (f32[3328]{0:T(1024)}, f32[3328]{0:T(1024)S(1)}, u32[]{:S(2)}) copy-start(f32[3328]{0:T(1024)S(1)} %get-tuple-element.470) | copy-start | bytes 39940
  166.3 23.0 %copy-start.39 = (f32[3328]{0:T(1024)}, f32[3328]{0:T(1024)S(1)}, u32[]{:S(2)}) copy-start(f32[3328]{0:T(1024)S(1)} %get-tuple-element.471) | copy-start | bytes 39940
  259.7 43.5 %copy-start.63 = (f32[2,48]{1,0:T(2,128)}, f32[2,48]{1,0:T(2,128)S(1)}, u32[]{:S(2)}) copy-start(f32[2,48]{1,0:T(2,128)S(1)} %get-tuple-element.747) | copy-start | bytes 1156
  456.3 50.3 %slice-start = ((s8[6291456]{0:T(1024)(128)(4,1)}), s8[2097152]{0:T(1024)(128)(4,1)S(1)}, s32[]{:S(2)}) async-start(s8[6291456]{0:T(1024)(128)(4,1)} %bitcast.266), calls=%async_computation.9 | async-start | bytes 4194304
  467.6 39.1 %copy-start.2 = (f32[2,256,48,64]{1,3,2,0:T(8,128)S(1)}, f32[2,256,48,64]{1,3,2,0:T(8,128)}, u32[]{:S(2)}) copy-start(f32[2,256,48,64]{1,3,2,0:T(8,128)} %copy.180) | copy-start | bytes 18874372
  467.6 39.1 %slice-start.1 = ((s8[6291456]{0:T(1024)(128)(4,1)}), s8[4194304]{0:T(1024)(128)(4,1)S(1)}, s32[]{:S(2)}) async-start(s8[6291456]{0:T(1024)(128)(4,1)} %bitcast.266), calls=%async_computation.10 | async-start | bytes 8388608
  548.2 18.0 %copy-start.23 = (f32[512,48]{0,1:T(8,128)S(1)}, f32[512,48]{0,1:T(8,128)}, u32[]{:S(2)}) copy-start(f32[512,48]{0,1:T(8,128)} %copy-done.22) | copy-start | bytes 294916
  548.2 18.0 %copy-start.66 = (f32[48]{0:T(128)S(1)}, f32[48]{0:T(128)}, u32[]{:S(2)}) copy-start(f32[48]{0:T(128)} %copy-done.65) | copy-start | bytes 580
  548.2 18.3 %copy-start.27 = (f32[2,256,256]{2,1,0:T(8,128)S(1)}, f32[2,256,256]{2,1,0:T(8,128)}, u32[]{:S(2)}) copy-start(f32[2,256,256]{2,1,0:T(8,128)} %fusion.138) | copy-start | bytes 1572868
  548.2 18.2 %copy-start.34 = (f32[2,48,256]{2,1,0:T(8,128)S(1)}, f32[2,48,256]{2,1,0:T(8,128)}, u32[]{:S(2)}) copy-start(f32[2,48,256]{2,1,0:T(8,128)} %copy-done.32) | copy-start | bytes 294916
  548.2 18.2 %copy-start.50 = (pred[256,256]{1,0:T(8,128)(4,1)S(1)}, pred[256,256]{1,0:T(8,128)(4,1)}, u32[]{:S(2)}) copy-start(pred[256,256]{1,0:T(8,128)(4,1)} %iota_compare_fusion) | copy-start | bytes 196612
  638.6 19.5 %copy-start.40 = (f32[3328]{0:T(1024)S(1)}, f32[3328]{0:T(1024)}, u32[]{:S(2)}) copy-start(f32[3328]{0:T(1024)} %copy-done.39) | copy-start | bytes 39940
  638.7 19.5 %copy-start.42 = (f32[3328]{0:T(1024)S(1)}, f32[3328]{0:T(1024)}, u32[]{:S(2)}) copy-start(f32[3328]{0:T(1024)} %get-tuple-element.472) | copy-start | bytes 39940
  638.7 19.5 %copy-start.44 = (f32[3328]{0:T(1024)S(1)}, f32[3328]{0:T(1024)}, u32[]{:S(2)}) copy-start(f32[3328]{0:T(1024)} %get-tuple-element.473) | copy-start | bytes 39940
  683.5 20.1 %copy-start.62 = (f32[512]{0:T(512)S(1)}, f32[512]{0:T(512)}, u32[]{:S(2)}) copy-start(f32[512]{0:T(512)} %get-tuple-element.540) | copy-start | bytes 6148
  683.5 20.7 %copy-start.16 = (bf16[512,1536]{1,0:T(8,128)(2,1)S(1)}, bf16[512,1536]{1,0:T(8,128)(2,1)}, u32[]{:S(2)}) copy-start(bf16[512,1536]{1,0:T(8,128)(2,1)} %param.20) | copy-start | bytes 4718596
  683.5 20.7 %copy-start.55 = (f32[3072]{0:T(1024)S(1)}, f32[3072]{0:T(1024)}, u32[]{:S(2)}) copy-start(f32[3072]{0:T(1024)} %convert_element_type.95) | copy-start | bytes 36868
  683.5 20.7 %copy-start.72 = (f32[512]{0:T(512)S(1)}, f32[512]{0:T(512)}, u32[]{:S(2)}) copy-start(f32[512]{0:T(512)} %fusion.113) | copy-start | bytes 6148
  703.6 225.7 %reduce-scatter.7.cloned.1.call-start = ((), (), s32[]{:S(2)}) async-start(), calls=%async_computation.6 | async-start | bytes 811008 | tf_op jit(solution)/shard_map/reduce_scatter | solution.py:227
  704.2 437.9 %reduce-scatter.9.cloned.1.call-start = ((), (), s32[]{:S(2)}) async-start(), calls=%async_computation.7 | async-start | bytes 19464192 | tf_op jit(solution)/shard_map/reduce_scatter | solution.py:231
  716.7 790.2 %reduce-scatter.5.cloned.1.call-start = ((), (), s32[]{:S(2)}) async-start(), calls=%async_computation.5 | async-start | bytes 40550400 | tf_op jit(solution)/shard_map/reduce_scatter | solution.py:226
  (53 other events, 445.4 us)
Sparse Core Ops, SparseCore 0:
  10.9 133.4 all-gather.3
  147.3 79.7 all-gather.5
  703.7 122.7 all-reduce.24
  832.1 97.1 reduce-scatter.6
  936.1 205.8 reduce-scatter.8
  1148.9 357.9 reduce-scatter.4
where the time goes:
time: 1520 us
  waiting for transfers between devices  749 us (49%)
  matrix products  308 us (20%)
  local copies, waits for them, and re-layouts  172 us (11%)
  other arithmetic  147 us (10%)
  blocking collectives  126 us (8%)
  between operations  16 us (1%)
    reduce_scatter x1, waiting for transfers between devices, shards(): lax.psum_scatter(totals[1], ('dp', 'fsdp'), scatter_dimension=0, tiled=True)  365 us
    reduce_scatter x1, waiting for transfers between devices, shards(): lax.psum_scatter(totals[6], ('dp', 'fsdp'), scatter_dimension=0, tiled=True)  213 us
    dot_general x4, matrix products, state_space(): jnp.einsum('khij,khjp->khip', mixing, scaled, precision=highest)  131 us
    reduce_scatter x1, waiting for transfers between devices, shards(): lax.psum_scatter(totals[2], ('dp', 'fsdp'), scatter_dimension=0, tiled=True)  97.6 us
    unnamed x7, waiting for transfers between devices  73.7 us
    reshape x6, local copies, waits for them, and re-layouts, state_space(): return result.reshape(length, head_count, head_dim)  65.1 us
    unnamed x1, blocking collectives  44.2 us
    all_gather x1, blocking collectives, shards(): lax.all_gather(dt_proj, ('dp', 'fsdp'), axis=0, tiled=True)  43.5 us
  transfers between devices with their start and end apart: 6, of which 4 were waited for; matrix products, arithmetic and copies ran while one was open for 22% of the time, Pallas kernels for 0%

commit v1 on v0

v1 whole, which is shorter than its diff:
```python
from functools import partial

import jax
import jax.numpy as jnp
from jax import lax
from jax.experimental import pallas as pl
from jax.experimental.pallas import tpu as pltpu
from jax.sharding import PartitionSpec as P

f32 = jnp.float32
bf16 = jnp.bfloat16
epsilon = 1e-05
highest = lax.Precision.HIGHEST
BLK = 128
GH = 8
HD = 64
GC = GH * HD
KEY = 128
NEG = -1e30


def sigmoid(v):
    return 0.5 * jnp.tanh(0.5 * v) + 0.5


def mm(a, b):
    return lax.dot_general(a, b, (((1,), (0,)), ((), ())), preferred_element_type=f32)


def mm_nt(a, b):
    return lax.dot_general(a, b, (((1,), (1,)), ((), ())), preferred_element_type=f32)


def mm_tn(a, b):
    return lax.dot_general(a, b, (((0,), (0,)), ((), ())), preferred_element_type=f32)


def mm_hi(a, b, dims=((1,), (0,))):
    return lax.dot_general(a, b, (dims, ((), ())), preferred_element_type=f32, precision=highest)


def split(v):
    hi = v.astype(bf16)
    lo = (v - hi.astype(f32)).astype(bf16)
    return jnp.concatenate([hi, lo], axis=1)


def iota(shape, dim):
    return lax.broadcasted_iota(jnp.int32, shape, dim)


def expander(g):
    rows = iota((2 * KEY, GC), 0)
    cols = iota((2 * KEY, GC), 1)
    return jnp.where(lax.rem(rows, KEY) == cols // HD + g * GH, 1.0, 0.0).astype(bf16)


def reducer(g):
    rows = iota((GC, KEY), 0)
    cols = iota((GC, KEY), 1)
    return jnp.where(rows // HD + g * GH == cols, 1.0, 0.0).astype(bf16)


def taps_of(window, par, cols):
    out = par[4:5, cols] + par[3:4, cols] * window[8:136]
    for k in range(3):
        out = out + par[k : k + 1, cols] * window[5 + k : 133 + k]
    return out


def fwd_kernel(
    gate_ref, rawv_ref, rawk_ref, dtr_ref, pv_ref, pk_ref, ph_ref,
    y_ref, p_ref, hst_ref, r_ref, s_ref, st_ref, hl_ref, ehl_ref, kb_ref, kt_ref, sc_ref,
    pad, padk, sg, hcar, ssq,
):
    g = pl.program_id(0)
    length = gate_ref.shape[0]
    blocks = length // BLK
    inner = HD * GH * pl.num_programs(0)

    @pl.when(g == 0)
    def _():
        dt = jax.nn.softplus(dtr_ref[...] + ph_ref[0:1, :])
        la = -dt * jnp.exp(ph_ref[1:2, :])
        tri = jnp.where(iota((BLK, BLK), 0) >= iota((BLK, BLK), 1), 1.0, 0.0).astype(f32)
        hl_ref[0] = split(dt)
        ehl_ref[...] = jnp.zeros_like(ehl_ref)
        for k in range(blocks):
            rows = slice(k * BLK, (k + 1) * BLK)
            s = mm_hi(tri, la[rows])
            s_ref[rows] = s
            st_ref[:, rows] = s.T
            hl_ref[1, rows] = split(jnp.exp(s))
            hl_ref[2, rows] = split(jnp.exp(s[BLK - 1 :] - s))
            ehl_ref[k : k + 1] = split(jnp.exp(s[BLK - 1 :]))
        padk[0:8] = jnp.zeros((8, 2 * KEY), f32)
        padk[8:] = rawk_ref[...]
        pad[0:8] = jnp.zeros((8, GC), f32)
        for k in range(blocks):
            rows = slice(k * BLK, (k + 1) * BLK)
            u = taps_of(padk[k * BLK : k * BLK + BLK + 8], pk_ref, slice(0, 2 * KEY))
            v = u * sigmoid(u)
            kb_ref[rows] = v.astype(bf16)
            kt_ref[:, rows] = v.T.astype(bf16)
            sc_ref[k] = mm_hi(v[:, KEY:], v[:, :KEY], ((1,), (1,)))
        ssq[...] = jnp.zeros_like(ssq)

    pad[8:] = rawv_ref[...]
    sg[...] = pltpu.roll(s_ref[...], lax.rem(KEY - g * GH, KEY), 1)
    ex = expander(g)
    bias = jnp.where(iota((BLK, BLK), 0) >= iota((BLK, BLK), 1), 0.0, NEG).astype(f32)
    low = iota((BLK, KEY), 1) < HD
    eend = mm(ehl_ref[...], ex)
    hcar[...] = jnp.zeros_like(hcar)
    for k in range(blocks):
        rows = slice(k * BLK, (k + 1) * BLK)
        dtx = mm(hl_ref[0, rows], ex)
        exx = mm(hl_ref[1, rows], ex)
        txx = mm(hl_ref[2, rows], ex)
        hb = hcar[...].astype(bf16)
        hst_ref[k] = hb
        outer = mm(kb_ref[rows, KEY:], hb)
        across = st_ref[pl.ds(pl.multiple_of(g * GH, GH), GH), rows]
        xts = []
        for q in range(GC // KEY):
            cols = slice(q * KEY, (q + 1) * KEY)
            u = taps_of(pad[k * BLK : k * BLK + BLK + 8, cols], pv_ref, cols)
            v = u * sigmoid(u)
            x = v * dtx[:, cols]
            xts.append((x * txx[:, cols]).astype(bf16))
            xb = x.astype(bf16)
            zero = jnp.zeros_like(xb)
            x2 = jnp.concatenate([jnp.where(low, xb, zero), jnp.where(low, zero, xb)], axis=0)
            ms = []
            for half in range(2):
                j = 2 * q + half
                spread = sg[rows, j : j + 1] - across[j : j + 1]
                ms.append((jnp.exp(spread + bias) * sc_ref[k]).astype(bf16))
            y = mm(jnp.concatenate(ms, axis=1), x2)
            y = y + outer[:, cols] * exx[:, cols] + pv_ref[6:7, cols] * v
            y_ref[rows, cols] = y
            gate = gate_ref[rows, cols]
            p = y * (gate * sigmoid(gate))
            p_ref[rows, cols] = p
            ssq[rows] += p * p
        if k + 1 < blocks:
            hcar[...] = eend[k : k + 1] * hcar[...] + mm(kt_ref[:KEY, rows], jnp.concatenate(xts, axis=1))

    @pl.when(g == pl.num_programs(0) - 1)
    def _():
        mean = jnp.sum(ssq[...], axis=1, keepdims=True) / inner
        r_ref[...] = jnp.broadcast_to(lax.rsqrt(mean + epsilon), r_ref.shape)


def bwd_kernel(
    gate_ref, rawv_ref, rawk_ref, dtr_ref, pv_ref, pk_ref, ph_ref,
    y_ref, gg_ref, hst_ref, r_ref, c_ref, s_ref, st_ref, hl_ref, ehl_ref, kb_ref, kt_ref, sc_ref,
    dproj_ref, sv_ref, sk_ref, sh_ref,
    pad, padk, dpad, dpadk, sg, dhcar, dsc, dkb, dsrow, dscol, ddt,
):
    g = pl.program_id(0)
    length = gate_ref.shape[0]
    blocks = length // BLK
    groups = gate_ref.shape[1] // GC
    inner = dproj_ref.shape[1] // 2 - 3 * KEY // 2
    groups = pl.num_programs(0)

    @pl.when(g == 0)
    def _():
        pad[0:8] = jnp.zeros((8, GC), f32)
        padk[0:8] = jnp.zeros((8, 2 * KEY), f32)
        padk[8:] = rawk_ref[...]
        dpad[length:] = jnp.zeros((8, GC), f32)
        dpadk[length:] = jnp.zeros((8, 2 * KEY), f32)
        dsc[...] = jnp.zeros_like(dsc)
        dkb[...] = jnp.zeros_like(dkb)
        dsrow[...] = jnp.zeros_like(dsrow)
        dscol[...] = jnp.zeros_like(dscol)
        ddt[...] = jnp.zeros_like(ddt)

    pad[8:] = rawv_ref[...]
    sg[...] = pltpu.roll(s_ref[...], lax.rem(KEY - g * GH, KEY), 1)
    ex = expander(g)
    red = reducer(g)
    row = iota((BLK, BLK), 0)
    col = iota((BLK, BLK), 1)
    bias = jnp.where(row >= col, 0.0, NEG).astype(f32)
    strict = row > col
    low = iota((BLK, KEY), 1) < HD
    eend = mm(ehl_ref[...], ex)
    dhcar[...] = jnp.zeros_like(dhcar)
    sv_ref[...] = jnp.zeros_like(sv_ref)
    for k in range(blocks - 1, -1, -1):
        rows = slice(k * BLK, (k + 1) * BLK)
        dtx = mm(hl_ref[0, rows], ex)
        exx = mm(hl_ref[1, rows], ex)
        txx = mm(hl_ref[2, rows], ex)
        hb = hst_ref[k]
        dhb = dhcar[...].astype(bf16)
        ch = mm(kb_ref[rows, KEY:], hb)
        qq = mm(kb_ref[rows, :KEY], dhb)
        across = st_ref[pl.ds(pl.multiple_of(g * GH, GH), GH), rows]
        dyes, xts, zs, oys, ddts, ecols = [], [], [], [], [], []
        dsrow_k = jnp.zeros((BLK, KEY), f32)
        for q in range(GC // KEY):
            cols = slice(q * KEY, (q + 1) * KEY)
            window = pad[k * BLK : k * BLK + BLK + 8, cols]
            u = taps_of(window, pv_ref, cols)
            su = sigmoid(u)
            v = u * su
            x = v * dtx[:, cols]
            xb = x.astype(bf16)
            gate = gate_ref[rows, cols]
            y = y_ref[rows, cols]
            gg = gg_ref[rows, cols]
            sgt = sigmoid(gate)
            silu_g = gate * sgt
            p = y * silu_g
            r = r_ref[rows]
            dgn = gg * r
            sv_ref[5:6, cols] += jnp.sum(dgn * p, axis=0, keepdims=True)
            dp = dgn * pv_ref[5:6, cols] - p * c_ref[rows]
            dgate = dp * y * (sgt + silu_g * (1.0 - sgt))
            off = pl.multiple_of(g * GC + q * KEY, KEY)
            dproj_ref[rows, pl.ds(off, KEY)] = dgate.astype(bf16)
            dy = dp * silu_g
            sv_ref[6:7, cols] += jnp.sum(dy * v, axis=0, keepdims=True)
            dyb = dy.astype(bf16)
            dye = dy * exx[:, cols]
            dyes.append(dye.astype(bf16))
            oys.append((dye * ch[:, cols]).astype(bf16))
            xt = x * txx[:, cols]
            xts.append(xt.astype(bf16))
            zs.append((xt * qq[:, cols]).astype(bf16))
            zero = jnp.zeros_like(dyb)
            dy2 = jnp.concatenate([jnp.where(low, dyb, zero), jnp.where(low, zero, dyb)], axis=0)
            dm2 = mm_nt(dy2, xb)
            ms = []
            for half in range(2):
                j = 2 * q + half
                spread = sg[rows, j : j + 1] - across[j : j + 1]
                decay = jnp.exp(spread + bias)
                m = decay * sc_ref[k]
                ms.append(m.astype(bf16))
                dm = dm2[half * BLK : (half + 1) * BLK]
                dsc[k] += decay * dm
                e = jnp.where(strict, m * dm, 0.0)
                dsrow_k = jnp.where(col == g * GH + j, jnp.sum(e, axis=1, keepdims=True), dsrow_k)
                ecols.append(jnp.sum(e, axis=0, keepdims=True))
            dx = mm_tn(jnp.concatenate(ms, axis=0), dy2) + qq[:, cols] * txx[:, cols]
            dv = dx * dtx[:, cols] + pv_ref[6:7, cols] * dy
            ddts.append((dx * v).astype(bf16))
            du = dv * (su + v * (1.0 - su))
            dpad[rows, cols] = du
            sv_ref[4:5, cols] += jnp.sum(du, axis=0, keepdims=True)
            for t in range(4):
                sv_ref[t : t + 1, cols] += jnp.sum(du * window[5 + t : 133 + t], axis=0, keepdims=True)
        dscol[pl.ds(pl.multiple_of(g * GH, GH), GH), rows] = jnp.concatenate(ecols, axis=0)
        dye = jnp.concatenate(dyes, axis=1)
        xt = jnp.concatenate(xts, axis=1)
        zsum = mm(jnp.concatenate(zs, axis=1), red)
        ddt[rows] += mm(jnp.concatenate(ddts, axis=1), red)
        hterm = eend[k : k + 1] * jnp.sum(dhcar[...] * hb.astype(f32), axis=0, keepdims=True)
        end = jnp.sum(zsum, axis=0, keepdims=True) + mm_hi(hterm, red.astype(f32))
        add = dsrow_k + mm(jnp.concatenate(oys, axis=1), red) - zsum
        dsrow[rows] += add + jnp.where(row == BLK - 1, end, 0.0)
        dkb[rows, KEY:] += mm_nt(dye, hb)
        dkb[rows, :KEY] += mm_nt(xt, dhb)
        if k:
            dhcar[...] = eend[k : k + 1] * dhcar[...] + mm(kt_ref[KEY:, rows], dye)

    inner_off = groups * GC
    for k in range(blocks):
        rows = slice(k * BLK, (k + 1) * BLK)
        for q in range(GC // KEY):
            cols = slice(q * KEY, (q + 1) * KEY)
            window = dpad[k * BLK : k * BLK + BLK + 8, cols]
            out = pv_ref[3:4, cols] * window[0:BLK]
            for t in range(3):
                out = out + pv_ref[t : t + 1, cols] * window[3 - t : 3 - t + BLK]
            off = pl.multiple_of(inner_off + g * GC + q * KEY, KEY)
            dproj_ref[rows, pl.ds(off, KEY)] = out.astype(bf16)

    @pl.when(g == groups - 1)
    def _():
        keys = dproj_ref.shape[1] - 3 * KEY
        sk_ref[...] = jnp.zeros_like(sk_ref)
        sh_ref[...] = jnp.zeros_like(sh_ref)
        upper = jnp.where(row <= col, 1.0, 0.0).astype(f32)
        for k in range(blocks):
            rows = slice(k * BLK, (k + 1) * BLK)
            window = padk[k * BLK : k * BLK + BLK + 8]
            u = taps_of(window, pk_ref, slice(0, 2 * KEY))
            su = sigmoid(u)
            ds = dsc[k].astype(bf16)
            db = dkb[rows, :KEY] + mm_tn(ds, kb_ref[rows, KEY:])
            dc = dkb[rows, KEY:] + mm(ds, kb_ref[rows, :KEY])
            du = jnp.concatenate([db, dc], axis=1) * (su + u * su * (1.0 - su))
            dpadk[rows] = du
            sk_ref[4:5] += jnp.sum(du, axis=0, keepdims=True)
            for t in range(4):
                sk_ref[t : t + 1] += jnp.sum(du * window[5 + t : 133 + t], axis=0, keepdims=True)
            dla = mm_hi(upper, dsrow[rows] - dscol[:, rows].T)
            z = dtr_ref[rows] + ph_ref[0:1, :]
            rate = jnp.exp(ph_ref[1:2, :])
            dt = jax.nn.softplus(z)
            sh_ref[1:2] += jnp.sum(dla * (-dt * rate), axis=0, keepdims=True)
            dz = (ddt[rows] - dla * rate) * sigmoid(z)
            sh_ref[0:1] += jnp.sum(dz, axis=0, keepdims=True)
            dproj_ref[rows, keys + 2 * KEY :] = dz.astype(bf16)
        for k in range(blocks):
            rows = slice(k * BLK, (k + 1) * BLK)
            window = dpadk[k * BLK : k * BLK + BLK + 8]
            out = pk_ref[3:4] * window[0:BLK]
            for t in range(3):
                out = out + pk_ref[t : t + 1] * window[3 - t : 3 - t + BLK]
            dproj_ref[rows, keys : keys + 2 * KEY] = out.astype(bf16)


def whole_spec(shape):
    return pl.BlockSpec(shape, lambda g: (0,) * len(shape))


def state_specs(length):
    return (
        ((length, KEY), f32),
        ((KEY, length), f32),
        ((3, length, 2 * KEY), bf16),
        ((8, 2 * KEY), bf16),
        ((length, 2 * KEY), bf16),
        ((2 * KEY, length), bf16),
        ((length // BLK, BLK, BLK), f32),
    )


def proj_specs(length, groups):
    wide = groups * GC
    return [
        pl.BlockSpec((length, GC), lambda g: (0, g)),
        pl.BlockSpec((length, GC), lambda g: (0, groups + g)),
        pl.BlockSpec((length, 2 * KEY), lambda g: (0, 2 * wide // (2 * KEY))),
        pl.BlockSpec((length, KEY), lambda g: (0, 2 * wide // KEY + 2)),
        pl.BlockSpec((8, GC), lambda g: (0, g)),
        whole_spec((8, 2 * KEY)),
        whole_spec((8, KEY)),
    ]


def mixer_forward(projected, pv, pk, ph):
    length = projected.shape[0]
    wide = pv.shape[1]
    groups = wide // GC
    blocks = length // BLK
    column = pl.BlockSpec((length, GC), lambda g: (0, g))
    shared = state_specs(length)
    return pl.pallas_call(
        fwd_kernel,
        grid=(groups,),
        in_specs=proj_specs(length, groups),
        out_specs=[
            column,
            column,
            pl.BlockSpec((blocks, KEY, GC), lambda g: (0, 0, g)),
            whole_spec((length, KEY)),
        ]
        + [whole_spec(shape) for shape, _ in shared],
        out_shape=[
            jax.ShapeDtypeStruct((length, wide), f32),
            jax.ShapeDtypeStruct((length, wide), f32),
            jax.ShapeDtypeStruct((blocks, KEY, wide), bf16),
            jax.ShapeDtypeStruct((length, KEY), f32),
        ]
        + [jax.ShapeDtypeStruct(shape, dtype) for shape, dtype in shared],
        scratch_shapes=[
            pltpu.VMEM((length + 8, GC), f32),
            pltpu.VMEM((length + 8, 2 * KEY), f32),
            pltpu.VMEM((length, KEY), f32),
            pltpu.VMEM((KEY, GC), f32),
            pltpu.VMEM((length, KEY), f32),
        ],
        name="mixer_forward",
    )(projected, projected, projected, projected, pv, pk, ph)


def mixer_backward(projected, pv, pk, ph, mixed, grad_gated, states, inverse, pull, shared):
    length, total = projected.shape
    wide = pv.shape[1]
    groups = wide // GC
    blocks = length // BLK
    column = pl.BlockSpec((length, GC), lambda g: (0, g))
    return pl.pallas_call(
        bwd_kernel,
        grid=(groups,),
        in_specs=proj_specs(length, groups)
        + [
            column,
            column,
            pl.BlockSpec((blocks, KEY, GC), lambda g: (0, 0, g)),
            whole_spec((length, KEY)),
            whole_spec((length, KEY)),
        ]
        + [whole_spec(shape) for shape, _ in state_specs(length)],
        out_specs=[
            whole_spec((length, total)),
            pl.BlockSpec((8, GC), lambda g: (0, g)),
            whole_spec((8, 2 * KEY)),
            whole_spec((8, KEY)),
        ],
        out_shape=[
            jax.ShapeDtypeStruct((length, total), bf16),
            jax.ShapeDtypeStruct((8, wide), f32),
            jax.ShapeDtypeStruct((8, 2 * KEY), f32),
            jax.ShapeDtypeStruct((8, KEY), f32),
        ],
        scratch_shapes=[
            pltpu.VMEM((length + 8, GC), f32),
            pltpu.VMEM((length + 8, 2 * KEY), f32),
            pltpu.VMEM((length + 8, GC), f32),
            pltpu.VMEM((length + 8, 2 * KEY), f32),
            pltpu.VMEM((length, KEY), f32),
            pltpu.VMEM((KEY, GC), f32),
            pltpu.VMEM((blocks, BLK, BLK), f32),
            pltpu.VMEM((length, 2 * KEY), f32),
            pltpu.VMEM((length, KEY), f32),
            pltpu.VMEM((KEY, length), f32),
            pltpu.VMEM((length, KEY), f32),
        ],
        name="mixer_backward",
    )(
        projected, projected, projected, projected, pv, pk, ph,
        mixed, grad_gated, states, inverse, pull, *shared,
    )


def pre_norm_inverse(rows):
    return lax.rsqrt(jnp.mean(rows * rows, axis=1, keepdims=True) + epsilon)


AXES = ("dp", "fsdp")
HEAD_LANES = KEY


def gather_rows(shard):
    return lax.all_gather(shard, AXES, axis=0, tiled=True)


def scatter_rows(whole):
    return lax.psum_scatter(whole, AXES, scatter_dimension=0, tiled=True)


def pack_columns(parts, rows, width):
    flat = jnp.concatenate([part.reshape(-1) for part in parts])
    return jnp.pad(flat, (0, rows * width - flat.shape[0])).reshape(rows, width)


def shards(
    hidden, cotangent, lengths, norm_gain, in_proj, dt_proj, conv_weight, conv_bias,
    dt_bias, a_log, skip_gain, gate_gain, out_proj,
):
    length, width = hidden.shape
    assert lengths.shape[0] == 1
    rows_in, columns = in_proj.shape
    heads = dt_bias.shape[0]
    parts = width // rows_in
    taps, conv_part = conv_weight.shape
    gate_part = gate_gain.shape[0]
    wide = gate_part * parts
    small_count = rows_in + taps * conv_part + conv_part + gate_part
    small_width = -(-small_count // (rows_in * 8)) * 8
    total = columns + KEY
    small_at = columns + heads

    small = pack_columns((norm_gain, conv_weight, conv_bias, gate_gain), rows_in, small_width)
    fill = jnp.zeros((rows_in, total - small_at - small_width), bf16)
    packed = jnp.concatenate([in_proj, dt_proj, small, fill], axis=1)
    w_in = gather_rows(packed)
    w_out = gather_rows(out_proj)
    small_all = w_in[:, small_at : small_at + small_width].astype(f32).reshape(parts, -1)
    ends = [rows_in, rows_in + taps * conv_part, small_count - gate_part, small_count]
    gain_one = small_all[:, : ends[0]].reshape(-1)
    conv_taps = jnp.transpose(small_all[:, ends[0] : ends[1]].reshape(parts, taps, conv_part), (1, 0, 2))
    conv_taps = conv_taps.reshape(taps, parts * conv_part)
    conv_shift = small_all[:, ends[1] : ends[2]].reshape(1, -1)
    gain_two = small_all[:, ends[2] : ends[3]].reshape(1, -1)

    rows_wide = hidden.astype(f32)
    live = (jnp.arange(length) < lengths[0]).astype(f32)[:, None]
    inverse_one = pre_norm_inverse(rows_wide)
    normed = (rows_wide * inverse_one * gain_one[None, :]).astype(bf16)
    projected = mm(normed, w_in)

    skip_wide = jnp.repeat(skip_gain.astype(f32), HD)[None]
    pv = jnp.concatenate(
        [conv_taps[:, :wide], conv_shift[:, :wide], gain_two, skip_wide, jnp.zeros((1, wide), f32)], axis=0
    )
    pk = jnp.concatenate([conv_taps[:, wide:], conv_shift[:, wide:], jnp.zeros((3, 2 * KEY), f32)], axis=0)
    ph = jnp.pad(jnp.stack([dt_bias, a_log]).astype(f32), ((0, 6), (0, KEY - heads)))
    mixed, product, states, inverse_two, *shared = mixer_forward(projected, pv, pk, ph)
    inv = inverse_two[:, :1]
    gated = (product * inv * gain_two).astype(bf16)
    output = (rows_wide + live * mm(gated, w_out)).astype(bf16)

    cot_wide = cotangent.astype(f32)
    upstream = (cot_wide * live).astype(bf16)
    grad_gated = mm_nt(upstream, w_out)
    pull = jnp.sum(grad_gated * gain_two * product, axis=1, keepdims=True)
    pull = jnp.broadcast_to(inv * inv * inv * pull / wide, inverse_two.shape)
    grad_proj, sums_v, sums_k, sums_h = mixer_backward(
        projected, pv, pk, ph, mixed, grad_gated, states, inverse_two, pull, shared
    )
    head_sums = lax.psum(
        jnp.concatenate([sums_h[:2, :heads], jnp.sum(sums_v[6].reshape(heads, HD), axis=1)[None]], axis=0), AXES
    )

    grad_normed = mm_nt(grad_proj, w_in)
    scaled = grad_normed * gain_one[None, :]
    dots = jnp.sum(scaled * rows_wide, axis=1, keepdims=True) / width
    grad_rows = inverse_one * scaled - rows_wide * (inverse_one * inverse_one * inverse_one * dots)
    input_grad = cot_wide + grad_rows
    grad_gain_one = jnp.sum(grad_normed * rows_wide * inverse_one, axis=0)

    conv_grad = jnp.concatenate([sums_v[:5], sums_k[:5]], axis=1)
    small_grad = jnp.concatenate(
        [
            grad_gain_one.reshape(parts, rows_in),
            jnp.transpose(conv_grad[:taps].reshape(taps, parts, conv_part), (1, 0, 2)).reshape(parts, -1),
            conv_grad[taps].reshape(parts, conv_part),
            sums_v[5].reshape(parts, gate_part),
            jnp.zeros((parts, rows_in * small_width - small_count), f32),
        ],
        axis=1,
    ).reshape(width, small_width)

    grad_out = scatter_rows(mm_tn(gated, upstream).astype(bf16)).astype(f32)
    grad_in = mm_tn(normed, grad_proj).astype(bf16)
    grad_in = lax.dynamic_update_slice(grad_in, small_grad.astype(bf16), (0, small_at))
    grad_in = scatter_rows(grad_in).astype(f32)
    small_sum = grad_in[:, small_at : small_at + small_width].reshape(-1)
    return (
        output,
        input_grad,
        small_sum[: ends[0]],
        grad_in[:, :columns],
        grad_in[:, columns:small_at],
        small_sum[ends[0] : ends[1]].reshape(taps, conv_part),
        small_sum[ends[1] : ends[2]],
        head_sums[0],
        head_sums[1],
        head_sums[2],
        small_sum[ends[2] : ends[3]],
        grad_out,
    )


def solution(mesh):
    rows = P(AXES, None)
    vector = P(AXES)
    last = P(None, AXES)
    return jax.shard_map(
        shards,
        mesh=mesh,
        in_specs=(rows, rows, vector, vector, rows, rows, last, vector, P(), P(), P(), vector, rows),
        out_specs=(rows, rows, vector, rows, rows, last, vector, P(), P(), P(), vector, rows),
        check_vma=False,
    )
```

time: 1520 us -> 622 us (0.41)
  waiting for transfers between devices: 749 us -> 375 us
  matrix products: 308 us -> 88.4 us
  local copies, waits for them, and re-layouts: 172 us -> 24.8 us
  other arithmetic: 147 us -> 11.8 us
  blocking collectives: 126 us -> 40.1 us
  Pallas kernels: 0 us -> 65.4 us
    reduce_scatter x3 -> x2, waiting for transfers between devices: 675 us -> 205 us  [scatter_rows(): return lax.psum_scatter(whole, AXES, scatter_dimension=0, tiled=True)]
    dot_general x24 -> x6, matrix products: 308 us -> 88.4 us  [the longest x2 31.5 us: mm_nt(): lax.dot_general(a, b, (((1,), (1,)), ((), ())), preferred_element_type=f32)]
    all_gather x2, waiting for transfers between devices: 0.01 us -> 170 us  [gather_rows(): return lax.all_gather(shard, AXES, axis=0, tiled=True)]
    reshape x16 -> x14, local copies, waits for them, and re-layouts: 112 us -> 2.76 us  [the longest x1 0.87 us: pack_columns(): flat = jnp.concatenate([part.reshape(-1) for part in parts])]
    all_gather x2 -> x0, blocking collectives: 81.3 us -> none  [the longest x1 43.5 us: shards(): lax.all_gather(dt_proj, ('dp', 'fsdp'), axis=0, tiled=True)]
    unnamed x7 -> x4, waiting for transfers between devices: 73.7 us -> 0.75 us
    pallas_call x0 -> x2, Pallas kernels: none -> 65.4 us  [the longest x1 45.5 us: mixer_backward(): pl.pallas_call(bwd_kernel, grid=(groups,), in_specs=proj_specs(length, gr...]
    reduce_sum x12 -> x2, other arithmetic: 63.8 us -> 0.49 us  [the longest x1 0.38 us: pre_norm_inverse(): return lax.rsqrt(jnp.mean(rows * rows, axis=1, keepdims=True) + epsilon)]
  transfers between devices with their start and end apart: 6 -> 4, of which waited for: 4 -> 3; matrix products, arithmetic and copies ran while one was open for 22% -> 14% of each run, Pallas kernels for 0% -> 11%
where the time goes in v1:
time: 622 us; the launch traced here: 621 us
  waiting for transfers between devices  375 us (60%)
  matrix products  88.4 us (14%)
  Pallas kernels  65.4 us (11%)
  blocking collectives  40.1 us (6%)
  local copies, waits for them, and re-layouts  24.8 us (4%)
  between operations  14.7 us (2%)
  other arithmetic  11.8 us (2%)
    reduce_scatter x2, waiting for transfers between devices, scatter_rows(): return lax.psum_scatter(whole, AXES, scatter_dimension=0, tiled=True)  205 us
    all_gather x2, waiting for transfers between devices, gather_rows(): return lax.all_gather(shard, AXES, axis=0, tiled=True)  170 us
    pallas_call x1, Pallas kernels, mixer_backward(): pl.pallas_call(bwd_kernel, grid=(groups,), in_specs=proj_specs(length, gr...  45.5 us
    psum x1, blocking collectives, shards(): lax.psum(jnp.concatenate([sums_h[:2, :heads], jnp.sum(sums_v[6].reshape(h...  40.1 us
    dot_general x2, matrix products, mm_nt(): lax.dot_general(a, b, (((1,), (1,)), ((), ())), preferred_element_type=f32)  31.5 us
    dot_general x2, matrix products, mm(): lax.dot_general(a, b, (((1,), (0,)), ((), ())), preferred_element_type=f32)  28.7 us
    dot_general x2, matrix products, mm_tn(): lax.dot_general(a, b, (((0,), (0,)), ((), ())), preferred_element_type=f32)  28.2 us
    pallas_call x1, Pallas kernels, mixer_forward(): pl.pallas_call(fwd_kernel, grid=(groups,), in_specs=proj_specs(length, gr...  19.9 us
  transfers between devices with their start and end apart: 4, of which 3 were waited for; matrix products, arithmetic and copies ran while one was open for 14% of the time, Pallas kernels for 11%

profile of v1, /device:TPU:0, one launch (start us, length us, event | category | flops | bytes accessed | tf_op | source)
XLA Modules:
  0.0 620.6 jit_solution(5423005356774545661)
XLA Ops:
  7.2 0.9 reshape.98
  8.1 0.8 fusion.33
  9.0 1.9 concatenate.23
  12.3 0.7 broadcast_in_dim.32
  13.2 1.3 fusion.30.ph_ref
  14.9 128.8 %all-gather.3.cloned.1.call-done = bf16[1536,6528]{1,0:T(8,128)(2,1)} async-done(((bf16[48,6528]{1,0:T(8,128)(2,1)}), bf16[1536,6528]{1,0:T(8,128)(2,1)}) %all-gather.3.cloned.1.call-update) | async-done | bytes 20054032 | tf_op jit(solution)/shard_map/all_gather | solution.py:444
  143.7 1.2 slice_convert_fusion
  146.1 0.7 concatenate.24.pv_ref
  147.5 17.7 %fusion.13.gate_ref.rawv_ref.rawk_ref.dtr_ref = f32[512,6528]{1,0:T(8,128)} fusion(bf16[1536,6528]{1,0:T(8,128)(2,1)} %all-gather.3.cloned.1.call-done, bf16[512,1536]{1,0:T(8,128)(2,1)S(1)} %copy-done, f32[1536]{0:T(1024)S(1)} %mul.133, f32[512]{0:T(512)S(1)} %add_rsqrt_fusion), kind=kOutput, calls=%fused_computation.23 | convolution fusion | flops 10270801920 | bytes 35004416 | tf_op jit(solution)/shard_map/dot_general | solution.py:27
  165.2 19.9 %mixer_forward.1 = (f32[512,3072]{1,0:T(8,128)}, f32[512,3072]{1,0:T(8,128)}, bf16[4,128,3072]{2,1,0:T(8,128)(2,1)}, f32[512,128]{1,0:T(8,128)}, f32[512,128]{1,...) custom-call(f32[512,6528]{1,0:T(8,128)} %fusion.13.gate_ref.rawv_ref, ...), custom_call_target="tpu_custom_call" | custom-call | tf_op jit(solution)/shard_map/mixer_forward/pallas_call | solution.py:356
  185.1 41.2 %all-gather.5.cloned.1.call-done = bf16[3072,1536]{1,0:T(8,128)(2,1)} async-done(((bf16[96,1536]{1,0:T(8,128)(2,1)}), bf16[3072,1536]{1,0:T(8,128)(2,1)}) %all-gather.5.cloned.1.call-update) | async-done | bytes 9437200 | tf_op jit(solution)/shard_map/all_gather | solution.py:444
  226.3 11.9 %multiply_reduce_fusion = (f32[512]{0:T(512)S(1)}, f32[512,3072]{1,0:T(8,128)}) fusion(f32[512,3072]{1,0:T(8,128)} %get-tuple-element.27, f32[3072]{0:T(1024)S(1)} %mul.139, bf16[3072,1536]{1,0:T(8,128)(2,1)} %all-gather.5.cloned.1.call-done, bf16[512,1536]{1,0:T(8,128)(2,1)S(1)} %copy-done.1, f32[512]{0:T(512)S(1)} %fusion.34), kind=kOutput, calls=%fused_computation.8 | convolution fusion | flops 4838915584 | bytes 23609344 | tf_op jit(solution)/shard_map/dot_general | solution.py:31
  238.1 0.9 copy.30
  239.0 1.2 fusion.17
  240.2 11.0 %convolution_convert_fusion.1 = bf16[3072,1536]{1,0:T(8,128)(2,1)} fusion(bf16[512,1536]{1,0:T(8,128)(2,1)S(1)} %copy-done.1, f32[512]{0:T(512)S(1)} %fusion.34, f32[512,3072]{1,0:T(8,128)} %get-tuple-element.27, f32[3072]{0:T(1024)S(1)} %mul.139, f32[512]{0:T(512)S(1)} %get-tuple-element.45), kind=kOutput, calls=%fused_computation.1 | convolution fusion | flops 4843634688 | bytes 17317888 | tf_op jit(solution)/shard_map/dot_general | solution.py:35
  251.3 0.8 broadcast_in_dim.37.c_ref
  252.1 45.5 %mixer_backward.1 = (bf16[512,6528]{1,0:T(8,128)(2,1)}, f32[8,3072]{1,0:T(8,128)}, f32[8,256]{1,0:T(8,128)}, f32[8,128]{1,0:T(8,128)}) custom-call(f32[512,6528]{1,0:T(8,128)} %fusion.13.gate_ref.rawv_ref.rawk_ref.dtr_ref, f32[512,6528]{1,0:T(8,128)} %fusion.13.gate_ref.rawv_ref.rawk_ref.dtr_ref, f32[512,6528]{1,0:T(8,128)} %fusion.13.gate_ref.rawv_ref.rawk_ref.dtr_ref, ...), custom_call_target="tpu_custom_call" | custom-call | tf_op jit(solution)/shard_map/mixer_backward/pallas_call | solution.py:391
  297.6 19.6 %fusion.8 = (bf16[1536]{0:T(1024)(128)(2,1)S(1)}, f32[512]{0:T(512)}, f32[512,1536]{1,0:T(8,128)}) fusion(bf16[512,1536]{1,0:T(8,128)(2,1)S(1)} %copy-done, f32[512]{0:T(512)S(1)} %add_rsqrt_fusion, f32[1536]{0:T(1024)S(1)} %mul.133, bf16[512,6528]{1,0:T(8,128)(2,1)} %get-tuple-element.38, bf16[1536,6528]{1,0:T(8,128)(2,1)} %all-gather.3.cloned.1.call-done), kind=kOutput, calls=%fused_computation.21 | convolution fusion | flops 10273159168 | bytes 31470592 | tf_op jit(solution)/shard_map/dot_general | solution.py:31
  317.9 0.7 concatenate.27
  318.7 1.1 convert_element_type.59
  319.8 17.3 %convolution_convert_fusion = bf16[1536,6528]{1,0:T(8,128)(2,1)} fusion(bf16[512,6528]{1,0:T(8,128)(2,1)} %get-tuple-element.38, bf16[512,1536]{1,0:T(8,128)(2,1)S(1)} %copy-done, f32[1536]{0:T(1024)S(1)} %mul.133, f32[512]{0:T(512)S(1)} %add_rsqrt_fusion), kind=kOutput, calls=%fused_computation | convolution fusion | flops 10280828928 | bytes 28319744 | tf_op jit(solution)/shard_map/dot_general | solution.py:35
  337.1 4.5 dynamic_update_slice.3
  341.6 0.9 slice_reduce_fusion.1
  343.4 40.1 %psum.7 = f32[3,48]{1,0:T(4,128)S(1)} all-reduce(f32[3,48]{1,0:T(4,128)S(1)} %pad_maximum_fusion), channel_id=1, replica_groups=mesh['dp'=8,'fsdp'=4] {'dp','fsdp'}, use_global_device_ids=true, to_apply=%region_6.7 | all-reduce | flops 144 | bytes 1152 | tf_op jit(solution)/shard_map/psum | solution.py:511
  384.1 4.3 convert_add_fusion.1
  388.4 11.0 %fusion.4 = bf16[512,1536]{1,0:T(8,128)(2,1)} fusion(bf16[512,1536]{1,0:T(8,128)(2,1)S(1)} %copy-done, bf16[3072,1536]{1,0:T(8,128)(2,1)} %all-gather.5.cloned.1.call-done, f32[512]{0:T(512)S(1)} %copy-done.10, f32[512,3072]{1,0:T(8,128)} %get-tuple-element.27, f32[3072]{0:T(1024)S(1)} %copy-done.5, f32[512]{0:T(512)S(1)} %copy-done.7), kind=kOutput, calls=%fused_computation.17 | convolution fusion | flops 4839702528 | bytes 18890752 | tf_op jit(solution)/shard_map/dot_general | solution.py:27
  399.4 1.8 convert_element_type.62
  401.3 204.6 %reduce-scatter.3.cloned.1.call-done = bf16[48,6528]{1,0:T(8,128)(2,1)} async-done(((bf16[1536,6528]{1,0:T(8,128)(2,1)}), bf16[48,6528]{1,0:T(8,128)(2,1)}) %reduce-scatter.3.cloned.1.call-update) | async-done | bytes 626704 | tf_op jit(solution)/shard_map/reduce_scatter | solution.py:448
  605.9 0.8 slice.133
  609.2 0.8 slice.132
  610.6 2.2 slice.130
  612.8 1.3 slice.131
  (84 shorter events, 8.7 us)
Async XLA Ops:
  7.2 7.3 %copy-start = (bf16[512,1536]{1,0:T(8,128)(2,1)S(1)}, bf16[512,1536]{1,0:T(8,128)(2,1)}, u32[]{:S(2)}) copy-start(bf16[512,1536]{1,0:T(8,128)(2,1)} %param.13) | copy-start | bytes 4718596
  7.2 136.5 %all-gather.3.cloned.1.call-start = ((), (), s32[]{:S(2)}) async-start(), calls=%async_computation.2 | async-start | bytes 20680704 | tf_op jit(solution)/shard_map/all_gather | solution.py:444
  10.9 215.4 %all-gather.5.cloned.1.call-start = ((), (), s32[]{:S(2)}) async-start(), calls=%async_computation.3 | async-start | bytes 9732096 | tf_op jit(solution)/shard_map/all_gather | solution.py:444
  11.6 387.8 %reduce-scatter.5.cloned.1.call-start = ((), (), s32[]{:S(2)}) async-start(), calls=%async_computation.5 | async-start | bytes 9732096 | tf_op jit(solution)/shard_map/reduce_scatter | solution.py:448
  13.2 226.9 %copy-start.9 = (f32[512]{0:T(512)}, f32[512]{0:T(512)S(1)}, u32[]{:S(2)}) copy-start(f32[512]{0:T(512)S(1)} %fusion.34) | copy-start | bytes 6148
  146.0 94.2 %copy-start.4 = (f32[3072]{0:T(1024)}, f32[3072]{0:T(1024)S(1)}, u32[]{:S(2)}) copy-start(f32[3072]{0:T(1024)S(1)} %mul.139) | copy-start | bytes 36868
  165.2 61.1 %copy-start.1 = (bf16[512,1536]{1,0:T(8,128)(2,1)S(1)}, bf16[512,1536]{1,0:T(8,128)(2,1)}, u32[]{:S(2)}) copy-start(bf16[512,1536]{1,0:T(8,128)(2,1)} %param.14) | copy-start | bytes 4718596
  226.3 12.7 %copy-start.2 = (f32[512,128]{1,0:T(8,128)S(1)}, f32[512,128]{1,0:T(8,128)}, u32[]{:S(2)}) copy-start(f32[512,128]{1,0:T(8,128)} %get-tuple-element.28.r_ref) | copy-start | bytes 786436
  240.2 11.0 %copy-start.6 = (f32[512]{0:T(512)}, f32[512]{0:T(512)S(1)}, u32[]{:S(2)}) copy-start(f32[512]{0:T(512)S(1)} %get-tuple-element.45) | copy-start | bytes 6148
  251.2 354.7 %reduce-scatter.3.cloned.1.call-start = ((), (), s32[]{:S(2)}) async-start(), calls=%async_computation.4 | async-start | bytes 20680704 | tf_op jit(solution)/shard_map/reduce_scatter | solution.py:448
  297.6 19.7 %copy-start.11 = (f32[8,256]{1,0:T(8,128)S(1)}, f32[8,256]{1,0:T(8,128)}, u32[]{:S(2)}) copy-start(f32[8,256]{1,0:T(8,128)} %get-tuple-element.40) | copy-start | bytes 24580
  297.6 19.7 %copy-start.3 = (f32[8,3072]{1,0:T(8,128)S(1)}, f32[8,3072]{1,0:T(8,128)}, u32[]{:S(2)}) copy-start(f32[8,3072]{1,0:T(8,128)} %get-tuple-element.39) | copy-start | bytes 294916
  341.6 42.5 %copy-start.8 = (f32[512]{0:T(512)S(1)}, f32[512]{0:T(512)}, u32[]{:S(2)}) copy-start(f32[512]{0:T(512)} %get-tuple-element.43) | copy-start | bytes 6148
  384.0 4.4 copy-start.5
  384.1 4.4 copy-start.7
  384.1 4.4 copy-start.10
Sparse Core Ops, SparseCore 0:
  11.5 132.1 all-gather.2
  146.6 79.6 all-gather.4
  251.3 135.5 reduce-scatter.4
  393.2 212.6 reduce-scatter.2

commit v2 on v1

--- a/solution.py
+++ b/solution.py
@@ -161,8 +161,6 @@
     g = pl.program_id(0)
     length = gate_ref.shape[0]
     blocks = length // BLK
-    groups = gate_ref.shape[1] // GC
-    inner = dproj_ref.shape[1] // 2 - 3 * KEY // 2
     groups = pl.num_programs(0)
 
     @pl.when(g == 0)
@@ -283,7 +281,7 @@
 
     @pl.when(g == groups - 1)
     def _():
-        keys = dproj_ref.shape[1] - 3 * KEY
+        keys = 2 * groups * GC
         sk_ref[...] = jnp.zeros_like(sk_ref)
         sh_ref[...] = jnp.zeros_like(sh_ref)
         upper = jnp.where(row <= col, 1.0, 0.0).astype(f32)
@@ -307,7 +305,8 @@
             sh_ref[1:2] += jnp.sum(dla * (-dt * rate), axis=0, keepdims=True)
             dz = (ddt[rows] - dla * rate) * sigmoid(z)
             sh_ref[0:1] += jnp.sum(dz, axis=0, keepdims=True)
-            dproj_ref[rows, keys + 2 * KEY :] = dz.astype(bf16)
+            dproj_ref[rows, keys + 2 * KEY : keys + 3 * KEY] = dz.astype(bf16)
+            dproj_ref[rows, keys + 3 * KEY :] = jnp.zeros((BLK, dproj_ref.shape[1] - keys - 3 * KEY), bf16)
         for k in range(blocks):
             rows = slice(k * BLK, (k + 1) * BLK)
             window = dpadk[k * BLK : k * BLK + BLK + 8]
@@ -432,6 +431,300 @@
     )
 
 
+MESH = pl.DeviceIdType.MESH
+HALF = 256
+
+
+def places():
+    d, f = lax.axis_index("dp"), lax.axis_index("fsdp")
+    z, x, y, c = d // 2, d % 2, f // 2, f % 2
+    over_core = (d, y * 2 + 1 - c)
+    over_x = (z * 2 + 1 - x, f)
+    over_y = (d, (1 - y) * 2 + c)
+    far = (((z + 2) % 4) * 2 + x, f)
+    near = ((z + 1 - 2 * (z % 2)) * 2 + x, f)
+    peers = ((over_core, over_x, over_y, far, near), (over_core, over_y, over_x, far, near))
+    own = ((c, x, y, z // 2, z % 2), (c, y, x, z // 2, z % 2))
+    return peers, own
+
+
+def greet(partners):
+    barrier = pltpu.get_barrier_semaphore()
+    for partner in partners:
+        pl.semaphore_signal(barrier, inc=1, device_id=partner, device_id_type=MESH)
+    pl.semaphore_wait(barrier, len(partners))
+
+
+def block_order(half, i):
+    z, x, y, c = i // 8, i // 4 % 2, i // 2 % 2, i % 2
+    first, second = (x, y) if half == 0 else (y, x)
+    return c, first * 8 + second * 4 + z
+
+
+def scatter_kernel(
+    n, rb, lhs_ref, rhs_ref, extra_ref, head_ref, out_ref, sums_ref,
+    parts, r0, r1, r2, r3, r4, sums, sums_in, send, recv, sums_sem,
+):
+    peers, own = places()
+    held = (r0, r1, r2, r3, r4)
+    greet(peers[0])
+
+    def sums_copy(stage):
+        return pltpu.make_async_remote_copy(
+            src_ref=sums.at[stage],
+            dst_ref=sums_in.at[stage],
+            send_sem=sums_sem.at[0, stage],
+            recv_sem=sums_sem.at[1, stage],
+            device_id=peers[0][stage],
+            device_id_type=MESH,
+        )
+
+    sums[0] = head_ref[...]
+    sums_copy(0).start()
+
+    def copy(stage, i, half):
+        count = 16 >> stage
+        if stage == 0:
+            src = parts.at[lax.rem(i, 2), 1 - own[half][0], half]
+        else:
+            src = held[stage - 1].at[i, half, pl.ds((1 - own[half][stage]) * count, count)]
+        return pltpu.make_async_remote_copy(
+            src_ref=src,
+            dst_ref=held[stage].at[i, half],
+            send_sem=send.at[i, half, stage],
+            recv_sem=recv.at[i, half, stage],
+            device_id=peers[half][stage],
+            device_id_type=MESH,
+        )
+
+    def tick(t, carry):
+        @pl.when(t < n)
+        def _():
+            slot = lax.rem(t, 2)
+
+            @pl.when(t >= 2)
+            def _():
+                for half in range(2):
+                    copy(0, t - 2, half).wait_send()
+
+            for half in range(2):
+                cols = pl.ds(pl.multiple_of(t * 2 * HALF + half * HALF, HALF), HALF)
+                right = rhs_ref[:, cols]
+                for z in range(4):
+                    rows = slice(z * 8 * rb, (z + 1) * 8 * rb)
+                    res = lax.dot_general(
+                        lhs_ref[rows], right, (((1,), (0,)), ((), ())), preferred_element_type=f32
+                    )
+                    for b in range(8):
+                        c, at = block_order(half, z * 8 + b)
+                        parts[slot, c, half, at] = res[b * rb : (b + 1) * rb].astype(bf16)
+
+            @pl.when(t == n - 1)
+            def _():
+                for i in range(32):
+                    c, at = block_order(1, i)
+                    rows = slice(i * rb, (i + 1) * rb)
+                    parts[slot, c, 1, at, :, :KEY] = (
+                        parts[slot, c, 1, at, :, :KEY].astype(f32) + extra_ref[rows]
+                    ).astype(bf16)
+
+            for half in range(2):
+                copy(0, t, half).start()
+
+        for stage in range(5):
+            i = t - stage - 1
+
+            @pl.when(i == 0)
+            def _(stage=stage):
+                sums_copy(stage).wait()
+                if stage < 4:
+                    sums[stage + 1] = sums[stage] + sums_in[stage]
+                    sums_copy(stage + 1).start()
+                else:
+                    sums_ref[...] = sums[stage] + sums_in[stage]
+
+            @pl.when((i >= 0) & (i < n))
+            def _(stage=stage, i=i):
+                count = 16 >> stage
+                for half in range(2):
+                    done = copy(stage, i, half)
+                    if stage == 0:
+                        done.wait_recv()
+                        mine = parts[lax.rem(i, 2), own[half][0], half]
+                    else:
+                        done.wait()
+                        mine = held[stage - 1][i, half, pl.ds(own[half][stage] * count, count)]
+                    if stage < 4:
+                        held[stage][i, half] = (
+                            held[stage][i, half].astype(f32) + mine.astype(f32)
+                        ).astype(bf16)
+                        copy(stage + 1, i, half).start()
+                    else:
+                        cols = pl.ds(pl.multiple_of(i * 2 * HALF + half * HALF, HALF), HALF)
+                        out_ref[:, cols] = held[stage][i, half, 0].astype(f32) + mine[0].astype(f32)
+
+        return carry
+
+    lax.fori_loop(0, n + 5, tick, 0)
+    for i in (n - 2, n - 1):
+        for half in range(2):
+            copy(0, i, half).wait_send()
+
+
+def scatter_product(lhs, rhs, extra, heads):
+    rows, depth = lhs.shape
+    columns = rhs.shape[1]
+    n, rb = columns // (2 * HALF), rows // 32
+    vmem = pl.BlockSpec(memory_space=pltpu.VMEM)
+    return pl.pallas_call(
+        partial(scatter_kernel, n, rb),
+        out_shape=(jax.ShapeDtypeStruct((rb, columns), f32), jax.ShapeDtypeStruct(heads.shape, f32)),
+        in_specs=[vmem] * 4,
+        out_specs=(vmem, vmem),
+        scratch_shapes=[pltpu.VMEM((2, 2, 2, 16, rb, HALF), bf16)]
+        + [pltpu.VMEM((n, 2, 16 >> stage, rb, HALF), bf16) for stage in range(5)]
+        + [pltpu.VMEM((5,) + heads.shape, f32)] * 2
+        + [pltpu.SemaphoreType.DMA((n, 2, 5))] * 2
+        + [pltpu.SemaphoreType.DMA((2, 5))],
+        compiler_params=pltpu.CompilerParams(
+            collective_id=1, has_side_effects=True, vmem_limit_bytes=60 << 20
+        ),
+        name="scatter_product",
+    )(lhs, rhs, extra, heads)
+
+
+def gather_kernel(
+    n, gain_at, hidden_ref, w_ref, w_out, proj_out, normed_ref, flipped_ref,
+    held, w_stage, proj_stage, send, recv, out_sem,
+):
+    rb = w_ref.shape[0]
+    peers, own = places()
+    greet(peers[0])
+    base = [own[h][0] * 16 + own[h][1] * 8 + own[h][2] * 4 + own[h][3] * 2 + own[h][4] for h in range(2)]
+    count = (1, 2, 4, 8, 16)
+    source = lambda i: lax.rem(i + n - 1, n)
+
+    def columns(i, half):
+        return pl.ds(pl.multiple_of(source(i) * 2 * HALF + half * HALF, HALF), HALF)
+
+    def copy(stage, i, half):
+        start = base[half] // count[stage] * count[stage]
+        block = held.at[i, half, pl.ds(start, count[stage])]
+        return pltpu.make_async_remote_copy(
+            src_ref=block,
+            dst_ref=block,
+            send_sem=send.at[i, half, stage],
+            recv_sem=recv.at[i, half, stage],
+            device_id=peers[half][4 - stage],
+            device_id_type=MESH,
+        )
+
+    def stores(i):
+        slot = lax.rem(i, 2)
+        cols = pl.ds(pl.multiple_of(source(i) * 2 * HALF, 2 * HALF), 2 * HALF)
+        return (
+            pltpu.make_async_copy(w_stage.at[slot], w_out.at[:, cols], out_sem.at[0, slot]),
+            pltpu.make_async_copy(proj_stage.at[slot], proj_out.at[:, cols], out_sem.at[1, slot]),
+        )
+
+    def land(i, carry):
+        for half in range(2):
+            held[i, half, base[half]] = w_ref[:, columns(i, half)]
+        return carry
+
+    lax.fori_loop(0, n, land, 0)
+
+    def tick(t, carry):
+        @pl.when(t < n)
+        def _():
+            for half in range(2):
+                copy(0, t, half).start()
+
+        for stage in range(5):
+            i = t - stage - 1
+
+            @pl.when((i >= 0) & (i < n))
+            def _(stage=stage, i=i):
+                for half in range(2):
+                    copy(stage, i, half).wait()
+                    if stage < 4:
+                        copy(stage + 1, i, half).start()
+                if stage == 4:
+                    slot = lax.rem(i, 2)
+
+                    @pl.when(i >= 2)
+                    def _():
+                        for store in stores(i - 2):
+                            store.wait()
+
+                    for half in range(2):
+                        for b in range(32):
+                            c, at = block_order(half, b)
+                            w_stage[slot, b * rb : (b + 1) * rb, half * HALF : (half + 1) * HALF] = held[
+                                i, half, c * 16 + at
+                            ]
+
+                    @pl.when(i == 0)
+                    def _():
+                        tile = w_stage[slot, :, HALF : HALF + KEY].astype(f32)
+                        gain = tile.T[gain_at : gain_at + 1]
+                        for k in range(0, hidden_ref.shape[0], KEY):
+                            wide = hidden_ref[k : k + KEY].astype(f32)
+                            mean = jnp.mean(wide * wide, axis=1, keepdims=True)
+                            normed = (wide * lax.rsqrt(mean + epsilon) * gain).astype(bf16)
+                            normed_ref[k : k + KEY] = normed
+                            flipped_ref[:, k : k + KEY] = normed.T
+
+                    for half in range(2):
+                        cols = slice(half * HALF, (half + 1) * HALF)
+                        proj_stage[slot, :, cols] = lax.dot_general(
+                            normed_ref[...],
+                            w_stage[slot, :, cols],
+                            (((1,), (0,)), ((), ())),
+                            preferred_element_type=f32,
+                        )
+                    for store in stores(i):
+                        store.start()
+
+        return carry
+
+    lax.fori_loop(0, n + 5, tick, 0)
+    for i in (n - 2, n - 1):
+        for store in stores(i):
+            store.wait()
+
+
+def gather_product(hidden, shard, gain_at):
+    length, width = hidden.shape
+    rb, columns = shard.shape
+    n = columns // (2 * HALF)
+    vmem = pl.BlockSpec(memory_space=pltpu.VMEM)
+    anywhere = pl.BlockSpec(memory_space=pl.ANY)
+    return pl.pallas_call(
+        partial(gather_kernel, n, gain_at),
+        out_shape=(
+            jax.ShapeDtypeStruct((width, columns), bf16),
+            jax.ShapeDtypeStruct((length, columns), f32),
+            jax.ShapeDtypeStruct((length, width), bf16),
+            jax.ShapeDtypeStruct((width, length), bf16),
+        ),
+        in_specs=[vmem, vmem],
+        out_specs=(anywhere, anywhere, vmem, vmem),
+        scratch_shapes=[
+            pltpu.VMEM((n, 2, 32, rb, HALF), bf16),
+            pltpu.VMEM((2, width, 2 * HALF), bf16),
+            pltpu.VMEM((2, length, 2 * HALF), f32),
+            pltpu.SemaphoreType.DMA((n, 2, 5)),
+            pltpu.SemaphoreType.DMA((n, 2, 5)),
+            pltpu.SemaphoreType.DMA((2, 2)),
+        ],
+        compiler_params=pltpu.CompilerParams(
+            collective_id=2, has_side_effects=True, vmem_limit_bytes=60 << 20
+        ),
+        name="gather_product",
+    )(hidden, shard)
+
+
 def pre_norm_inverse(rows):
     return lax.rsqrt(jnp.mean(rows * rows, axis=1, keepdims=True) + epsilon)
 
@@ -454,7 +747,7 @@
 
 
 def shards(
-    hidden, cotangent, lengths, norm_gain, in_proj, dt_proj, conv_weight, conv_bias,
+    kernels, hidden, cotangent, lengths, norm_gain, in_proj, dt_proj, conv_weight, conv_bias,
     dt_bias, a_log, skip_gain, gate_gain, out_proj,
 ):
     length, width = hidden.shape
@@ -465,29 +758,33 @@
     taps, conv_part = conv_weight.shape
     gate_part = gate_gain.shape[0]
     wide = gate_part * parts
-    small_count = rows_in + taps * conv_part + conv_part + gate_part
-    small_width = -(-small_count // (rows_in * 8)) * 8
-    total = columns + KEY
-    small_at = columns + heads
-
-    small = pack_columns((norm_gain, conv_weight, conv_bias, gate_gain), rows_in, small_width)
+    small_count = taps * conv_part + conv_part + gate_part
+    small_width = -(-small_count // rows_in)
+    total = columns + 2 * KEY
+    gain_at = columns + heads
+    small_at = gain_at + 1
+
+    small = pack_columns((conv_weight, conv_bias, gate_gain), rows_in, small_width)
     fill = jnp.zeros((rows_in, total - small_at - small_width), bf16)
-    packed = jnp.concatenate([in_proj, dt_proj, small, fill], axis=1)
-    w_in = gather_rows(packed)
+    packed = jnp.concatenate([in_proj, dt_proj, norm_gain[:, None], small, fill], axis=1)
     w_out = gather_rows(out_proj)
+    rows_wide = hidden.astype(f32)
+    inverse_one = pre_norm_inverse(rows_wide)
+    if kernels:
+        w_in, projected, normed, flipped = gather_product(hidden, packed, heads)
+        gain_one = w_in[:, gain_at].astype(f32)
+    else:
+        w_in = gather_rows(packed)
+        gain_one = w_in[:, gain_at].astype(f32)
+        normed = (rows_wide * inverse_one * gain_one[None, :]).astype(bf16)
+        projected = mm(normed, w_in)
     small_all = w_in[:, small_at : small_at + small_width].astype(f32).reshape(parts, -1)
-    ends = [rows_in, rows_in + taps * conv_part, small_count - gate_part, small_count]
-    gain_one = small_all[:, : ends[0]].reshape(-1)
-    conv_taps = jnp.transpose(small_all[:, ends[0] : ends[1]].reshape(parts, taps, conv_part), (1, 0, 2))
+    ends = [taps * conv_part, small_count - gate_part, small_count]
+    conv_taps = jnp.transpose(small_all[:, : ends[0]].reshape(parts, taps, conv_part), (1, 0, 2))
     conv_taps = conv_taps.reshape(taps, parts * conv_part)
-    conv_shift = small_all[:, ends[1] : ends[2]].reshape(1, -1)
-    gain_two = small_all[:, ends[2] : ends[3]].reshape(1, -1)
-
-    rows_wide = hidden.astype(f32)
+    conv_shift = small_all[:, ends[0] : ends[1]].reshape(1, -1)
+    gain_two = small_all[:, ends[1] : ends[2]].reshape(1, -1)
     live = (jnp.arange(length) < lengths[0]).astype(f32)[:, None]
-    inverse_one = pre_norm_inverse(rows_wide)
-    normed = (rows_wide * inverse_one * gain_one[None, :]).astype(bf16)
-    projected = mm(normed, w_in)
 
     skip_wide = jnp.repeat(skip_gain.astype(f32), HD)[None]
     pv = jnp.concatenate(
@@ -508,9 +805,8 @@
     grad_proj, sums_v, sums_k, sums_h = mixer_backward(
         projected, pv, pk, ph, mixed, grad_gated, states, inverse_two, pull, shared
     )
-    head_sums = lax.psum(
-        jnp.concatenate([sums_h[:2, :heads], jnp.sum(sums_v[6].reshape(heads, HD), axis=1)[None]], axis=0), AXES
-    )
+    skip_grad = jnp.pad(jnp.sum(sums_v[6].reshape(heads, HD), axis=1), (0, KEY - heads))[None]
+    head_grads = jnp.concatenate([sums_h[:2], skip_grad, jnp.zeros((5, KEY), f32)], axis=0)
 
     grad_normed = mm_nt(grad_proj, w_in)
     scaled = grad_normed * gain_one[None, :]
@@ -522,7 +818,6 @@
     conv_grad = jnp.concatenate([sums_v[:5], sums_k[:5]], axis=1)
     small_grad = jnp.concatenate(
         [
-            grad_gain_one.reshape(parts, rows_in),
             jnp.transpose(conv_grad[:taps].reshape(taps, parts, conv_part), (1, 0, 2)).reshape(parts, -1),
             conv_grad[taps].reshape(parts, conv_part),
             sums_v[5].reshape(parts, gate_part),
@@ -530,24 +825,37 @@
         ],
         axis=1,
     ).reshape(width, small_width)
+    extra = jnp.concatenate(
+        [
+            jnp.zeros((width, heads), f32),
+            grad_gain_one[:, None],
+            small_grad,
+            jnp.zeros((width, KEY - heads - 1 - small_width), f32),
+        ],
+        axis=1,
+    )
 
     grad_out = scatter_rows(mm_tn(gated, upstream).astype(bf16)).astype(f32)
-    grad_in = mm_tn(normed, grad_proj).astype(bf16)
-    grad_in = lax.dynamic_update_slice(grad_in, small_grad.astype(bf16), (0, small_at))
-    grad_in = scatter_rows(grad_in).astype(f32)
+    if kernels:
+        grad_in, head_sums = scatter_product(flipped, grad_proj, extra, head_grads)
+    else:
+        head_sums = lax.psum(head_grads, AXES)
+        grad_in = mm_tn(normed, grad_proj)
+        grad_in = grad_in + jnp.pad(extra, ((0, 0), (columns, total - columns - KEY)))
+        grad_in = scatter_rows(grad_in.astype(bf16)).astype(f32)
     small_sum = grad_in[:, small_at : small_at + small_width].reshape(-1)
     return (
         output,
         input_grad,
-        small_sum[: ends[0]],
+        grad_in[:, gain_at],
         grad_in[:, :columns],
-        grad_in[:, columns:small_at],
-        small_sum[ends[0] : ends[1]].reshape(taps, conv_part),
+        grad_in[:, columns:gain_at],
+        small_sum[: ends[0]].reshape(taps, conv_part),
+        small_sum[ends[0] : ends[1]],
+        head_sums[0, :heads],
+        head_sums[1, :heads],
+        head_sums[2, :heads],
         small_sum[ends[1] : ends[2]],
-        head_sums[0],
-        head_sums[1],
-        head_sums[2],
-        small_sum[ends[2] : ends[3]],
         grad_out,
     )
 
@@ -557,7 +865,7 @@
     vector = P(AXES)
     last = P(None, AXES)
     return jax.shard_map(
-        shards,
+        partial(shards, mesh.shape["dp"] == 8 and mesh.shape["fsdp"] == 4),
         mesh=mesh,
         in_specs=(rows, rows, vector, vector, rows, rows, last, vector, P(), P(), P(), vector, rows),
         out_specs=(rows, rows, vector, rows, rows, last, vector, P(), P(), P(), vector, rows),

time: 622 us -> 433 us (0.70)
  waiting for transfers between devices: 375 us -> 0.72 us
  Pallas kernels: 65.4 us -> 328 us
  blocking collectives: 40.1 us -> 0 us
  matrix products: 88.4 us -> 52.1 us
    pallas_call x0 -> x2, Pallas kernels: none -> 261 us  [the longest x1 144 us: gather_product(): pl.pallas_call(partial(gather_kernel, n, gain_at), out_shape=(jax.ShapeDt...]
    reduce_scatter x2 -> x1, waiting for transfers between devices: 205 us -> 0.01 us  [scatter_rows(): return lax.psum_scatter(whole, AXES, scatter_dimension=0, tiled=True)]
    all_gather x2 -> x1, waiting for transfers between devices: 170 us -> 0.02 us  [gather_rows(): return lax.all_gather(shard, AXES, axis=0, tiled=True)]
    psum x1 -> x0, blocking collectives: 40.1 us -> none  [shards(): lax.psum(jnp.concatenate([sums_h[:2, :heads], jnp.sum(sums_v[6].reshape(h...]
    dot_general x2 -> x1, matrix products: 28.7 us -> 11 us  [mm(): lax.dot_general(a, b, (((1,), (0,)), ((), ())), preferred_element_type=f32)]
    dot_general x2 -> x1, matrix products: 28.2 us -> 11 us  [mm_tn(): lax.dot_general(a, b, (((0,), (0,)), ((), ())), preferred_element_type=f32)]
  transfers between devices with their start and end apart: 4 -> 2, of which waited for: 3 -> 0; matrix products, arithmetic and copies ran while one was open for 14% -> 15% of each run, Pallas kernels for 11% -> 76%
where the time goes in v2:
time: 433 us; the launch traced here: 432 us
  Pallas kernels  328 us (76%)
  matrix products  52.1 us (12%)
  local copies, waits for them, and re-layouts  20.5 us (5%)
  other arithmetic  15.5 us (4%)
  between operations  15 us (3%)
    pallas_call x1, Pallas kernels, gather_product(): pl.pallas_call(partial(gather_kernel, n, gain_at), out_shape=(jax.ShapeDt...  144 us
    pallas_call x1, Pallas kernels, scatter_product(): pl.pallas_call(partial(scatter_kernel, n, rb), out_shape=(jax.ShapeDtypeS...  117 us
    pallas_call x1, Pallas kernels, mixer_backward(): pl.pallas_call(bwd_kernel, grid=(groups,), in_specs=proj_specs(length, gr...  46.8 us
    dot_general x2, matrix products, mm_nt(): lax.dot_general(a, b, (((1,), (1,)), ((), ())), preferred_element_type=f32)  30.2 us
    pallas_call x1, Pallas kernels, mixer_forward(): pl.pallas_call(fwd_kernel, grid=(groups,), in_specs=proj_specs(length, gr...  20.2 us
    dot_general x1, matrix products, mm_tn(): lax.dot_general(a, b, (((0,), (0,)), ((), ())), preferred_element_type=f32)  11 us
    dot_general x1, matrix products, mm(): lax.dot_general(a, b, (((1,), (0,)), ((), ())), preferred_element_type=f32)  11 us
  transfers between devices with their start and end apart: 2, of which 0 were waited for; matrix products, arithmetic and copies ran while one was open for 15% of the time, Pallas kernels for 76%

profile of v2, /device:TPU:0, one launch (start us, length us, event | category | flops | bytes accessed | tf_op | source)
XLA Modules:
  0.0 432.0 jit_solution(11003168883620583104)
XLA Ops:
  7.2 0.7 all-gather.2.cloned.1.call-update
  8.0 0.8 copy.33
  8.7 0.8 reshape.99
  9.5 0.7 fusion.27
  10.4 1.9 concatenate.25.w_ref
  12.3 143.9 %gather_product.1 = (bf16[1536,6656]{1,0:T(8,128)(2,1)}, f32[512,6656]{1,0:T(8,128)}, bf16[512,1536]{1,0:T(8,128)(2,1)}, bf16[1536,512]{1,0:T(8,128)(2,1)}) custom-call(bf16[512,1536]{1,0:T(8,128)(2,1)} %hidden_ref.1, bf16[48,6656]{1,0:T(8,128)(2,1)} %concatenate.25.w_ref), custom_call_target="tpu_custom_call" | custom-call | tf_op jit(solution)/shard_map/gather_product/pallas_call | solution.py:703
  156.3 1.2 slice_convert_fusion
  159.4 0.7 concatenate.26.pv_ref
  160.7 0.7 maximum_maximum_fusion.2.pk_ref
  161.4 20.2 %mixer_forward.1 = (f32[512,3072]{1,0:T(8,128)}, f32[512,3072]{1,0:T(8,128)}, bf16[4,128,3072]{2,1,0:T(8,128)(2,1)}, f32[512,128]{1,0:T(8,128)}, f32[512,128]{1,...) custom-call(f32[512,6656]{1,0:T(8,128)} %get-tuple-element.32.gate_r, ...), custom_call_target="tpu_custom_call" | custom-call | tf_op jit(solution)/shard_map/mixer_forward/pallas_call | solution.py:355
  181.7 11.9 %multiply_reduce_fusion = (f32[512]{0:T(512)S(1)}, f32[512,3072]{1,0:T(8,128)}) fusion(f32[512,3072]{1,0:T(8,128)} %get-tuple-element.34, f32[3072]{0:T(1024)S(1)} %mul.119, bf16[3072,1536]{1,0:T(8,128)(2,1)} %all-gather.2.cloned.1.call-done, bf16[512,1536]{1,0:T(8,128)(2,1)S(1)} %copy-done.1, f32[512]{0:T(512)S(1)} %fusion.28), kind=kOutput, calls=%fused_computation.1 | convolution fusion | flops 4838915584 | bytes 23609344 | tf_op jit(solution)/shard_map/dot_general | solution.py:31
  193.9 11.0 %convolution_convert_fusion = bf16[3072,1536]{1,0:T(8,128)(2,1)} fusion(bf16[512,1536]{1,0:T(8,128)(2,1)S(1)} %copy-done.1, f32[512]{0:T(512)S(1)} %fusion.28, f32[512,3072]{1,0:T(8,128)} %get-tuple-element.34, f32[3072]{0:T(1024)S(1)} %mul.119, f32[512]{0:T(512)S(1)} %get-tuple-element.55), kind=kOutput, calls=%fused_computation | convolution fusion | flops 4843634688 | bytes 17317888 | tf_op jit(solution)/shard_map/dot_general | solution.py:35
  205.2 1.4 convert_reduce_fusion
  207.0 0.8 broadcast_in_dim.54.c_ref
  207.9 46.8 %mixer_backward.1 = (bf16[512,6656]{1,0:T(8,128)(2,1)}, f32[8,3072]{1,0:T(8,128)}, f32[8,256]{1,0:T(8,128)}, f32[8,128]{1,0:T(8,128)}) custom-call(f32[512,6656]{1,0:T(8,128)} %get-tuple-element.32.gate_ref.rawv_ref.rawk_ref.dtr_ref, f32[512,6656]{1,0:T(8,128)} %get-tuple-element.32.gate_ref.rawv_ref.rawk_ref.dtr_ref, ...), custom_call_target="tpu_custom_call" | custom-call | tf_op jit(solution)/shard_map/mixer_backward/pallas_call | solution.py:390
  254.6 1.0 slice_reduce_fusion.2
  255.8 1.0 fusion.14
  256.8 0.9 fusion.13
  258.5 18.3 %fusion.6 = (f32[1536]{0:T(1024)S(1)}, f32[512]{0:T(512)S(1)}, f32[512,1536]{1,0:T(8,128)}) fusion(bf16[512,1536]{1,0:T(8,128)(2,1)S(1)} %copy-done, f32[512]{0:T(512)S(1)} %add_rsqrt_fusion, f32[1536]{0:T(1024)S(1)} %convert_reduce_fusion, bf16[512,6656]{1,0:T(8,128)(2,1)} %get-tuple-element.45.rhs_ref, bf16[1536,6656]{1,0:T(8,128)(2,1)} %get-tuple-element.33), kind=kOutput, calls=%fused_computation.17 | convolution fusion | flops 10474485760 | bytes 31997952 | tf_op jit(solution)/shard_map/dot_general | solution.py:31
  277.3 0.7 slice.102
  278.6 1.4 maximum_maximum_fusion.extra_ref
  280.0 117.1 %scatter_product.1 = (f32[48,6656]{1,0:T(8,128)}, f32[8,128]{1,0:T(8,128)}) custom-call(bf16[1536,512]{1,0:T(8,128)(2,1)} %get-tuple-element.46.lhs_ref, bf16[512,6656]{1,0:T(8,128)(2,1)} %get-tuple-element.45.rhs_ref, f32[1536,128]{1,0:T(8,128)} %maximum_maximum_fusion.extra_ref, f32[8,128]{1,0:T(8,128)} %maximum_maximum_fusion.3.head_ref), custom_call_target="tpu_custom_call" | custom-call | tf_op jit(solution)/shard_map/scatter_product/pallas_call | solution.py:579
  397.1 2.5 slice.105
  399.6 1.3 slice.106
  400.9 0.8 slice.107
  401.7 0.7 slice.108
  402.5 0.8 slice.113
  405.2 1.4 slice_reduce_fusion.1
  406.7 1.3 slice_bitcast_fusion
  408.0 4.3 %convert_add_fusion.1 = f32[512,1536]{1,0:T(8,128)} fusion(bf16[512,1536]{1,0:T(8,128)(2,1)S(1)} %copy-done.2, bf16[512,1536]{1,0:T(8,128)(2,1)S(1)} %copy-done, f32[512,1536]{1,0:T(8,128)} %get-tuple-element.63, f32[512]{0:T(512)S(1)} %fusion.23, f32[1536]{0:T(1024)S(1)} %convert_reduce_fusion, f32[512]{0:T(512)S(1)} %add_rsqrt_fusion), kind=kLoop, calls=%fused_computation.8 | loop fusion | flops 5505024 | bytes 9447424 | tf_op jit(solution)/shard_map/add | solution.py:815
  412.3 11.0 %fusion.1 = bf16[512,1536]{1,0:T(8,128)(2,1)} fusion(bf16[512,1536]{1,0:T(8,128)(2,1)S(1)} %copy-done, bf16[3072,1536]{1,0:T(8,128)(2,1)} %all-gather.2.cloned.1.call-done, f32[512]{0:T(512)S(1)} %fusion.28, f32[512,3072]{1,0:T(8,128)} %get-tuple-element.34, f32[3072]{0:T(1024)S(1)} %mul.119, f32[512]{0:T(512)S(1)} %get-tuple-element.55), kind=kOutput, calls=%fused_computation.12 | convolution fusion | flops 4839702528 | bytes 18890752 | tf_op jit(solution)/shard_map/dot_general | solution.py:27
  423.3 1.8 convert_element_type.59
  (71 shorter events, 7.1 us)
Async XLA Ops:
  7.2 174.5 %all-gather.2.cloned.1.call-start = ((), (), s32[]{:S(2)}) async-start(), calls=%async_computation.1 | async-start | bytes 9732096 | tf_op jit(solution)/shard_map/all_gather | solution.py:737
  7.9 415.4 %reduce-scatter.2.cloned.1.call-start = ((), (), s32[]{:S(2)}) async-start(), calls=%async_computation.2 | async-start | bytes 9732096 | tf_op jit(solution)/shard_map/reduce_scatter | solution.py:741
  10.4 148.8 %copy-start.4 = (bf16[48]{0:T(256)(128)(2,1)S(1)}, bf16[48]{0:T(256)(128)(2,1)}, u32[]{:S(2)}) copy-start(bf16[48]{0:T(256)(128)(2,1)} %param.23) | copy-start | bytes 292
  10.4 149.7 %copy-start.5 = (bf16[48]{0:T(256)(128)(2,1)S(1)}, bf16[48]{0:T(256)(128)(2,1)}, u32[]{:S(2)}) copy-start(bf16[48]{0:T(256)(128)(2,1)} %param.22) | copy-start | bytes 292
  10.4 149.7 %copy-start.6 = (bf16[48]{0:T(256)(128)(2,1)S(1)}, bf16[48]{0:T(256)(128)(2,1)}, u32[]{:S(2)}) copy-start(bf16[48]{0:T(256)(128)(2,1)} %param.21) | copy-start | bytes 292
  161.4 20.3 %copy-start.1 = (bf16[512,1536]{1,0:T(8,128)(2,1)S(1)}, bf16[512,1536]{1,0:T(8,128)(2,1)}, u32[]{:S(2)}) copy-start(bf16[512,1536]{1,0:T(8,128)(2,1)} %param.14) | copy-start | bytes 4718596
  181.7 12.0 %copy-start.3 = (f32[512,128]{1,0:T(8,128)S(1)}, f32[512,128]{1,0:T(8,128)}, u32[]{:S(2)}) copy-start(f32[512,128]{1,0:T(8,128)} %get-tuple-element.35.r_ref) | copy-start | bytes 786436
  204.9 1.7 copy-start
  397.1 10.9 %copy-start.2 = (bf16[512,1536]{1,0:T(8,128)(2,1)S(1)}, bf16[512,1536]{1,0:T(8,128)(2,1)}, u32[]{:S(2)}) copy-start(bf16[512,1536]{1,0:T(8,128)(2,1)} %param.14) | copy-start | bytes 4718596
Sparse Core Ops, SparseCore 0:
  10.9 123.4 all-gather.1
  205.0 151.2 reduce-scatter.1

commit v3 on v1

v3 whole, which is shorter than its diff:
```python
from functools import partial

import jax
import jax.numpy as jnp
from jax import lax
from jax.experimental import pallas as pl
from jax.experimental.pallas import tpu as pltpu
from jax.sharding import PartitionSpec as P

f32 = jnp.float32
bf16 = jnp.bfloat16
epsilon = 1e-05
highest = lax.Precision.HIGHEST
BLK = 128
GH = 4
HD = 64
GC = GH * HD
KEY = 128
NEG = -1e30


def sigmoid(v):
    return 0.5 * jnp.tanh(0.5 * v) + 0.5


def mm(a, b):
    return lax.dot_general(a, b, (((1,), (0,)), ((), ())), preferred_element_type=f32)


def mm_nt(a, b):
    return lax.dot_general(a, b, (((1,), (1,)), ((), ())), preferred_element_type=f32)


def mm_tn(a, b):
    return lax.dot_general(a, b, (((0,), (0,)), ((), ())), preferred_element_type=f32)


def mm_hi(a, b, dims=((1,), (0,))):
    return lax.dot_general(a, b, (dims, ((), ())), preferred_element_type=f32, precision=highest)


def split(v):
    hi = v.astype(bf16)
    lo = (v - hi.astype(f32)).astype(bf16)
    return jnp.concatenate([hi, lo], axis=1)


def iota(shape, dim):
    return lax.broadcasted_iota(jnp.int32, shape, dim)


def expander(g):
    rows = iota((2 * KEY, GC), 0)
    cols = iota((2 * KEY, GC), 1)
    return jnp.where(lax.rem(rows, KEY) == cols // HD + g * GH, 1.0, 0.0).astype(bf16)


def reducer(g):
    rows = iota((GC, KEY), 0)
    cols = iota((GC, KEY), 1)
    return jnp.where(rows // HD + g * GH == cols, 1.0, 0.0).astype(bf16)


def taps_of(window, par):
    out = par[4:5] + par[3:4] * window[8:136]
    for k in range(3):
        out = out + par[k : k + 1] * window[5 + k : 133 + k]
    return out


def group_rows(st_ref, g, half, rows):
    tile = st_ref[pl.ds(pl.multiple_of(g // 2 * 8, 8), 8), rows]
    return jnp.where(half == 0, tile[:GH], tile[GH:])


def forward_shared(
    rawk_ref, dtr_ref, pv_ref, key_at, ph_ref, s_ref, st_ref, hl_ref, ehl_ref, kb_ref, kt_ref, sc_ref, padk
):
    blocks = rawk_ref.shape[0] // BLK
    dt = jax.nn.softplus(dtr_ref[...] + ph_ref[0:1, :])
    la = -dt * jnp.exp(ph_ref[1:2, :])
    tri = jnp.where(iota((BLK, BLK), 0) >= iota((BLK, BLK), 1), 1.0, 0.0).astype(f32)
    hl_ref[0] = split(dt)
    ehl_ref[...] = jnp.zeros_like(ehl_ref)
    padk[0:8] = jnp.zeros((8, 2 * KEY), f32)
    padk[8:] = rawk_ref[...]
    par = pv_ref[:, key_at : key_at + 2 * KEY]
    for k in range(blocks):
        rows = slice(k * BLK, (k + 1) * BLK)
        s = mm_hi(tri, la[rows])
        s_ref[rows] = s
        st_ref[:, rows] = s.T
        hl_ref[1, rows] = split(jnp.exp(s))
        hl_ref[2, rows] = split(jnp.exp(s[BLK - 1 :] - s))
        ehl_ref[k : k + 1] = split(jnp.exp(s[BLK - 1 :]))
        u = taps_of(padk[k * BLK : k * BLK + BLK + 8], par)
        v = u * sigmoid(u)
        kb_ref[rows] = v.astype(bf16)
        kt_ref[:, rows] = v.T.astype(bf16)
        sc_ref[k] = mm_hi(v[:, KEY:], v[:, :KEY], ((1,), (1,)))


def forward_group(
    g, gate_ref, rawv_ref, pv_ref, s_ref, st_ref, hl_ref, ehl_ref, kb_ref, kt_ref, sc_ref,
    y_ref, p_ref, hst_ref, pad, sg, hcar, ssq,
):
    blocks = gate_ref.shape[0] // BLK
    pad[8:] = rawv_ref[...]
    sg[...] = pltpu.roll(s_ref[...], lax.rem(KEY - g * GH, KEY), 1)
    ex = expander(g)
    bias = jnp.where(iota((BLK, BLK), 0) >= iota((BLK, BLK), 1), 0.0, NEG).astype(f32)
    low = iota((BLK, KEY), 1) < HD
    eend = mm(ehl_ref[...], ex)
    parg = pv_ref[:, pl.ds(pl.multiple_of(g * GC, GC), GC)]
    half = lax.rem(g, 8 // GH)
    hcar[...] = jnp.zeros_like(hcar)
    for k in range(blocks):
        rows = slice(k * BLK, (k + 1) * BLK)
        dtx = mm(hl_ref[0, rows], ex)
        exx = mm(hl_ref[1, rows], ex)
        txx = mm(hl_ref[2, rows], ex)
        hb = hcar[...].astype(bf16)
        hst_ref[k] = hb
        outer = mm(kb_ref[rows, KEY:], hb)
        across = group_rows(st_ref, g, half, rows)
        xts = []
        for q in range(GC // KEY):
            cols = slice(q * KEY, (q + 1) * KEY)
            par = parg[:, cols]
            u = taps_of(pad[k * BLK : k * BLK + BLK + 8, cols], par)
            v = u * sigmoid(u)
            x = v * dtx[:, cols]
            xts.append((x * txx[:, cols]).astype(bf16))
            xb = x.astype(bf16)
            zero = jnp.zeros_like(xb)
            x2 = jnp.concatenate([jnp.where(low, xb, zero), jnp.where(low, zero, xb)], axis=0)
            ms = []
            for side in range(2):
                j = 2 * q + side
                spread = sg[rows, j : j + 1] - across[j : j + 1]
                ms.append((jnp.exp(spread + bias) * sc_ref[k]).astype(bf16))
            y = mm(jnp.concatenate(ms, axis=1), x2)
            y = y + outer[:, cols] * exx[:, cols] + par[6:7] * v
            y_ref[rows, cols] = y
            gate = gate_ref[rows, cols]
            p = y * (gate * sigmoid(gate))
            p_ref[rows, pl.ds(pl.multiple_of(g * GC + q * KEY, KEY), KEY)] = p
            ssq[rows] += p * p
        if k + 1 < blocks:
            hcar[...] = eend[k : k + 1] * hcar[...] + mm(kt_ref[:KEY, rows], jnp.concatenate(xts, axis=1))


def fwd_kernel(
    gate_ref, rawv_ref, rawk_ref, dtr_ref, pv_ref, ph_ref,
    y_ref, p_ref, hst_ref, r_ref, s_ref, st_ref, hl_ref, ehl_ref, kb_ref, kt_ref, sc_ref,
    pad, padk, sg, hcar, ssq,
):
    g = pl.program_id(0)
    wide = p_ref.shape[1]
    shared = (s_ref, st_ref, hl_ref, ehl_ref, kb_ref, kt_ref, sc_ref)

    @pl.when(g == 0)
    def _():
        forward_shared(rawk_ref, dtr_ref, pv_ref, wide, ph_ref, *shared, padk)
        pad[0:8] = jnp.zeros((8, GC), f32)
        ssq[...] = jnp.zeros_like(ssq)

    forward_group(g, gate_ref, rawv_ref, pv_ref, *shared, y_ref, p_ref, hst_ref, pad, sg, hcar, ssq)

    @pl.when(g == pl.num_programs(0) - 1)
    def _():
        mean = jnp.sum(ssq[...], axis=1, keepdims=True) / wide
        r_ref[...] = jnp.broadcast_to(lax.rsqrt(mean + epsilon), r_ref.shape)


def backward_start(length, pad, dpad, dsc, dkb, dsrow, dscol, ddt):
    pad[0:8] = jnp.zeros((8, GC), f32)
    dpad[length:] = jnp.zeros((8, GC), f32)
    for ref in (dsc, dkb, dsrow, dscol, ddt):
        ref[...] = jnp.zeros_like(ref)


def backward_group(
    g, gate_ref, rawv_ref, y_ref, gg_ref, hst_ref, r_ref, c_ref, pv_ref, shared,
    dgate_ref, draw_ref, sv_ref, pad, dpad, sg, dhcar, dsc, dkb, dsrow, dscol, ddt,
):
    s_ref, st_ref, hl_ref, ehl_ref, kb_ref, kt_ref, sc_ref = shared
    blocks = gate_ref.shape[0] // BLK
    pad[8:] = rawv_ref[...]
    sg[...] = pltpu.roll(s_ref[...], lax.rem(KEY - g * GH, KEY), 1)
    ex = expander(g)
    red = reducer(g)
    row = iota((BLK, BLK), 0)
    col = iota((BLK, BLK), 1)
    bias = jnp.where(row >= col, 0.0, NEG).astype(f32)
    strict = row > col
    low = iota((BLK, KEY), 1) < HD
    eend = mm(ehl_ref[...], ex)
    parg = pv_ref[:, pl.ds(pl.multiple_of(g * GC, GC), GC)]
    half = lax.rem(g, 8 // GH)
    tile_at = pl.ds(pl.multiple_of(g // 2 * 8, 8), 8)
    mine = (iota((8, BLK), 0) < GH) == (half == 0)
    dhcar[...] = jnp.zeros_like(dhcar)
    sv_ref[...] = jnp.zeros_like(sv_ref)
    for k in range(blocks - 1, -1, -1):
        rows = slice(k * BLK, (k + 1) * BLK)
        dtx = mm(hl_ref[0, rows], ex)
        exx = mm(hl_ref[1, rows], ex)
        txx = mm(hl_ref[2, rows], ex)
        hb = hst_ref[k]
        dhb = dhcar[...].astype(bf16)
        ch = mm(kb_ref[rows, KEY:], hb)
        qq = mm(kb_ref[rows, :KEY], dhb)
        across = group_rows(st_ref, g, half, rows)
        dyes, xts, zs, oys, ddts, ecols = [], [], [], [], [], []
        dsrow_k = jnp.zeros((BLK, KEY), f32)
        for q in range(GC // KEY):
            cols = slice(q * KEY, (q + 1) * KEY)
            par = parg[:, cols]
            window = pad[k * BLK : k * BLK + BLK + 8, cols]
            u = taps_of(window, par)
            su = sigmoid(u)
            v = u * su
            x = v * dtx[:, cols]
            xb = x.astype(bf16)
            gate = gate_ref[rows, cols]
            y = y_ref[rows, cols]
            sgt = sigmoid(gate)
            silu_g = gate * sgt
            p = y * silu_g
            dgn = gg_ref[rows, cols] * r_ref[rows]
            sv_ref[5:6, cols] += jnp.sum(dgn * p, axis=0, keepdims=True)
            dp = dgn * par[5:6] - p * c_ref[rows]
            dgate_ref[rows, cols] = (dp * y * (sgt + silu_g * (1.0 - sgt))).astype(bf16)
            dy = dp * silu_g
            sv_ref[6:7, cols] += jnp.sum(dy * v, axis=0, keepdims=True)
            dyb = dy.astype(bf16)
            dye = dy * exx[:, cols]
            dyes.append(dye.astype(bf16))
            oys.append((dye * ch[:, cols]).astype(bf16))
            xt = x * txx[:, cols]
            xts.append(xt.astype(bf16))
            zs.append((xt * qq[:, cols]).astype(bf16))
            zero = jnp.zeros_like(dyb)
            dy2 = jnp.concatenate([jnp.where(low, dyb, zero), jnp.where(low, zero, dyb)], axis=0)
            dm2 = mm_nt(dy2, xb)
            ms = []
            for side in range(2):
                j = 2 * q + side
                spread = sg[rows, j : j + 1] - across[j : j + 1]
                decay = jnp.exp(spread + bias)
                m = decay * sc_ref[k]
                ms.append(m.astype(bf16))
                dm = dm2[side * BLK : (side + 1) * BLK]
                dsc[k] += decay * dm
                e = jnp.where(strict, m * dm, 0.0)
                dsrow_k = jnp.where(col == g * GH + j, jnp.sum(e, axis=1, keepdims=True), dsrow_k)
                ecols.append(jnp.sum(e, axis=0, keepdims=True))
            dx = mm_tn(jnp.concatenate(ms, axis=0), dy2) + qq[:, cols] * txx[:, cols]
            dv = dx * dtx[:, cols] + par[6:7] * dy
            ddts.append((dx * v).astype(bf16))
            du = dv * (su + v * (1.0 - su))
            dpad[rows, cols] = du
            sv_ref[4:5, cols] += jnp.sum(du, axis=0, keepdims=True)
            for t in range(4):
                sv_ref[t : t + 1, cols] += jnp.sum(du * window[5 + t : 133 + t], axis=0, keepdims=True)
        dscol[tile_at, rows] += jnp.where(mine, jnp.concatenate(ecols + ecols, axis=0), 0.0)
        dye = jnp.concatenate(dyes, axis=1)
        xt = jnp.concatenate(xts, axis=1)
        zsum = mm(jnp.concatenate(zs, axis=1), red)
        ddt[rows] += mm(jnp.concatenate(ddts, axis=1), red)
        hterm = eend[k : k + 1] * jnp.sum(dhcar[...] * hb.astype(f32), axis=0, keepdims=True)
        end = jnp.sum(zsum, axis=0, keepdims=True) + mm_hi(hterm, red.astype(f32))
        add = dsrow_k + mm(jnp.concatenate(oys, axis=1), red) - zsum
        dsrow[rows] += add + jnp.where(row == BLK - 1, end, 0.0)
        dkb[rows, KEY:] += mm_nt(dye, hb)
        dkb[rows, :KEY] += mm_nt(xt, dhb)
        if k:
            dhcar[...] = eend[k : k + 1] * dhcar[...] + mm(kt_ref[KEY:, rows], dye)

    for k in range(blocks):
        rows = slice(k * BLK, (k + 1) * BLK)
        for q in range(GC // KEY):
            cols = slice(q * KEY, (q + 1) * KEY)
            par = parg[:, cols]
            window = dpad[k * BLK : k * BLK + BLK + 8, cols]
            out = par[3:4] * window[0:BLK]
            for t in range(3):
                out = out + par[t : t + 1] * window[3 - t : 3 - t + BLK]
            draw_ref[rows, cols] = out.astype(bf16)


def backward_shared(
    rawk_ref, dtr_ref, pv_ref, key_at, ph_ref, kb_ref, dkeys_ref, ddt_ref, sk_ref, sh_ref,
    padk, dpadk, dsc, dkb, dsrow, dscol, ddt,
):
    length = rawk_ref.shape[0]
    blocks = length // BLK
    row = iota((BLK, BLK), 0)
    col = iota((BLK, BLK), 1)
    padk[0:8] = jnp.zeros((8, 2 * KEY), f32)
    padk[8:] = rawk_ref[...]
    dpadk[length:] = jnp.zeros((8, 2 * KEY), f32)
    sk_ref[...] = jnp.zeros_like(sk_ref)
    sh_ref[...] = jnp.zeros_like(sh_ref)
    upper = jnp.where(row <= col, 1.0, 0.0).astype(f32)
    par = pv_ref[:, key_at : key_at + 2 * KEY]
    for k in range(blocks):
        rows = slice(k * BLK, (k + 1) * BLK)
        window = padk[k * BLK : k * BLK + BLK + 8]
        u = taps_of(window, par)
        su = sigmoid(u)
        ds = dsc[k].astype(bf16)
        db = dkb[rows, :KEY] + mm_tn(ds, kb_ref[rows, KEY:])
        dc = dkb[rows, KEY:] + mm(ds, kb_ref[rows, :KEY])
        du = jnp.concatenate([db, dc], axis=1) * (su + u * su * (1.0 - su))
        dpadk[rows] = du
        sk_ref[4:5] += jnp.sum(du, axis=0, keepdims=True)
        for t in range(4):
            sk_ref[t : t + 1] += jnp.sum(du * window[5 + t : 133 + t], axis=0, keepdims=True)
        dla = mm_hi(upper, dsrow[rows] - dscol[:, rows].T)
        z = dtr_ref[rows] + ph_ref[0:1, :]
        rate = jnp.exp(ph_ref[1:2, :])
        dt = jax.nn.softplus(z)
        sh_ref[1:2] += jnp.sum(dla * (-dt * rate), axis=0, keepdims=True)
        dz = (ddt[rows] - dla * rate) * sigmoid(z)
        sh_ref[0:1] += jnp.sum(dz, axis=0, keepdims=True)
        ddt_ref[rows] = dz.astype(bf16)
    for k in range(blocks):
        rows = slice(k * BLK, (k + 1) * BLK)
        window = dpadk[k * BLK : k * BLK + BLK + 8]
        out = par[3:4] * window[0:BLK]
        for t in range(3):
            out = out + par[t : t + 1] * window[3 - t : 3 - t + BLK]
        dkeys_ref[rows] = out.astype(bf16)


def bwd_kernel(
    gate_ref, rawv_ref, rawk_ref, dtr_ref, pv_ref, ph_ref,
    y_ref, gg_ref, hst_ref, r_ref, c_ref, s_ref, st_ref, hl_ref, ehl_ref, kb_ref, kt_ref, sc_ref,
    dproj_ref, sv_ref, sk_ref, sh_ref,
    pad, padk, dpad, dpadk, sg, dhcar, dsc, dkb, dsrow, dscol, ddt,
):
    g = pl.program_id(0)
    length, total = dproj_ref.shape
    wide = GC * pl.num_programs(0)
    shared = (s_ref, st_ref, hl_ref, ehl_ref, kb_ref, kt_ref, sc_ref)

    @pl.when(g == 0)
    def _():
        backward_start(length, pad, dpad, dsc, dkb, dsrow, dscol, ddt)

    gate_at = pl.ds(pl.multiple_of(g * GC, GC), GC)
    draw_at = pl.ds(pl.multiple_of(wide + g * GC, GC), GC)
    backward_group(
        g, gate_ref, rawv_ref, y_ref, gg_ref, hst_ref, r_ref, c_ref, pv_ref, shared,
        dproj_ref.at[:, gate_at], dproj_ref.at[:, draw_at], sv_ref,
        pad, dpad, sg, dhcar, dsc, dkb, dsrow, dscol, ddt,
    )

    @pl.when(g == pl.num_programs(0) - 1)
    def _():
        keys = 2 * wide
        dproj_ref[:, keys + 3 * KEY :] = jnp.zeros((length, total - keys - 3 * KEY), bf16)
        backward_shared(
            rawk_ref, dtr_ref, pv_ref, wide, ph_ref, kb_ref,
            dproj_ref.at[:, keys : keys + 2 * KEY], dproj_ref.at[:, keys + 2 * KEY : keys + 3 * KEY],
            sk_ref, sh_ref, padk, dpadk, dsc, dkb, dsrow, dscol, ddt,
        )


def whole_spec(shape):
    return pl.BlockSpec(shape, lambda g: (0,) * len(shape))


def state_specs(length):
    return (
        ((length, KEY), f32),
        ((KEY, length), f32),
        ((3, length, 2 * KEY), bf16),
        ((8, 2 * KEY), bf16),
        ((length, 2 * KEY), bf16),
        ((2 * KEY, length), bf16),
        ((length // BLK, BLK, BLK), f32),
    )


def proj_specs(length, groups):
    wide = groups * GC
    return [
        pl.BlockSpec((length, GC), lambda g: (0, g)),
        pl.BlockSpec((length, GC), lambda g: (0, groups + g)),
        pl.BlockSpec((length, 2 * KEY), lambda g: (0, 2 * wide // (2 * KEY))),
        pl.BlockSpec((length, KEY), lambda g: (0, 2 * wide // KEY + 2)),
        whole_spec((8, wide + 2 * KEY)),
        whole_spec((8, KEY)),
    ]


def mixer_forward(projected, pv, ph):
    length = projected.shape[0]
    wide = pv.shape[1] - 2 * KEY
    groups = wide // GC
    blocks = length // BLK
    column = pl.BlockSpec((length, GC), lambda g: (0, g))
    shared = state_specs(length)
    return pl.pallas_call(
        fwd_kernel,
        grid=(groups,),
        in_specs=proj_specs(length, groups),
        out_specs=[
            column,
            whole_spec((length, wide)),
            pl.BlockSpec((blocks, KEY, GC), lambda g: (0, 0, g)),
            whole_spec((length, KEY)),
        ]
        + [whole_spec(shape) for shape, _ in shared],
        out_shape=[
            jax.ShapeDtypeStruct((length, wide), f32),
            jax.ShapeDtypeStruct((length, wide), f32),
            jax.ShapeDtypeStruct((blocks, KEY, wide), bf16),
            jax.ShapeDtypeStruct((length, KEY), f32),
        ]
        + [jax.ShapeDtypeStruct(shape, dtype) for shape, dtype in shared],
        scratch_shapes=[
            pltpu.VMEM((length + 8, GC), f32),
            pltpu.VMEM((length + 8, 2 * KEY), f32),
            pltpu.VMEM((length, KEY), f32),
            pltpu.VMEM((KEY, GC), f32),
            pltpu.VMEM((length, KEY), f32),
        ],
        name="mixer_forward",
    )(projected, projected, projected, projected, pv, ph)


def backward_scratch(length):
    return [
        pltpu.VMEM((length + 8, GC), f32),
        pltpu.VMEM((length + 8, 2 * KEY), f32),
        pltpu.VMEM((length + 8, GC), f32),
        pltpu.VMEM((length + 8, 2 * KEY), f32),
        pltpu.VMEM((length, KEY), f32),
        pltpu.VMEM((KEY, GC), f32),
        pltpu.VMEM((length // BLK, BLK, BLK), f32),
        pltpu.VMEM((length, 2 * KEY), f32),
        pltpu.VMEM((length, KEY), f32),
        pltpu.VMEM((KEY, length), f32),
        pltpu.VMEM((length, KEY), f32),
    ]


def mixer_backward(projected, pv, ph, mixed, grad_gated, states, inverse, pull, shared):
    length, total = projected.shape
    wide = pv.shape[1] - 2 * KEY
    groups = wide // GC
    blocks = length // BLK
    column = pl.BlockSpec((length, GC), lambda g: (0, g))
    return pl.pallas_call(
        bwd_kernel,
        grid=(groups,),
        in_specs=proj_specs(length, groups)
        + [
            column,
            column,
            pl.BlockSpec((blocks, KEY, GC), lambda g: (0, 0, g)),
            whole_spec((length, KEY)),
            whole_spec((length, KEY)),
        ]
        + [whole_spec(shape) for shape, _ in state_specs(length)],
        out_specs=[
            whole_spec((length, total)),
            pl.BlockSpec((8, GC), lambda g: (0, g)),
            whole_spec((8, 2 * KEY)),
            whole_spec((8, KEY)),
        ],
        out_shape=[
            jax.ShapeDtypeStruct((length, total), bf16),
            jax.ShapeDtypeStruct((8, wide), f32),
            jax.ShapeDtypeStruct((8, 2 * KEY), f32),
            jax.ShapeDtypeStruct((8, KEY), f32),
        ],
        scratch_shapes=backward_scratch(length),
        name="mixer_backward",
    )(projected, projected, projected, projected, pv, ph, mixed, grad_gated, states, inverse, pull, *shared)


MESH = pl.DeviceIdType.MESH
HALF = 256


def places():
    d, f = lax.axis_index("dp"), lax.axis_index("fsdp")
    z, x, y, c = d // 2, d % 2, f // 2, f % 2
    over_core = (d, y * 2 + 1 - c)
    over_x = (z * 2 + 1 - x, f)
    over_y = (d, (1 - y) * 2 + c)
    near = ((z + 1 - 2 * (z % 2)) * 2 + x, f)
    far = (((z + 2) % 4) * 2 + x, f)
    peers = ((over_core, over_x, over_y, near, far), (over_core, over_y, over_x, near, far))
    own = ((c, x, y, z % 2, z // 2), (c, y, x, z % 2, z // 2))
    return peers, own


def greet(partners):
    barrier = pltpu.get_barrier_semaphore()
    for partner in partners:
        pl.semaphore_signal(barrier, inc=1, device_id=partner, device_id_type=MESH)
    pl.semaphore_wait(barrier, len(partners))


def block_order(half, i):
    z, x, y, c = i // 8, i // 4 % 2, i // 2 % 2, i % 2
    first, second = (x, y) if half == 0 else (y, x)
    return c, first * 8 + second * 4 + z % 2 * 2 + z // 2


def spread_lanes(tiles, width, lane, count):
    out = [jnp.zeros(tiles[0].shape, f32) for _ in range(count)]
    for i, tile in enumerate(tiles):
        at, shift = divmod(i * width, KEY)
        turned = pltpu.roll(tile, shift, 1) if shift else tile
        end = shift + width
        out[at] = out[at] + jnp.where((lane >= shift) & (lane < end), turned, 0.0)
        if end > KEY:
            out[at + 1] = out[at + 1] + jnp.where(lane < end - KEY, turned, 0.0)
    return out


def forward_kernel(
    n_in, n_out, hidden_ref, cot_ref, live_ref, w_ref, wo_ref, tile_ref, skip_ref, ph_ref,
    w_out, proj_out, mixed_out, states_out, flipped_gated_out, gg_out,
    out_ref, flipped_ref, pv_ref, gain, r_ref, c_ref, s_ref, st_ref, hl_ref, ehl_ref, kb_ref, kt_ref, sc_ref,
    held, tiles, w_stage, wo_stage, proj_stage, mixed_stage, states_stage, flip_stage, normed, gated, big,
    pad, padk, sg, hcar, ssq, dots,
    send, recv, tile_sem, out_sem,
):
    rb = w_ref.shape[0]
    length, width = hidden_ref.shape
    wide = big.shape[1]
    n = n_in + n_out
    peers, own = places()
    greet(peers[0])
    base = [sum(bit * (16 >> k) for k, bit in enumerate(own[h])) for h in range(2)]
    count = (1, 2, 4, 8, 16)

    def columns(i, half):
        group = (i - 1) * HALF + half * wide
        return pl.ds(pl.multiple_of(jnp.where(i == 0, 2 * wide + half * HALF, group), HALF), HALF)

    def copy(stage, i, half):
        start = base[half] // count[stage] * count[stage]
        block = held.at[i, half, pl.ds(start, count[stage])]
        return pltpu.make_async_remote_copy(
            src_ref=block,
            dst_ref=block,
            send_sem=send.at[i, half, stage],
            recv_sem=recv.at[i, half, stage],
            device_id=peers[half][4 - stage],
            device_id_type=MESH,
        )

    def tile_copy(stage):
        block = tiles.at[pl.ds(base[0] // count[stage] * count[stage], count[stage])]
        return pltpu.make_async_remote_copy(
            src_ref=block,
            dst_ref=block,
            send_sem=tile_sem.at[0, stage],
            recv_sem=tile_sem.at[1, stage],
            device_id=peers[0][4 - stage],
            device_id_type=MESH,
        )

    def weight_stores(i):
        slot = lax.rem(i, 2)
        copies = []
        for half in range(2):
            cols = slice(half * HALF, (half + 1) * HALF)
            copies.append(
                pltpu.make_async_copy(
                    w_stage.at[slot, :, cols], w_out.at[:, columns(i, half)], out_sem.at[half, slot]
                )
            )
            copies.append(
                pltpu.make_async_copy(
                    proj_stage.at[slot, :, cols], proj_out.at[:, columns(i, half)], out_sem.at[2 + half, slot]
                )
            )
        return copies

    def group_stores(i):
        slot = lax.rem(i, 2)
        cols = pl.ds(pl.multiple_of((i - 1) * HALF, HALF), HALF)
        return (
            pltpu.make_async_copy(mixed_stage.at[slot], mixed_out.at[:, cols], out_sem.at[4, slot]),
            pltpu.make_async_copy(states_stage.at[slot], states_out.at[:, :, cols], out_sem.at[5, slot]),
        )

    def flip_store(k):
        return pltpu.make_async_copy(
            flip_stage.at[k % 2], flipped_gated_out.at[k * HALF : (k + 1) * HALF], out_sem.at[6, k % 2]
        )

    tiles[base[0]] = tile_ref[...]
    tile_copy(0).start()

    def land(i, carry):
        for half in range(2):
            held[i, half, base[half]] = w_ref[:, columns(i, half)]
        return carry

    lax.fori_loop(0, n_in, land, 0)
    for j in range(n_out):
        for half in range(2):
            held[n_in + j, half, base[half]] = wo_ref[half * rb : (half + 1) * rb, j * HALF : (j + 1) * HALF]

    def keys_chunk(slot):
        lane = iota((8, KEY), 1)
        row = iota((8, KEY), 0)
        order = [tiles[c * 16 + at] for c, at in (block_order(0, i) for i in range(32))]
        conv = spread_lanes(order, (wide + 2 * KEY) // 32, lane, wide // KEY + 2)
        gate = spread_lanes(order, wide // 32, lane, wide // KEY)
        pre = spread_lanes(order, width // 32, lane, width // KEY)
        for k, tile in enumerate(conv):
            cols = slice(k * KEY, (k + 1) * KEY)
            if k < wide // KEY:
                tile = jnp.where(row == 5, gate[k], jnp.where(row == 6, skip_ref[:, cols], tile))
            pv_ref[:, cols] = tile
        for k, tile in enumerate(pre):
            gain[:, k * KEY : (k + 1) * KEY] = tile
        for k in range(0, length, KEY):
            values = hidden_ref[k : k + KEY].astype(f32)
            mean = jnp.mean(values * values, axis=1, keepdims=True)
            rows = (values * lax.rsqrt(mean + epsilon) * gain[6:7]).astype(bf16)
            normed[k : k + KEY] = rows
            flipped_ref[:, k : k + KEY] = rows.T
        project(slot)
        forward_shared(
            proj_stage.at[slot, :, 0:HALF], proj_stage.at[slot, :, HALF : HALF + KEY], pv_ref, wide, ph_ref,
            s_ref, st_ref, hl_ref, ehl_ref, kb_ref, kt_ref, sc_ref, padk,
        )
        pad[0:8] = jnp.zeros((8, GC), f32)
        ssq[...] = jnp.zeros_like(ssq)
        dots[...] = jnp.zeros_like(dots)

    def project(slot):
        for half in range(2):
            cols = slice(half * HALF, (half + 1) * HALF)
            proj_stage[slot, :, cols] = mm(normed[...], w_stage[slot, :, cols])

    def group_chunk(slot, g):
        project(slot)
        forward_group(
            g, proj_stage.at[slot, :, 0:HALF], proj_stage.at[slot, :, HALF : 2 * HALF], pv_ref,
            s_ref, st_ref, hl_ref, ehl_ref, kb_ref, kt_ref, sc_ref,
            mixed_stage.at[slot], big, states_stage.at[slot], pad, sg, hcar, ssq,
        )

    def finish_groups():
        mean = jnp.sum(ssq[...], axis=1, keepdims=True) / wide
        r_ref[...] = jnp.broadcast_to(lax.rsqrt(mean + epsilon), r_ref.shape)
        for k in range(wide // HALF):
            if k >= 2:
                flip_store(k - 2).wait()
            for q in range(HALF // KEY):
                cols = slice(k * HALF + q * KEY, k * HALF + (q + 1) * KEY)
                part = (big[:, cols] * r_ref[...] * pv_ref[5:6, cols]).astype(bf16)
                gated[:, cols] = part
                flip_stage[k % 2, q * KEY : (q + 1) * KEY] = part.T
            flip_store(k).start()
        for k in range(wide // HALF - 2, wide // HALF):
            flip_store(k).wait()

    def out_chunk(i):
        j = i - n_in
        for b in range(32):
            for half in range(2):
                c, at = block_order(half, b)
                wo_stage[(2 * b + half) * rb : (2 * b + half + 1) * rb] = held[i, half, c * 16 + at]
        cols = pl.ds(pl.multiple_of(j * HALF, HALF), HALF)
        branch = mm(gated[...], wo_stage[...])
        live = jnp.concatenate([live_ref[...]] * (HALF // KEY), axis=1)
        out_ref[:, cols] = (hidden_ref[:, cols].astype(f32) + live * branch).astype(bf16)
        upstream = (cot_ref[:, cols].astype(f32) * live).astype(bf16)
        dots[...] += upstream.astype(f32) * branch
        for q in range(0, wide, 512):
            more = mm_nt(upstream, wo_stage[q : q + 512])

            @pl.when(j == 0)
            def _():
                big[:, q : q + 512] = more

            @pl.when(j > 0)
            def _():
                big[:, q : q + 512] += more

    def consume(i):
        slot = lax.rem(i, 2)

        @pl.when(i < n_in)
        def _():
            @pl.when(i >= 2)
            def _():
                for store in weight_stores(i - 2):
                    store.wait()

            for half in range(2):
                for b in range(32):
                    c, at = block_order(half, b)
                    w_stage[slot, b * rb : (b + 1) * rb, half * HALF : (half + 1) * HALF] = held[i, half, c * 16 + at]

            @pl.when(i == 0)
            def _():
                keys_chunk(slot)

            @pl.when(i > 0)
            def _():
                @pl.when(i >= 3)
                def _():
                    for store in group_stores(i - 2):
                        store.wait()

                group_chunk(slot, i - 1)
                for store in group_stores(i):
                    store.start()

            for store in weight_stores(i):
                store.start()

            @pl.when(i == n_in - 1)
            def _():
                finish_groups()

        @pl.when(i >= n_in)
        def _():
            out_chunk(i)

    def tick(t, carry):
        @pl.when(t < n)
        def _():
            for half in range(2):
                copy(0, t, half).start()

        for stage in range(5):
            i = t - stage - 1

            @pl.when(i == 0)
            def _(stage=stage):
                tile_copy(stage).wait()
                if stage < 4:
                    tile_copy(stage + 1).start()

            @pl.when((i >= 0) & (i < n))
            def _(stage=stage, i=i):
                for half in range(2):
                    copy(stage, i, half).wait()
                    if stage < 4:
                        copy(stage + 1, i, half).start()
                if stage == 4:
                    consume(i)

        return carry

    lax.fori_loop(0, n + 5, tick, 0)
    whole = pltpu.make_async_copy(big, gg_out, out_sem.at[6, 0])
    whole.start()
    pull = jnp.sum(dots[...], axis=1, keepdims=True) / wide
    c_ref[...] = r_ref[...] * r_ref[...] * pull
    for i in (n_in - 2, n_in - 1):
        for store in weight_stores(i) + list(group_stores(i)):
            store.wait()
    whole.wait()


def gather_forward(hidden, cotangent, live, shard, out_shard, tile, skip_rows, ph):
    length, width = hidden.shape
    rb, columns = shard.shape
    wide = out_shard.shape[0] * 32
    n_in, n_out = columns // (2 * HALF), width // HALF
    blocks = length // BLK
    vmem = pl.BlockSpec(memory_space=pltpu.VMEM)
    anywhere = pl.BlockSpec(memory_space=pl.ANY)
    struct = jax.ShapeDtypeStruct
    shared = [struct(shape, dtype) for shape, dtype in state_specs(length)]
    return pl.pallas_call(
        partial(forward_kernel, n_in, n_out),
        out_shape=[
            struct((width, columns), bf16),
            struct((length, columns), f32),
            struct((length, wide), f32),
            struct((blocks, KEY, wide), bf16),
            struct((wide, length), bf16),
            struct((length, wide), f32),
            struct((length, width), bf16),
            struct((width, length), bf16),
            struct((8, wide + 2 * KEY), f32),
            struct((8, width), f32),
            struct((length, KEY), f32),
            struct((length, KEY), f32),
        ]
        + shared,
        in_specs=[vmem] * 8,
        out_specs=[anywhere] * 6 + [vmem] * (6 + len(shared)),
        scratch_shapes=[
            pltpu.VMEM((n_in + n_out, 2, 32, rb, HALF), bf16),
            pltpu.VMEM((32, 8, KEY), f32),
            pltpu.VMEM((2, width, 2 * HALF), bf16),
            pltpu.VMEM((wide, HALF), bf16),
            pltpu.VMEM((2, length, 2 * HALF), f32),
            pltpu.VMEM((2, length, HALF), f32),
            pltpu.VMEM((2, blocks, KEY, HALF), bf16),
            pltpu.VMEM((2, HALF, length), bf16),
            pltpu.VMEM((length, width), bf16),
            pltpu.VMEM((length, wide), bf16),
            pltpu.VMEM((length, wide), f32),
            pltpu.VMEM((length + 8, GC), f32),
            pltpu.VMEM((length + 8, 2 * KEY), f32),
            pltpu.VMEM((length, KEY), f32),
            pltpu.VMEM((KEY, GC), f32),
            pltpu.VMEM((length, KEY), f32),
            pltpu.VMEM((length, HALF), f32),
            pltpu.SemaphoreType.DMA((n_in + n_out, 2, 5)),
            pltpu.SemaphoreType.DMA((n_in + n_out, 2, 5)),
            pltpu.SemaphoreType.DMA((2, 5)),
            pltpu.SemaphoreType.DMA((7, 2)),
        ],
        compiler_params=pltpu.CompilerParams(
            collective_id=2, has_side_effects=True, vmem_limit_bytes=63 << 20
        ),
        name="gather_forward",
    )(hidden, cotangent, live, shard, out_shard, tile, skip_rows, ph)


def scatter_kernel(
    n, rb, lhs_ref, rhs_ref, tile_ref, head_ref, out_ref, tile_out, sums_ref,
    parts, r0, r1, r2, r3, r4, tiles, t0, t1, t2, t3, t4, sums, sums_in, send, recv, tile_sem, sums_sem,
):
    peers, own = places()
    held = (r0, r1, r2, r3, r4)
    tile_held = (t0, t1, t2, t3, t4)
    greet(peers[0])

    def sums_copy(stage):
        return pltpu.make_async_remote_copy(
            src_ref=sums.at[stage],
            dst_ref=sums_in.at[stage],
            send_sem=sums_sem.at[0, stage],
            recv_sem=sums_sem.at[1, stage],
            device_id=peers[0][stage],
            device_id_type=MESH,
        )

    def tile_copy(stage):
        count = 16 >> stage
        source = (tiles,) + tile_held
        return pltpu.make_async_remote_copy(
            src_ref=source[stage].at[pl.ds((1 - own[0][stage]) * count, count)],
            dst_ref=tile_held[stage],
            send_sem=tile_sem.at[0, stage],
            recv_sem=tile_sem.at[1, stage],
            device_id=peers[0][stage],
            device_id_type=MESH,
        )

    sums[0] = head_ref[...]
    sums_copy(0).start()
    for i in range(32):
        c, at = block_order(0, i)
        tiles[c * 16 + at] = tile_ref[i]
    tile_copy(0).start()

    def copy(stage, i, half):
        count = 16 >> stage
        if stage == 0:
            src = parts.at[lax.rem(i, 2), 1 - own[half][0], half]
        else:
            src = held[stage - 1].at[i, half, pl.ds((1 - own[half][stage]) * count, count)]
        return pltpu.make_async_remote_copy(
            src_ref=src,
            dst_ref=held[stage].at[i, half],
            send_sem=send.at[i, half, stage],
            recv_sem=recv.at[i, half, stage],
            device_id=peers[half][stage],
            device_id_type=MESH,
        )

    def tick(t, carry):
        @pl.when(t < n)
        def _():
            slot = lax.rem(t, 2)

            @pl.when(t >= 2)
            def _():
                for half in range(2):
                    copy(0, t - 2, half).wait_send()

            for half in range(2):
                cols = pl.ds(pl.multiple_of(t * 2 * HALF + half * HALF, HALF), HALF)
                right = rhs_ref[:, cols]
                for z in range(4):
                    res = mm(lhs_ref[z * 8 * rb : (z + 1) * 8 * rb], right)
                    for b in range(8):
                        c, at = block_order(half, z * 8 + b)
                        parts[slot, c, half, at] = res[b * rb : (b + 1) * rb].astype(bf16)
            for half in range(2):
                copy(0, t, half).start()

        for stage in range(5):
            i = t - stage - 1

            @pl.when(i == 0)
            def _(stage=stage):
                count = 16 >> stage
                sums_copy(stage).wait()
                tile_copy(stage).wait()
                total = tile_held[stage][...] + ((tiles,) + tile_held)[stage][pl.ds(own[0][stage] * count, count)]
                if stage < 4:
                    sums[stage + 1] = sums[stage] + sums_in[stage]
                    sums_copy(stage + 1).start()
                    tile_held[stage][...] = total
                    tile_copy(stage + 1).start()
                else:
                    sums_ref[...] = sums[stage] + sums_in[stage]
                    tile_out[...] = total[0]

            @pl.when((i >= 0) & (i < n))
            def _(stage=stage, i=i):
                count = 16 >> stage
                for half in range(2):
                    done = copy(stage, i, half)
                    if stage == 0:
                        done.wait_recv()
                        mine = parts[lax.rem(i, 2), own[half][0], half]
                    else:
                        done.wait()
                        mine = held[stage - 1][i, half, pl.ds(own[half][stage] * count, count)]
                    if stage < 4:
                        held[stage][i, half] = (
                            held[stage][i, half].astype(f32) + mine.astype(f32)
                        ).astype(bf16)
                        copy(stage + 1, i, half).start()
                    else:
                        cols = pl.ds(pl.multiple_of(i * 2 * HALF + half * HALF, HALF), HALF)
                        out_ref[:, cols] = held[stage][i, half, 0].astype(f32) + mine[0].astype(f32)

        return carry

    lax.fori_loop(0, n + 5, tick, 0)
    for i in (n - 2, n - 1):
        for half in range(2):
            copy(0, i, half).wait_send()


def scatter_product(lhs, rhs, tiles, heads):
    rows, depth = lhs.shape
    columns = rhs.shape[1]
    n, rb = columns // (2 * HALF), rows // 32
    vmem = pl.BlockSpec(memory_space=pltpu.VMEM)
    return pl.pallas_call(
        partial(scatter_kernel, n, rb),
        out_shape=(
            jax.ShapeDtypeStruct((rb, columns), f32),
            jax.ShapeDtypeStruct(tiles.shape[1:], f32),
            jax.ShapeDtypeStruct(heads.shape, f32),
        ),
        in_specs=[vmem] * 4,
        out_specs=(vmem, vmem, vmem),
        scratch_shapes=[pltpu.VMEM((2, 2, 2, 16, rb, HALF), bf16)]
        + [pltpu.VMEM((n, 2, 16 >> stage, rb, HALF), bf16) for stage in range(5)]
        + [pltpu.VMEM(((32 >> stage),) + tiles.shape[1:], f32) for stage in range(6)]
        + [pltpu.VMEM((5,) + heads.shape, f32)] * 2
        + [pltpu.SemaphoreType.DMA((n, 2, 5))] * 2
        + [pltpu.SemaphoreType.DMA((2, 5))] * 2,
        compiler_params=pltpu.CompilerParams(
            collective_id=1, has_side_effects=True, vmem_limit_bytes=60 << 20
        ),
        name="scatter_product",
    )(lhs, rhs, tiles, heads)


def pre_norm_inverse(rows):
    return lax.rsqrt(jnp.mean(rows * rows, axis=1, keepdims=True) + epsilon)


AXES = ("dp", "fsdp")


def gather_rows(shard):
    return lax.all_gather(shard, AXES, axis=0, tiled=True)


def scatter_rows(whole):
    return lax.psum_scatter(whole, AXES, scatter_dimension=0, tiled=True)


def vector_tile(conv_weight, conv_bias, gate_gain, norm_gain):
    rows = [conv_weight, conv_bias[None], gate_gain[None], norm_gain[None]]
    rows = [jnp.pad(row.astype(f32), ((0, 0), (0, KEY - row.shape[1]))) for row in rows]
    return jnp.concatenate(rows + [jnp.zeros((1, KEY), f32)], axis=0)


def vector_tiles(conv, gate, pre, parts):
    rows = []
    for whole in (conv, gate, pre):
        part = whole.shape[1] // parts
        split_up = jnp.transpose(whole.reshape(-1, parts, part), (1, 0, 2))
        rows.append(jnp.pad(split_up, ((0, 0), (0, 0), (0, KEY - part))))
    return jnp.concatenate(rows + [jnp.zeros((parts, 1, KEY), f32)], axis=1)


def shards(
    kernels, hidden, cotangent, lengths, norm_gain, in_proj, dt_proj, conv_weight, conv_bias,
    dt_bias, a_log, skip_gain, gate_gain, out_proj,
):
    length, width = hidden.shape
    assert lengths.shape[0] == 1
    rows_in, columns = in_proj.shape
    heads = dt_bias.shape[0]
    parts = width // rows_in
    taps, conv_part = conv_weight.shape
    gate_part = gate_gain.shape[0]
    wide = gate_part * parts
    total = columns + 2 * KEY

    fill = jnp.zeros((rows_in, total - columns - heads), bf16)
    packed = jnp.concatenate([in_proj, dt_proj, fill], axis=1)
    tile = vector_tile(conv_weight, conv_bias, gate_gain, norm_gain)
    ph = jnp.pad(jnp.stack([dt_bias, a_log]).astype(f32), ((0, 6), (0, KEY - heads)))
    skip_wide = jnp.repeat(skip_gain.astype(f32), HD)[None]
    live = (jnp.arange(length) < lengths[0]).astype(f32)[:, None]
    rows_wide = hidden.astype(f32)
    cot_wide = cotangent.astype(f32)
    upstream = (cot_wide * live).astype(bf16)
    inverse_one = pre_norm_inverse(rows_wide)
    if kernels:
        skip_rows = jnp.broadcast_to(skip_wide, (8, wide))
        (
            w_in, projected, mixed, states, gated_flipped, grad_gated, output, flipped, pv, gains, inverse_two, pull,
            *shared,
        ) = gather_forward(
            hidden, cotangent, jnp.broadcast_to(live, (length, KEY)), packed, out_proj, tile, skip_rows, ph
        )
        gain_one = gains[6]
        grad_out = mm(gated_flipped, upstream)
    else:
        w_in, w_out = gather_rows(packed), gather_rows(out_proj)
        tiles = gather_rows(tile[None])
        whole = lambda rows, part: jnp.transpose(tiles[:, rows, :part], (1, 0, 2)).reshape(-1, parts * part)
        conv_all = whole(slice(0, 5), conv_part)
        gain_two = whole(slice(5, 6), gate_part)
        gain_one = whole(slice(6, 7), rows_in)[0]
        rest = jnp.concatenate([gain_two, skip_wide, jnp.zeros((1, wide), f32)], axis=0)
        pv = jnp.concatenate([conv_all, jnp.pad(rest, ((0, 0), (0, 2 * KEY)))], axis=0)
        normed = (rows_wide * inverse_one * gain_one[None, :]).astype(bf16)
        projected = mm(normed, w_in)
        mixed, product, states, inverse_two, *shared = mixer_forward(projected, pv, ph)
        inv = inverse_two[:, :1]
        gated = (product * inv * gain_two).astype(bf16)
        output = (rows_wide + live * mm(gated, w_out)).astype(bf16)
        grad_gated = mm_nt(upstream, w_out)
        pull = jnp.sum(grad_gated * gain_two * product, axis=1, keepdims=True)
        pull = jnp.broadcast_to(inv * inv * inv * pull / wide, inverse_two.shape)
        grad_out = mm_tn(gated, upstream)
    grad_proj, sums_v, sums_k, sums_h = mixer_backward(
        projected, pv, ph, mixed, grad_gated, states, inverse_two, pull, shared
    )
    skip_grad = jnp.pad(jnp.sum(sums_v[6].reshape(heads, HD), axis=1), (0, KEY - heads))[None]
    head_grads = jnp.concatenate([sums_h[:2], skip_grad, jnp.zeros((5, KEY), f32)], axis=0)

    grad_normed = mm_nt(grad_proj, w_in)
    scaled = grad_normed * gain_one[None, :]
    row_sums = jnp.sum(scaled * rows_wide, axis=1, keepdims=True) / width
    grad_rows = inverse_one * scaled - rows_wide * (inverse_one * inverse_one * inverse_one * row_sums)
    input_grad = cot_wide + grad_rows
    grad_gain_one = jnp.sum(grad_normed * rows_wide * inverse_one, axis=0, keepdims=True)

    conv_grad = jnp.concatenate([sums_v[:5], sums_k[:5]], axis=1)
    small = vector_tiles(conv_grad, sums_v[5:6], grad_gain_one, parts)
    grad_out = scatter_rows(grad_out.astype(bf16)).astype(f32)
    if kernels:
        grad_in, small_sum, head_sums = scatter_product(flipped, grad_proj, small, head_grads)
    else:
        head_sums = lax.psum(head_grads, AXES)
        grad_in = scatter_rows(mm_tn(normed, grad_proj).astype(bf16)).astype(f32)
        small_sum = scatter_rows(small)[0]
    return (
        output,
        input_grad,
        small_sum[6, :rows_in],
        grad_in[:, :columns],
        grad_in[:, columns : columns + heads],
        small_sum[:taps, :conv_part],
        small_sum[taps, :conv_part],
        head_sums[0, :heads],
        head_sums[1, :heads],
        head_sums[2, :heads],
        small_sum[5, :gate_part],
        grad_out,
    )


def solution(mesh):
    rows = P(AXES, None)
    vector = P(AXES)
    last = P(None, AXES)
    return jax.shard_map(
        partial(shards, mesh.shape["dp"] == 8 and mesh.shape["fsdp"] == 4),
        mesh=mesh,
        in_specs=(rows, rows, vector, vector, rows, rows, last, vector, P(), P(), P(), vector, rows),
        out_specs=(rows, rows, vector, rows, rows, last, vector, P(), P(), P(), vector, rows),
        check_vma=False,
    )
```

time: 622 us -> 406 us (0.65)
  waiting for transfers between devices: 375 us -> 0.02 us
  Pallas kernels: 65.4 us -> 332 us
  matrix products: 88.4 us -> 29.3 us
  blocking collectives: 40.1 us -> 0 us
  local copies, waits for them, and re-layouts: 24.8 us -> 18.1 us
    pallas_call x1 -> x2, Pallas kernels: 19.9 us -> 285 us  [the longest x1 163 us: gather_forward(): pl.pallas_call(partial(forward_kernel, n_in, n_out), out_shape=[struct((w...]
    reduce_scatter x2 -> x1, waiting for transfers between devices: 205 us -> 0.01 us  [scatter_rows(): return lax.psum_scatter(whole, AXES, scatter_dimension=0, tiled=True)]
    all_gather x2 -> x0, waiting for transfers between devices: 170 us -> none  [gather_rows(): return lax.all_gather(shard, AXES, axis=0, tiled=True)]
    psum x1 -> x0, blocking collectives: 40.1 us -> none  [shards(): lax.psum(jnp.concatenate([sums_h[:2, :heads], jnp.sum(sums_v[6].reshape(h...]
    dot_general x2 -> x0, matrix products: 28.2 us -> none  [mm_tn(): lax.dot_general(a, b, (((0,), (0,)), ((), ())), preferred_element_type=f32)]
    dot_general x2 -> x1, matrix products: 28.7 us -> 10.2 us  [mm(): lax.dot_general(a, b, (((1,), (0,)), ((), ())), preferred_element_type=f32)]
    dot_general x2 -> x1, matrix products: 31.5 us -> 19.1 us  [mm_nt(): lax.dot_general(a, b, (((1,), (1,)), ((), ())), preferred_element_type=f32)]
  transfers between devices with their start and end apart: 4 -> 1, of which waited for: 3 -> 0; matrix products, arithmetic and copies ran while one was open for 14% -> 9% of each run, Pallas kernels for 11% -> 42%
where the time goes in v3:
time: 406 us
  Pallas kernels  332 us (82%)
  matrix products  29.3 us (7%)
  local copies, waits for them, and re-layouts  18.1 us (4%)
  between operations  14.8 us (4%)
  other arithmetic  11.5 us (3%)
    pallas_call x1, Pallas kernels, gather_forward(): pl.pallas_call(partial(forward_kernel, n_in, n_out), out_shape=[struct((w...  163 us
    pallas_call x1, Pallas kernels, scatter_product(): pl.pallas_call(partial(scatter_kernel, n, rb), out_shape=(jax.ShapeDtypeS...  122 us
    pallas_call x1, Pallas kernels, mixer_backward(): pl.pallas_call(bwd_kernel, grid=(groups,), in_specs=proj_specs(length, gr...  46.6 us
    dot_general x1, matrix products, mm_nt(): lax.dot_general(a, b, (((1,), (1,)), ((), ())), preferred_element_type=f32)  19.1 us
    dot_general x1, matrix products, mm(): lax.dot_general(a, b, (((1,), (0,)), ((), ())), preferred_element_type=f32)  10.2 us
  transfers between devices with their start and end apart: 1, of which 0 were waited for; matrix products, arithmetic and copies ran while one was open for 9% of the time, Pallas kernels for 42%

profile of v3, /device:TPU:0, one launch (start us, length us, event | category | flops | bytes accessed | tf_op | source)
XLA Modules:
  0.0 405.8 jit_solution(7426091396193159020)
XLA Ops:
  7.9 0.7 pad_convert_fusion
  8.6 0.7 pad_convert_fusion.3
  9.2 0.7 broadcast_in_dim.39
  10.0 0.7 pad_convert_fusion.1
  10.7 1.3 fusion.18.ph_ref
  12.0 1.9 concatenate.15.w_ref
  13.9 0.6 concatenate.16.tile_ref
  14.5 0.8 broadcast_in_dim.36.live_ref
  15.3 0.6 broadcast_in_dim.41.skip_ref
  16.0 163.0 %gather_forward.1 = (bf16[1536,6656]{1,0:T(8,128)(2,1)}, f32[512,6656]{1,0:T(8,128)}, f32[512,3072]{1,0:T(8,128)}, bf16[4,128,3072]{2,1,0:T(8,128)(2,1)}, bf16[3...) custom-call(bf16[512,1536]{1,0:T(8,128)(2,1)} %hidden_ref.1, ...), custom_call_target="tpu_custom_call" | custom-call | tf_op jit(solution)/shard_map/gather_forward/pallas_call | solution.py:784
  179.0 10.2 %convolution_convert_fusion = bf16[3072,1536]{1,0:T(8,128)(2,1)} fusion(bf16[3072,512]{1,0:T(8,128)(2,1)} %get-tuple-element.63, bf16[512,1536]{1,0:T(8,128)(2,1)} %cot_ref.1, f32[512]{0:T(512)S(1)} %fusion.19), kind=kOutput, calls=%fused_computation | convolution fusion | flops 4838916096 | bytes 14157824 | tf_op jit(solution)/shard_map/dot_general | solution.py:27
  189.2 46.6 %mixer_backward.1 = (bf16[512,6656]{1,0:T(8,128)(2,1)}, f32[8,3072]{1,0:T(8,128)}, f32[8,256]{1,0:T(8,128)}, f32[8,128]{1,0:T(8,128)}) custom-call(f32[512,6656]{1,0:T(8,128)} %get-tuple-element.39.gate_ref.rawv_ref.rawk_ref.dtr_ref, f32[512,6656]{1,0:T(8,128)} %get-tuple-element.39.gate_ref.rawv_ref.rawk_ref.dtr_ref, ...), custom_call_target="tpu_custom_call" | custom-call | tf_op jit(solution)/shard_map/mixer_backward/pallas_call | solution.py:458
  235.8 0.8 slice_reduce_fusion.2
  236.7 0.4 fusion.1
  237.1 19.1 %fusion.5 = (f32[1536]{0:T(1024)S(1)}, f32[512]{0:T(512)S(1)}, f32[512,1536]{1,0:T(8,128)}) fusion(bf16[512,1536]{1,0:T(8,128)(2,1)S(1)} %copy-done, f32[512]{0:T(512)S(1)} %add_rsqrt_fusion, f32[1536]{0:T(1024)S(1)} %slice_reduce_fusion.2, bf16[512,6656]{1,0:T(8,128)(2,1)} %get-tuple-element.53.rhs_ref, bf16[1536,6656]{1,0:T(8,128)(2,1)} %get-tuple-element.54), kind=kOutput, calls=%fused_computation.12 | convolution fusion | flops 10474485760 | bytes 31997952 | tf_op jit(solution)/shard_map/dot_general | solution.py:31
  256.3 0.1 transpose_reshape.3
  256.5 0.1 reshape.59
  256.7 0.1 reduce_sum.39
  256.8 0.7 slice.49
  257.7 0.7 maximum_maximum_fusion.head_ref
  258.4 0.7 fusion.8.tile_ref
  259.1 122.3 %scatter_product.1 = (f32[48,6656]{1,0:T(8,128)}, f32[8,128]{1,0:T(8,128)}, f32[8,128]{1,0:T(8,128)}) custom-call(bf16[1536,512]{1,0:T(8,128)(2,1)} %get-tuple-element.56.lhs_ref, bf16[512,6656]{1,0:T(8,128)(2,1)} %get-tuple-element.53.rhs_ref, f32[32,8,128]{2,1,0:T(8,128)} %fusion.8.tile_ref, f32[8,128]{1,0:T(8,128)} %maximum_maximum_fusion.head_ref), custom_call_target="tpu_custom_call" | custom-call | tf_op jit(solution)/shard_map/scatter_product/pallas_call | solution.py:958
  381.4 2.5 slice.52
  383.9 1.3 slice.53
  385.3 1.3 slice.54
  386.5 1.2 slice_bitcast_fusion.5
  387.7 1.2 slice_bitcast_fusion.4
  388.9 1.2 slice_bitcast_fusion
  390.1 1.3 slice_bitcast_fusion.1
  391.4 4.5 %convert_add_fusion = f32[512,1536]{1,0:T(8,128)} fusion(bf16[512,1536]{1,0:T(8,128)(2,1)S(1)} %copy-done.1, bf16[512,1536]{1,0:T(8,128)(2,1)S(1)} %copy-done, f32[512,1536]{1,0:T(8,128)} %get-tuple-element.71, f32[512]{0:T(512)S(1)} %fusion.16, f32[1536]{0:T(1024)S(1)} %slice_reduce_fusion.2, f32[512]{0:T(512)S(1)} %add_rsqrt_fusion), kind=kLoop, calls=%fused_computation.6 | loop fusion | flops 5505024 | bytes 9447424 | tf_op jit(solution)/shard_map/add | solution.py:1073
  395.9 1.8 convert_element_type.66
  397.8 1.1 copy.30
  (28 shorter events, 0.6 us)
Async XLA Ops:
  7.2 388.8 %reduce-scatter.2.cloned.1.call-start = ((), (), s32[]{:S(2)}) async-start(), calls=%async_computation.1 | async-start | bytes 9732096 | tf_op jit(solution)/shard_map/reduce_scatter | solution.py:992
  189.2 47.4 %copy-start = (bf16[512,1536]{1,0:T(8,128)(2,1)S(1)}, bf16[512,1536]{1,0:T(8,128)(2,1)}, u32[]{:S(2)}) copy-start(bf16[512,1536]{1,0:T(8,128)(2,1)} %hidden_ref.1) | copy-start | bytes 4718596
  237.1 19.2 %copy-start.3 = (f32[8,3072]{1,0:T(8,128)S(1)}, f32[8,3072]{1,0:T(8,128)}, u32[]{:S(2)}) copy-start(f32[8,3072]{1,0:T(8,128)} %get-tuple-element.57) | copy-start | bytes 294916
  237.1 19.4 %copy-start.4 = (f32[8,256]{1,0:T(8,128)S(1)}, f32[8,256]{1,0:T(8,128)}, u32[]{:S(2)}) copy-start(f32[8,256]{1,0:T(8,128)} %get-tuple-element.58) | copy-start | bytes 24580
  381.4 10.0 %copy-start.1 = (bf16[512,1536]{1,0:T(8,128)(2,1)S(1)}, bf16[512,1536]{1,0:T(8,128)(2,1)}, u32[]{:S(2)}) copy-start(bf16[512,1536]{1,0:T(8,128)(2,1)} %cot_ref.1) | copy-start | bytes 4718596
  391.4 6.3 %copy-start.2 = (bf16[512,1536]{1,0:T(8,128)(2,1)S(1)}, bf16[512,1536]{1,0:T(8,128)(2,1)}, u32[]{:S(2)}) copy-start(bf16[512,1536]{1,0:T(8,128)(2,1)} %get-tuple-element.86) | copy-start | bytes 4718596
Sparse Core Ops, SparseCore 0:
  189.3 158.1 reduce-scatter.1

commit v4 on v3

--- a/solution.py
+++ b/solution.py
@@ -830,14 +830,80 @@
     )(hidden, cotangent, live, shard, out_shard, tile, skip_rows, ph)
 
 
-def scatter_kernel(
-    n, rb, lhs_ref, rhs_ref, tile_ref, head_ref, out_ref, tile_out, sums_ref,
-    parts, r0, r1, r2, r3, r4, tiles, t0, t1, t2, t3, t4, sums, sums_in, send, recv, tile_sem, sums_sem,
+EARLY = 6
+
+
+def gather_lanes(row_tiles, width, lane, i):
+    at, shift = divmod(i * width, KEY)
+    if shift == 0:
+        return row_tiles[at]
+    first = pltpu.roll(row_tiles[at], KEY - shift, 1)
+    if shift + width <= KEY:
+        return first
+    return jnp.where(lane < KEY - shift, first, pltpu.roll(row_tiles[at + 1], KEY - shift, 1))
+
+
+def backward_kernel(
+    n_in, n_out, hidden_ref, cot_ref, live_ref, flipped_ref, gated_ref, pv_ref, gain_ref, ph_ref, r_ref, c_ref,
+    s_ref, st_ref, hl_ref, ehl_ref, kb_ref, kt_ref, sc_ref,
+    proj_in, mixed_in, gg_in, states_in, w_in,
+    rows_out, in_ref, dt_ref, out_ref, tile_out, sums_ref,
+    parts, r0, r1, r2, r3, r4, tiles, t0, t1, t2, t3, t4, sums, sums_in,
+    stage_in, states_stage, w_stage, keys_stage, dchunk, rows_grad, sv, sv_all, sk, sh, skip_sum, gain_sum,
+    pad, padk, dpad, dpadk, sg, dhcar, dsc, dkb, dsrow, dscol, ddt,
+    send, recv, tile_sem, sums_sem, in_sem, out_sem,
 ):
+    length, width = hidden_ref.shape
+    wide = mixed_in.shape[1]
+    rb = in_ref.shape[0]
+    n = n_in + n_out
+    groups = n_in - 1
+    keys_tick = n - 2
+    shared = (s_ref, st_ref, hl_ref, ehl_ref, kb_ref, kt_ref, sc_ref)
     peers, own = places()
     held = (r0, r1, r2, r3, r4)
-    tile_held = (t0, t1, t2, t3, t4)
+    tile_source = (tiles, t0, t1, t2, t3, t4)
     greet(peers[0])
+
+    def is_out(t):
+        return ((t < 3 * n_out - 3) & (lax.rem(t, 3) == 0)) | (t == n - 1)
+
+    def out_index(t):
+        return jnp.where(t == n - 1, n_out - 1, t // 3)
+
+    def group_index(t):
+        return jnp.where(t < 3 * n_out - 3, t // 3 * 2 + lax.rem(t, 3) - 1, t - n_out + 1)
+
+    def loads(g):
+        slot = lax.rem(g, 2)
+        near = pl.ds(pl.multiple_of(g * HALF, HALF), HALF)
+        far = pl.ds(pl.multiple_of(wide + g * HALF, HALF), HALF)
+        pairs = (
+            (proj_in.at[:, near], stage_in.at[slot, 0]),
+            (proj_in.at[:, far], stage_in.at[slot, 1]),
+            (mixed_in.at[:, near], stage_in.at[slot, 2]),
+            (gg_in.at[:, near], stage_in.at[slot, 3]),
+            (states_in.at[:, :, near], states_stage.at[slot]),
+        )
+        return [pltpu.make_async_copy(a, b, in_sem.at[k, slot]) for k, (a, b) in enumerate(pairs)]
+
+    def weight_loads(g):
+        slot = lax.rem(g, 2)
+        first = jnp.where(g == groups, 2 * wide, g * HALF)
+        second = jnp.where(g == groups, 2 * wide + HALF, wide + g * HALF)
+        return [
+            pltpu.make_async_copy(
+                w_in.at[:, pl.ds(pl.multiple_of(at, HALF), HALF)],
+                w_stage.at[slot, :, half * HALF : (half + 1) * HALF],
+                in_sem.at[5 + half, slot],
+            )
+            for half, at in enumerate((first, second))
+        ]
+
+    keys_load = pltpu.make_async_copy(proj_in.at[:, 2 * wide : 2 * wide + 3 * KEY], keys_stage, in_sem.at[7, 0])
+    for load in loads(0) + weight_loads(0) + [keys_load]:
+        load.start()
+    rows_store = pltpu.make_async_copy(rows_grad, rows_out, out_sem.at[0])
 
     def sums_copy(stage):
         return pltpu.make_async_remote_copy(
@@ -851,38 +917,140 @@
 
     def tile_copy(stage):
         count = 16 >> stage
-        source = (tiles,) + tile_held
         return pltpu.make_async_remote_copy(
-            src_ref=source[stage].at[pl.ds((1 - own[0][stage]) * count, count)],
-            dst_ref=tile_held[stage],
+            src_ref=tile_source[stage].at[pl.ds((1 - own[0][stage]) * count, count)],
+            dst_ref=tile_source[stage + 1],
             send_sem=tile_sem.at[0, stage],
             recv_sem=tile_sem.at[1, stage],
             device_id=peers[0][stage],
             device_id_type=MESH,
         )
 
-    sums[0] = head_ref[...]
-    sums_copy(0).start()
-    for i in range(32):
-        c, at = block_order(0, i)
-        tiles[c * 16 + at] = tile_ref[i]
-    tile_copy(0).start()
+    def place(stage, i):
+        return lax.rem(i, EARLY) if stage == 0 else i
 
     def copy(stage, i, half):
         count = 16 >> stage
         if stage == 0:
             src = parts.at[lax.rem(i, 2), 1 - own[half][0], half]
         else:
-            src = held[stage - 1].at[i, half, pl.ds((1 - own[half][stage]) * count, count)]
+            src = held[stage - 1].at[place(stage - 1, i), half, pl.ds((1 - own[half][stage]) * count, count)]
         return pltpu.make_async_remote_copy(
             src_ref=src,
-            dst_ref=held[stage].at[i, half],
+            dst_ref=held[stage].at[place(stage, i), half],
             send_sem=send.at[i, half, stage],
             recv_sem=recv.at[i, half, stage],
             device_id=peers[half][stage],
             device_id_type=MESH,
         )
 
+    backward_start(length, pad, dpad, dsc, dkb, dsrow, dscol, ddt)
+    skip_sum[...] = jnp.zeros_like(skip_sum)
+    rows_grad[...] = jnp.zeros_like(rows_grad)
+
+    def out_chunk(slot, j):
+        cols = pl.ds(pl.multiple_of(j * HALF, HALF), HALF)
+        live = jnp.concatenate([live_ref[...]] * (HALF // KEY), axis=1)
+        upstream = (cot_ref[:, cols].astype(f32) * live).astype(bf16)
+        for z in range(4):
+            res = mm(gated_ref[z * 16 * rb : (z + 1) * 16 * rb], upstream)
+            for b in range(8):
+                for half in range(2):
+                    c, at = block_order(half, z * 8 + b)
+                    at_row = (2 * b + half) * rb
+                    parts[slot, c, half, at] = res[at_row : at_row + rb].astype(bf16)
+
+    def weight_chunk(slot, g):
+        for load in weight_loads(g):
+            load.wait()
+        at = lax.rem(g, 2)
+        for half in range(2):
+            right = dchunk[:, half * HALF : (half + 1) * HALF]
+            for z in range(4):
+                res = mm(flipped_ref[z * 8 * rb : (z + 1) * 8 * rb], right)
+                for b in range(8):
+                    c, where = block_order(half, z * 8 + b)
+                    parts[slot, c, half, where] = res[b * rb : (b + 1) * rb].astype(bf16)
+        for k in range(0, width, 512):
+            rows_grad[:, k : k + 512] += mm_nt(dchunk[...], w_stage[at, k : k + 512])
+
+    def group_chunk(slot, g):
+        for load in weight_loads(g + 1):
+            load.start()
+
+        @pl.when(g + 1 < groups)
+        def _():
+            for load in loads(g + 1):
+                load.start()
+
+        for load in loads(g):
+            load.wait()
+        at = lax.rem(g, 2)
+        backward_group(
+            g, stage_in.at[at, 0], stage_in.at[at, 1], stage_in.at[at, 2], stage_in.at[at, 3], states_stage.at[at],
+            r_ref, c_ref, pv_ref, shared, dchunk.at[:, 0:HALF], dchunk.at[:, HALF : 2 * HALF], sv,
+            pad, dpad, sg, dhcar, dsc, dkb, dsrow, dscol, ddt,
+        )
+        sv_all[:, pl.ds(pl.multiple_of(g * HALF, HALF), HALF)] = sv[...]
+        skip_sum[...] += mm_hi(sv[...], reducer(g).astype(f32))
+        weight_chunk(slot, g)
+
+    def keys_chunk(slot):
+        keys_load.wait()
+        dchunk[:, 3 * KEY :] = jnp.zeros((length, KEY), bf16)
+        backward_shared(
+            keys_stage.at[:, 0:HALF], keys_stage.at[:, HALF : HALF + KEY], pv_ref, wide, ph_ref, kb_ref,
+            dchunk.at[:, 0:HALF], dchunk.at[:, HALF : HALF + KEY], sk, sh,
+            padk, dpadk, dsc, dkb, dsrow, dscol, ddt,
+        )
+        weight_chunk(slot, groups)
+        for half in range(2):
+            copy(0, keys_tick, half).start()
+        gain = gain_ref[6:7]
+        gain_sum[...] = jnp.zeros_like(gain_sum)
+        for k in range(0, length, KEY):
+            values = hidden_ref[k : k + KEY].astype(f32)
+            inverse = lax.rsqrt(jnp.mean(values * values, axis=1, keepdims=True) + epsilon)
+            grads = rows_grad[k : k + KEY]
+            gain_sum[0:1] += jnp.sum(grads * values * inverse, axis=0, keepdims=True)
+            scaled = grads * gain
+            pull = jnp.sum(scaled * values, axis=1, keepdims=True) / width
+            back = inverse * scaled - values * (inverse * inverse * inverse * pull)
+            rows_grad[k : k + KEY] = cot_ref[k : k + KEY].astype(f32) + back
+        rows_store.start()
+        row = iota((8, KEY), 0)
+        lane = iota((8, KEY), 1)
+        conv = [sv_all[:, k * KEY : (k + 1) * KEY] for k in range(wide // KEY)]
+        gate = conv
+        conv = conv + [sk[:, 0:KEY], sk[:, KEY : 2 * KEY]]
+        pre = [jnp.broadcast_to(gain_sum[0:1, k * KEY : (k + 1) * KEY], (8, KEY)) for k in range(width // KEY)]
+        for i in range(32):
+            c, at = block_order(0, i)
+            tile = gather_lanes(conv, (wide + 2 * KEY) // 32, lane, i)
+            tile = jnp.where(row == 5, gather_lanes(gate, wide // 32, lane, i), tile)
+            tiles[c * 16 + at] = jnp.where(row == 6, gather_lanes(pre, width // 32, lane, i), tile)
+        tile_copy(0).start()
+        sums[0] = jnp.where(row == 2, skip_sum[6:7], sh[...])
+        sums_copy(0).start()
+
+    def write_out(i, half, value):
+        @pl.when(is_out(i))
+        def _():
+            cols = pl.ds(pl.multiple_of(out_index(i) * HALF, HALF), HALF)
+            out_ref[half * rb : (half + 1) * rb, cols] = value
+
+        @pl.when(jnp.logical_not(is_out(i)) & (i != keys_tick))
+        def _():
+            cols = pl.ds(pl.multiple_of(half * wide + group_index(i) * HALF, HALF), HALF)
+            in_ref[:, cols] = value
+
+        @pl.when(i == keys_tick)
+        def _():
+            if half == 0:
+                in_ref[:, 2 * wide : 2 * wide + HALF] = value
+            else:
+                dt_ref[...] = value[:, :KEY]
+
     def tick(t, carry):
         @pl.when(t < n)
         def _():
@@ -893,38 +1061,43 @@
                 for half in range(2):
                     copy(0, t - 2, half).wait_send()
 
-            for half in range(2):
-                cols = pl.ds(pl.multiple_of(t * 2 * HALF + half * HALF, HALF), HALF)
-                right = rhs_ref[:, cols]
-                for z in range(4):
-                    res = mm(lhs_ref[z * 8 * rb : (z + 1) * 8 * rb], right)
-                    for b in range(8):
-                        c, at = block_order(half, z * 8 + b)
-                        parts[slot, c, half, at] = res[b * rb : (b + 1) * rb].astype(bf16)
-            for half in range(2):
-                copy(0, t, half).start()
+            @pl.when(is_out(t))
+            def _():
+                out_chunk(slot, out_index(t))
+
+            @pl.when(jnp.logical_not(is_out(t)) & (t != keys_tick))
+            def _():
+                group_chunk(slot, group_index(t))
+
+            @pl.when(t == keys_tick)
+            def _():
+                keys_chunk(slot)
+
+            @pl.when(t != keys_tick)
+            def _():
+                for half in range(2):
+                    copy(0, t, half).start()
 
         for stage in range(5):
             i = t - stage - 1
-
-            @pl.when(i == 0)
-            def _(stage=stage):
-                count = 16 >> stage
+            count = 16 >> stage
+
+            @pl.when(i == keys_tick)
+            def _(stage=stage, count=count):
                 sums_copy(stage).wait()
                 tile_copy(stage).wait()
-                total = tile_held[stage][...] + ((tiles,) + tile_held)[stage][pl.ds(own[0][stage] * count, count)]
+                total = tile_source[stage + 1][...] + tile_source[stage][pl.ds(own[0][stage] * count, count)]
                 if stage < 4:
                     sums[stage + 1] = sums[stage] + sums_in[stage]
                     sums_copy(stage + 1).start()
-                    tile_held[stage][...] = total
+                    tile_source[stage + 1][...] = total
                     tile_copy(stage + 1).start()
                 else:
                     sums_ref[...] = sums[stage] + sums_in[stage]
                     tile_out[...] = total[0]
 
             @pl.when((i >= 0) & (i < n))
-            def _(stage=stage, i=i):
-                count = 16 >> stage
+            def _(stage=stage, i=i, count=count):
                 for half in range(2):
                     done = copy(stage, i, half)
                     if stage == 0:
@@ -932,15 +1105,15 @@
                         mine = parts[lax.rem(i, 2), own[half][0], half]
                     else:
                         done.wait()
-                        mine = held[stage - 1][i, half, pl.ds(own[half][stage] * count, count)]
+                        mine = held[stage - 1][place(stage - 1, i), half, pl.ds(own[half][stage] * count, count)]
                     if stage < 4:
-                        held[stage][i, half] = (
-                            held[stage][i, half].astype(f32) + mine.astype(f32)
+                        at = place(stage, i)
+                        held[stage][at, half] = (
+                            held[stage][at, half].astype(f32) + mine.astype(f32)
                         ).astype(bf16)
                         copy(stage + 1, i, half).start()
                     else:
-                        cols = pl.ds(pl.multiple_of(i * 2 * HALF + half * HALF, HALF), HALF)
-                        out_ref[:, cols] = held[stage][i, half, 0].astype(f32) + mine[0].astype(f32)
+                        write_out(i, half, held[stage][i, half, 0].astype(f32) + mine[0].astype(f32))
 
         return carry
 
@@ -948,33 +1121,64 @@
     for i in (n - 2, n - 1):
         for half in range(2):
             copy(0, i, half).wait_send()
-
-
-def scatter_product(lhs, rhs, tiles, heads):
-    rows, depth = lhs.shape
-    columns = rhs.shape[1]
-    n, rb = columns // (2 * HALF), rows // 32
+    rows_store.wait()
+
+
+def backward_scatter(
+    hidden, cotangent, live, flipped, gated_flipped, pv, gains, ph, inverse, pull, shared,
+    projected, mixed, grad_gated, states, w_in, rb,
+):
+    length, width = hidden.shape
+    columns = projected.shape[1]
+    wide = mixed.shape[1]
+    n_in, n_out = columns // (2 * HALF), width // HALF
+    n = n_in + n_out
+    blocks = length // BLK
     vmem = pl.BlockSpec(memory_space=pltpu.VMEM)
+    anywhere = pl.BlockSpec(memory_space=pl.ANY)
+    struct = jax.ShapeDtypeStruct
     return pl.pallas_call(
-        partial(scatter_kernel, n, rb),
-        out_shape=(
-            jax.ShapeDtypeStruct((rb, columns), f32),
-            jax.ShapeDtypeStruct(tiles.shape[1:], f32),
-            jax.ShapeDtypeStruct(heads.shape, f32),
+        partial(backward_kernel, n_in, n_out),
+        out_shape=[
+            struct((length, width), f32),
+            struct((rb, columns - 2 * KEY), f32),
+            struct((rb, KEY), f32),
+            struct((2 * rb, width), f32),
+            struct((8, KEY), f32),
+            struct((8, KEY), f32),
+        ],
+        in_specs=[vmem] * 17 + [anywhere] * 5,
+        out_specs=[anywhere] + [vmem] * 5,
+        scratch_shapes=[pltpu.VMEM((2, 2, 2, 16, rb, HALF), bf16)]
+        + [pltpu.VMEM((n if stage else EARLY, 2, 16 >> stage, rb, HALF), bf16) for stage in range(5)]
+        + [pltpu.VMEM((32 >> stage, 8, KEY), f32) for stage in range(6)]
+        + [pltpu.VMEM((5, 8, KEY), f32)] * 2
+        + [
+            pltpu.VMEM((2, 4, length, HALF), f32),
+            pltpu.VMEM((2, blocks, KEY, HALF), bf16),
+            pltpu.VMEM((2, width, 2 * HALF), bf16),
+            pltpu.VMEM((length, 3 * KEY), f32),
+            pltpu.VMEM((length, 2 * HALF), bf16),
+            pltpu.VMEM((length, width), f32),
+            pltpu.VMEM((8, HALF), f32),
+            pltpu.VMEM((8, wide), f32),
+            pltpu.VMEM((8, HALF), f32),
+            pltpu.VMEM((8, KEY), f32),
+            pltpu.VMEM((8, KEY), f32),
+            pltpu.VMEM((8, width), f32),
+        ]
+        + backward_scratch(length)
+        + [pltpu.SemaphoreType.DMA((n, 2, 5))] * 2
+        + [pltpu.SemaphoreType.DMA((2, 5))] * 2
+        + [pltpu.SemaphoreType.DMA((8, 2)), pltpu.SemaphoreType.DMA((1,))],
+        compiler_params=pltpu.CompilerParams(
+            collective_id=1, has_side_effects=True, vmem_limit_bytes=67043328
         ),
-        in_specs=[vmem] * 4,
-        out_specs=(vmem, vmem, vmem),
-        scratch_shapes=[pltpu.VMEM((2, 2, 2, 16, rb, HALF), bf16)]
-        + [pltpu.VMEM((n, 2, 16 >> stage, rb, HALF), bf16) for stage in range(5)]
-        + [pltpu.VMEM(((32 >> stage),) + tiles.shape[1:], f32) for stage in range(6)]
-        + [pltpu.VMEM((5,) + heads.shape, f32)] * 2
-        + [pltpu.SemaphoreType.DMA((n, 2, 5))] * 2
-        + [pltpu.SemaphoreType.DMA((2, 5))] * 2,
-        compiler_params=pltpu.CompilerParams(
-            collective_id=1, has_side_effects=True, vmem_limit_bytes=60 << 20
-        ),
-        name="scatter_product",
-    )(lhs, rhs, tiles, heads)
+        name="backward_scatter",
+    )(
+        hidden, cotangent, live, flipped, gated_flipped, pv, gains, ph, inverse, pull, *shared,
+        projected, mixed, grad_gated, states, w_in,
+    )
 
 
 def pre_norm_inverse(rows):
@@ -1027,10 +1231,6 @@
     ph = jnp.pad(jnp.stack([dt_bias, a_log]).astype(f32), ((0, 6), (0, KEY - heads)))
     skip_wide = jnp.repeat(skip_gain.astype(f32), HD)[None]
     live = (jnp.arange(length) < lengths[0]).astype(f32)[:, None]
-    rows_wide = hidden.astype(f32)
-    cot_wide = cotangent.astype(f32)
-    upstream = (cot_wide * live).astype(bf16)
-    inverse_one = pre_norm_inverse(rows_wide)
     if kernels:
         skip_rows = jnp.broadcast_to(skip_wide, (8, wide))
         (
@@ -1039,9 +1239,15 @@
         ) = gather_forward(
             hidden, cotangent, jnp.broadcast_to(live, (length, KEY)), packed, out_proj, tile, skip_rows, ph
         )
-        gain_one = gains[6]
-        grad_out = mm(gated_flipped, upstream)
+        input_grad, grad_in, grad_dt, grad_out, small_sum, head_sums = backward_scatter(
+            hidden, cotangent, jnp.broadcast_to(live, (length, KEY)), flipped, gated_flipped, pv, gains, ph,
+            inverse_two, pull, shared, projected, mixed, grad_gated, states, w_in, rows_in,
+        )
     else:
+        rows_wide = hidden.astype(f32)
+        cot_wide = cotangent.astype(f32)
+        upstream = (cot_wide * live).astype(bf16)
+        inverse_one = pre_norm_inverse(rows_wide)
         w_in, w_out = gather_rows(packed), gather_rows(out_proj)
         tiles = gather_rows(tile[None])
         whole = lambda rows, part: jnp.transpose(tiles[:, rows, :part], (1, 0, 2)).reshape(-1, parts * part)
@@ -1060,34 +1266,32 @@
         pull = jnp.sum(grad_gated * gain_two * product, axis=1, keepdims=True)
         pull = jnp.broadcast_to(inv * inv * inv * pull / wide, inverse_two.shape)
         grad_out = mm_tn(gated, upstream)
-    grad_proj, sums_v, sums_k, sums_h = mixer_backward(
-        projected, pv, ph, mixed, grad_gated, states, inverse_two, pull, shared
-    )
-    skip_grad = jnp.pad(jnp.sum(sums_v[6].reshape(heads, HD), axis=1), (0, KEY - heads))[None]
-    head_grads = jnp.concatenate([sums_h[:2], skip_grad, jnp.zeros((5, KEY), f32)], axis=0)
-
-    grad_normed = mm_nt(grad_proj, w_in)
-    scaled = grad_normed * gain_one[None, :]
-    row_sums = jnp.sum(scaled * rows_wide, axis=1, keepdims=True) / width
-    grad_rows = inverse_one * scaled - rows_wide * (inverse_one * inverse_one * inverse_one * row_sums)
-    input_grad = cot_wide + grad_rows
-    grad_gain_one = jnp.sum(grad_normed * rows_wide * inverse_one, axis=0, keepdims=True)
-
-    conv_grad = jnp.concatenate([sums_v[:5], sums_k[:5]], axis=1)
-    small = vector_tiles(conv_grad, sums_v[5:6], grad_gain_one, parts)
-    grad_out = scatter_rows(grad_out.astype(bf16)).astype(f32)
-    if kernels:
-        grad_in, small_sum, head_sums = scatter_product(flipped, grad_proj, small, head_grads)
-    else:
+        grad_proj, sums_v, sums_k, sums_h = mixer_backward(
+            projected, pv, ph, mixed, grad_gated, states, inverse_two, pull, shared
+        )
+        skip_grad = jnp.pad(jnp.sum(sums_v[6].reshape(heads, HD), axis=1), (0, KEY - heads))[None]
+        head_grads = jnp.concatenate([sums_h[:2], skip_grad, jnp.zeros((5, KEY), f32)], axis=0)
+
+        grad_normed = mm_nt(grad_proj, w_in)
+        scaled = grad_normed * gain_one[None, :]
+        row_sums = jnp.sum(scaled * rows_wide, axis=1, keepdims=True) / width
+        grad_rows = inverse_one * scaled - rows_wide * (inverse_one * inverse_one * inverse_one * row_sums)
+        input_grad = cot_wide + grad_rows
+        grad_gain_one = jnp.sum(grad_normed * rows_wide * inverse_one, axis=0, keepdims=True)
+
+        conv_grad = jnp.concatenate([sums_v[:5], sums_k[:5]], axis=1)
+        small = vector_tiles(conv_grad, sums_v[5:6], grad_gain_one, parts)
+        grad_out = scatter_rows(grad_out.astype(bf16)).astype(f32)
         head_sums = lax.psum(head_grads, AXES)
-        grad_in = scatter_rows(mm_tn(normed, grad_proj).astype(bf16)).astype(f32)
+        grad_all = scatter_rows(mm_tn(normed, grad_proj).astype(bf16)).astype(f32)
+        grad_in, grad_dt = grad_all[:, :columns], grad_all[:, columns:]
         small_sum = scatter_rows(small)[0]
     return (
         output,
         input_grad,
         small_sum[6, :rows_in],
-        grad_in[:, :columns],
-        grad_in[:, columns : columns + heads],
+        grad_in,
+        grad_dt[:, :heads],
         small_sum[:taps, :conv_part],
         small_sum[taps, :conv_part],
         head_sums[0, :heads],

time: 406 us -> 342 us (0.84)
  matrix products: 29.3 us -> 0 us
  between operations: 14.8 us -> 1.33 us
  Pallas kernels: 332 us -> 319 us
  other arithmetic: 11.5 us -> 3.29 us
    dot_general x2 -> x0, matrix products: 29.3 us -> none  [the longest x1 19.1 us: mm_nt(): lax.dot_general(a, b, (((1,), (1,)), ((), ())), preferred_element_type=f32)]
    pallas_call x2 -> x1, Pallas kernels: 169 us -> 156 us  [backward_scatter(): pl.pallas_call(partial(backward_kernel, n_in, n_out), out_shape=[struct((...]
    unnamed x11 -> x13, local copies, waits for them, and re-layouts: 1.17 us -> 7.25 us
    slice x5 -> x0, local copies, waits for them, and re-layouts: 5.45 us -> none  [the longest x1 2.51 us: shards(): grad_in[:, :columns]]
    add x1 -> x0, other arithmetic: 4.48 us -> none  [shards(): input_grad = cot_wide + grad_rows]
  transfers between devices with their start and end apart: 1 -> 0, of which waited for: 0 -> 0; matrix products, arithmetic and copies ran while one was open for 9% -> 0% of each run, Pallas kernels for 42% -> 0%
where the time goes in v4:
time: 342 us
  Pallas kernels  319 us (93%)
  local copies, waits for them, and re-layouts  18.3 us (5%)
    pallas_call x1, Pallas kernels, gather_forward(): pl.pallas_call(partial(forward_kernel, n_in, n_out), out_shape=[struct((w...  163 us
    pallas_call x1, Pallas kernels, backward_scatter(): pl.pallas_call(partial(backward_kernel, n_in, n_out), out_shape=[struct((...  156 us
    unnamed x13, local copies, waits for them, and re-layouts  7.25 us

profile of v4, /device:TPU:0, one launch (start us, length us, event | category | flops | bytes accessed | tf_op | source)
XLA Modules:
  0.0 341.7 jit_solution(13710640161220960855)
XLA Ops:
  1.3 0.7 pad_convert_fusion.3
  2.0 0.7 pad_convert_fusion.1
  2.6 0.7 pad_convert_fusion
  3.3 0.6 concatenate.7.tile_ref
  3.9 1.3 fusion.6.ph_ref
  5.2 0.7 broadcast_in_dim.15
  5.9 0.1 broadcast_in_dim.32
  6.0 0.7 broadcast_in_dim.33.skip_ref
  6.7 0.8 broadcast_in_dim.12.live_ref
  7.5 1.9 concatenate.6.w_ref
  9.4 163.0 %gather_forward.1 = (bf16[1536,6656]{1,0:T(8,128)(2,1)}, f32[512,6656]{1,0:T(8,128)}, f32[512,3072]{1,0:T(8,128)}, bf16[4,128,3072]{2,1,0:T(8,128)(2,1)}, bf16[3...) custom-call(bf16[512,1536]{1,0:T(8,128)(2,1)} %hidden_ref.3, ...), custom_call_target="tpu_custom_call" | custom-call | tf_op jit(solution)/shard_map/gather_forward/pallas_call | solution.py:784
  172.4 155.7 %backward_scatter.1 = (f32[512,1536]{1,0:T(8,128)}, f32[48,6400]{1,0:T(8,128)}, f32[48,128]{1,0:T(8,128)}, f32[96,1536]{1,0:T(8,128)}, f32[8,128]{1,0:T(8,128)}, /*index=5*/f32[8,128]{1,0:T(8,128)}) custom-call(bf16[512,1536]{1,0:T(8,128)(2,1)} %hidden_ref.3, bf16[512,1536]{1,0:T(8,128)(2,1)} %cot_ref.3, f32[512,128]{1,0:T(8,128)} %broadcast_in_dim.12.live_ref, ...), custom_call_target="tpu_custom_call" | custom-call | tf_op jit(solution)/shard_map/backward_scatter/pallas_call | solution.py:1140
  328.1 0.0 copy-start
  328.1 1.3 slice_bitcast_fusion
  329.5 1.2 slice_bitcast_fusion.4
  330.6 1.2 slice_bitcast_fusion.5
  331.8 1.3 slice.26
  333.1 1.3 slice_bitcast_fusion.1
  334.4 2.7 copy.31
  337.1 0.0 copy-done
  337.1 0.0 copy-start.1
  337.1 0.0 copy-start.3
  337.1 0.0 copy-start.2
  337.1 1.7 copy.32
  338.7 0.5 copy-done.1
  339.2 1.0 copy.33
  340.2 0.0 copy-done.3
  340.2 0.6 copy.34
  340.8 0.0 copy-done.2
  340.8 0.8 copy.35
  (3 shorter events, 0.0 us)
Async XLA Ops:
  328.1 9.0 %copy-start = (f32[512,1536]{1,0:T(8,128)S(1)}, f32[512,1536]{1,0:T(8,128)}, u32[]{:S(2)}) copy-start(f32[512,1536]{1,0:T(8,128)} %get-tuple-element.80) | copy-start | bytes 9437188
  337.1 2.1 copy-start.1
  337.1 3.2 copy-start.3
  337.1 3.8 %copy-start.2 = (f32[96,1536]{1,0:T(8,128)S(1)}, f32[96,1536]{1,0:T(8,128)}, u32[]{:S(2)}) copy-start(f32[96,1536]{1,0:T(8,128)} %get-tuple-element.90) | copy-start | bytes 1769476

commit v5 on v4

--- a/solution.py
+++ b/solution.py
@@ -488,17 +488,56 @@
 HALF = 256
 
 
+ORDERS = ("xylh", "yxlh", "lhxy")
+GATHER_WAITS = (2, 4, 8, 13, 15)
+SCATTER_WAITS = (2, 6, 10, 14, 18)
+
+
 def places():
     d, f = lax.axis_index("dp"), lax.axis_index("fsdp")
-    z, x, y, c = d // 2, d % 2, f // 2, f % 2
-    over_core = (d, y * 2 + 1 - c)
-    over_x = (z * 2 + 1 - x, f)
-    over_y = (d, (1 - y) * 2 + c)
-    near = ((z + 1 - 2 * (z % 2)) * 2 + x, f)
-    far = (((z + 2) % 4) * 2 + x, f)
-    peers = ((over_core, over_x, over_y, near, far), (over_core, over_y, over_x, near, far))
-    own = ((c, x, y, z % 2, z // 2), (c, y, x, z % 2, z // 2))
-    return peers, own
+    bits = {"x": d % 2, "y": f // 2, "l": d // 2 % 2, "h": d // 4, "c": f % 2}
+    far = {"x": (1, 0), "y": (0, 2), "l": (2, 0), "h": (4, 0), "c": (0, 1)}
+    hops = {k: tuple(w * (1 - 2 * bits[k]) if w else 0 for w in far[k]) for k in far}
+    return d, f, bits, hops
+
+
+def kind_of(u):
+    r = lax.rem(u, 9)
+    along_y = (r == 1) | (r == 3) | (r == 6) | ((r == 7) & (lax.rem(u // 9, 2) == 1))
+    return jnp.where((r == 4) | (r == 8), 2, jnp.where(along_y, 1, 0))
+
+
+def pick(kind, values):
+    if isinstance(kind, int):
+        return values[kind]
+    if all(v is values[0] for v in values):
+        return values[0]
+    return jnp.where(kind == 0, values[0], jnp.where(kind == 1, values[1], values[2]))
+
+
+def exchange(place, kind, stage):
+    d, f, bits, hops = place
+    axes = "ccc" if stage == 0 else [order[stage - 1] for order in ORDERS]
+    side = pick(kind, [bits[a] for a in axes])
+    return side, (d + pick(kind, [hops[a][0] for a in axes]), f + pick(kind, [hops[a][1] for a in axes]))
+
+
+def strides(kind):
+    return {a: pick(kind, [8 >> order.index(a) for order in ORDERS]) for a in "xylh"}
+
+
+def position(kind, bits):
+    step = strides(kind)
+    return sum(bits[a] * step[a] for a in "xylh")
+
+
+def all_positions(kind):
+    step = strides(kind)
+    out = []
+    for i in range(32):
+        bits = {"x": i // 4 % 2, "y": i // 2 % 2, "l": i // 8 % 2, "h": i // 16}
+        out.append((i % 2, sum(step[a] for a in "xylh" if bits[a])))
+    return out
 
 
 def greet(partners):
@@ -506,12 +545,6 @@
     for partner in partners:
         pl.semaphore_signal(barrier, inc=1, device_id=partner, device_id_type=MESH)
     pl.semaphore_wait(barrier, len(partners))
-
-
-def block_order(half, i):
-    z, x, y, c = i // 8, i // 4 % 2, i // 2 % 2, i % 2
-    first, second = (x, y) if half == 0 else (y, x)
-    return c, first * 8 + second * 4 + z % 2 * 2 + z // 2
 
 
 def spread_lanes(tiles, width, lane, count):
@@ -527,9 +560,10 @@
 
 
 def forward_kernel(
-    n_in, n_out, hidden_ref, cot_ref, live_ref, w_ref, wo_ref, tile_ref, skip_ref, ph_ref,
+    n_in, n_out, lengths_ref, hidden_ref, cot_ref, w_ref, wd_ref, wo_ref, conv_ref, shift_ref, gate_ref, pre_ref,
+    dt_ref, log_ref, skip_ref,
     w_out, proj_out, mixed_out, states_out, flipped_gated_out, gg_out,
-    out_ref, flipped_ref, pv_ref, gain, r_ref, c_ref, s_ref, st_ref, hl_ref, ehl_ref, kb_ref, kt_ref, sc_ref,
+    out_ref, flipped_ref, live_ref, ph_ref, pv_ref, gain, r_ref, c_ref, s_ref, st_ref, hl_ref, ehl_ref, kb_ref, kt_ref, sc_ref,
     held, tiles, w_stage, wo_stage, proj_stage, mixed_stage, states_stage, flip_stage, normed, gated, big,
     pad, padk, sg, hcar, ssq, dots,
     send, recv, tile_sem, out_sem,
@@ -538,35 +572,38 @@
     length, width = hidden_ref.shape
     wide = big.shape[1]
     n = n_in + n_out
-    peers, own = places()
-    greet(peers[0])
-    base = [sum(bit * (16 >> k) for k, bit in enumerate(own[h])) for h in range(2)]
+    place = places()
+    greet([exchange(place, 0, stage)[1] for stage in range(5)])
     count = (1, 2, 4, 8, 16)
 
     def columns(i, half):
         group = (i - 1) * HALF + half * wide
         return pl.ds(pl.multiple_of(jnp.where(i == 0, 2 * wide + half * HALF, group), HALF), HALF)
 
-    def copy(stage, i, half):
-        start = base[half] // count[stage] * count[stage]
-        block = held.at[i, half, pl.ds(start, count[stage])]
+    def own_at(kind):
+        return place[2]["c"] * 16 + position(kind, place[2])
+
+    def copy(stage, u):
+        kind = kind_of(u)
+        start = own_at(kind) // count[stage] * count[stage]
+        block = held.at[u, pl.ds(start, count[stage])]
         return pltpu.make_async_remote_copy(
             src_ref=block,
             dst_ref=block,
-            send_sem=send.at[i, half, stage],
-            recv_sem=recv.at[i, half, stage],
-            device_id=peers[half][4 - stage],
+            send_sem=send.at[u, stage],
+            recv_sem=recv.at[u, stage],
+            device_id=exchange(place, kind, 4 - stage)[1],
             device_id_type=MESH,
         )
 
     def tile_copy(stage):
-        block = tiles.at[pl.ds(base[0] // count[stage] * count[stage], count[stage])]
+        block = tiles.at[pl.ds(own_at(0) // count[stage] * count[stage], count[stage])]
         return pltpu.make_async_remote_copy(
             src_ref=block,
             dst_ref=block,
             send_sem=tile_sem.at[0, stage],
             recv_sem=tile_sem.at[1, stage],
-            device_id=peers[0][4 - stage],
+            device_id=exchange(place, 0, 4 - stage)[1],
             device_id_type=MESH,
         )
 
@@ -600,30 +637,49 @@
             flip_stage.at[k % 2], flipped_gated_out.at[k * HALF : (k + 1) * HALF], out_sem.at[6, k % 2]
         )
 
-    tiles[base[0]] = tile_ref[...]
+    tile = tiles.at[own_at(0)]
+    tile[...] = jnp.zeros((8, KEY), f32)
+    tile[0:4, 0 : conv_ref.shape[1]] = conv_ref[...].astype(f32)
+    tile[4:5, 0 : shift_ref.shape[1]] = shift_ref[...].astype(f32)
+    tile[5:6, 0 : gate_ref.shape[1]] = gate_ref[...].astype(f32)
+    tile[6:7, 0 : pre_ref.shape[1]] = pre_ref[...].astype(f32)
     tile_copy(0).start()
-
-    def land(i, carry):
-        for half in range(2):
-            held[i, half, base[half]] = w_ref[:, columns(i, half)]
+    heads = dt_ref.shape[1]
+    ph_ref[...] = jnp.zeros_like(ph_ref)
+    ph_ref[0:1, 0:heads] = dt_ref[...].astype(f32)
+    ph_ref[1:2, 0:heads] = log_ref[...].astype(f32)
+    ph_ref[2:3, 0:heads] = skip_ref[...].astype(f32)
+    live_ref[...] = jnp.where(iota((length, KEY), 0) < lengths_ref[0], 1.0, 0.0).astype(f32)
+
+    held[0, own_at(kind_of(0))] = w_ref[:, 2 * wide : 2 * wide + HALF]
+    held[1, own_at(kind_of(1))] = jnp.zeros((rb, HALF), bf16)
+    held[1, own_at(kind_of(1)), :, 0:heads] = wd_ref[...]
+
+    def land(u, carry):
+        group = pl.ds(pl.multiple_of((u // 2 - 1) * HALF + lax.rem(u, 2) * wide, HALF), HALF)
+        held[u, own_at(kind_of(u))] = w_ref[:, group]
         return carry
 
-    lax.fori_loop(0, n_in, land, 0)
-    for j in range(n_out):
-        for half in range(2):
-            held[n_in + j, half, base[half]] = wo_ref[half * rb : (half + 1) * rb, j * HALF : (j + 1) * HALF]
-
-    def keys_chunk(slot):
+    lax.fori_loop(2, 2 * n_in, land, 0)
+    for u in range(2 * n_out):
+        rows = slice(u % 2 * rb, (u % 2 + 1) * rb)
+        held[2 * n_in + u, own_at(kind_of(2 * n_in + u))] = wo_ref[rows, u // 2 * HALF : (u // 2 + 1) * HALF]
+
+    def first_chunk():
         lane = iota((8, KEY), 1)
         row = iota((8, KEY), 0)
-        order = [tiles[c * 16 + at] for c, at in (block_order(0, i) for i in range(32))]
+        order = [tiles[c * 16 + at] for c, at in all_positions(0)]
         conv = spread_lanes(order, (wide + 2 * KEY) // 32, lane, wide // KEY + 2)
         gate = spread_lanes(order, wide // 32, lane, wide // KEY)
         pre = spread_lanes(order, width // 32, lane, width // KEY)
+        skips = split(jnp.broadcast_to(ph_ref[2:3], (8, KEY)))
         for k, tile in enumerate(conv):
             cols = slice(k * KEY, (k + 1) * KEY)
             if k < wide // KEY:
-                tile = jnp.where(row == 5, gate[k], jnp.where(row == 6, skip_ref[:, cols], tile))
+                if k % 2 == 0:
+                    skip = mm(skips, expander(k // 2))
+                skip_part = skip[:, k % 2 * KEY : (k % 2 + 1) * KEY]
+                tile = jnp.where(row == 5, gate[k], jnp.where(row == 6, skip_part, tile))
             pv_ref[:, cols] = tile
         for k, tile in enumerate(pre):
             gain[:, k * KEY : (k + 1) * KEY] = tile
@@ -633,7 +689,8 @@
             rows = (values * lax.rsqrt(mean + epsilon) * gain[6:7]).astype(bf16)
             normed[k : k + KEY] = rows
             flipped_ref[:, k : k + KEY] = rows.T
-        project(slot)
+
+    def keys_chunk(slot):
         forward_shared(
             proj_stage.at[slot, :, 0:HALF], proj_stage.at[slot, :, HALF : HALF + KEY], pv_ref, wide, ph_ref,
             s_ref, st_ref, hl_ref, ehl_ref, kb_ref, kt_ref, sc_ref, padk,
@@ -648,7 +705,6 @@
             proj_stage[slot, :, cols] = mm(normed[...], w_stage[slot, :, cols])
 
     def group_chunk(slot, g):
-        project(slot)
         forward_group(
             g, proj_stage.at[slot, :, 0:HALF], proj_stage.at[slot, :, HALF : 2 * HALF], pv_ref,
             s_ref, st_ref, hl_ref, ehl_ref, kb_ref, kt_ref, sc_ref,
@@ -670,18 +726,23 @@
         for k in range(wide // HALF - 2, wide // HALF):
             flip_store(k).wait()
 
-    def out_chunk(i):
+    def out_chunk_first(i):
         j = i - n_in
-        for b in range(32):
-            for half in range(2):
-                c, at = block_order(half, b)
-                wo_stage[(2 * b + half) * rb : (2 * b + half + 1) * rb] = held[i, half, c * 16 + at]
+        for half in range(2):
+            for b, (c, at) in enumerate(all_positions(kind_of(2 * i + half))):
+                wo_stage[(2 * b + half) * rb : (2 * b + half + 1) * rb] = held[2 * i + half, c * 16 + at]
         cols = pl.ds(pl.multiple_of(j * HALF, HALF), HALF)
         branch = mm(gated[...], wo_stage[...])
         live = jnp.concatenate([live_ref[...]] * (HALF // KEY), axis=1)
         out_ref[:, cols] = (hidden_ref[:, cols].astype(f32) + live * branch).astype(bf16)
         upstream = (cot_ref[:, cols].astype(f32) * live).astype(bf16)
         dots[...] += upstream.astype(f32) * branch
+
+    def out_chunk_second(i):
+        j = i - n_in
+        cols = pl.ds(pl.multiple_of(j * HALF, HALF), HALF)
+        live = jnp.concatenate([live_ref[...]] * (HALF // KEY), axis=1)
+        upstream = (cot_ref[:, cols].astype(f32) * live).astype(bf16)
         for q in range(0, wide, 512):
             more = mm_nt(upstream, wo_stage[q : q + 512])
 
@@ -693,7 +754,7 @@
             def _():
                 big[:, q : q + 512] += more
 
-    def consume(i):
+    def consume_first(i):
         slot = lax.rem(i, 2)
 
         @pl.when(i < n_in)
@@ -704,63 +765,82 @@
                     store.wait()
 
             for half in range(2):
-                for b in range(32):
-                    c, at = block_order(half, b)
-                    w_stage[slot, b * rb : (b + 1) * rb, half * HALF : (half + 1) * HALF] = held[i, half, c * 16 + at]
+                for b, (c, at) in enumerate(all_positions(kind_of(2 * i + half))):
+                    w_stage[slot, b * rb : (b + 1) * rb, half * HALF : (half + 1) * HALF] = held[
+                        2 * i + half, c * 16 + at
+                    ]
 
             @pl.when(i == 0)
             def _():
-                keys_chunk(slot)
-
-            @pl.when(i > 0)
-            def _():
-                @pl.when(i >= 3)
-                def _():
-                    for store in group_stores(i - 2):
-                        store.wait()
-
-                group_chunk(slot, i - 1)
-                for store in group_stores(i):
-                    store.start()
-
+                first_chunk()
+
+            project(slot)
             for store in weight_stores(i):
                 store.start()
 
-            @pl.when(i == n_in - 1)
+        @pl.when(i >= n_in)
+        def _():
+            out_chunk_first(i)
+
+    def consume_second(i):
+        slot = lax.rem(i, 2)
+
+        @pl.when(i == 0)
+        def _():
+            keys_chunk(slot)
+
+        @pl.when((i > 0) & (i < n_in))
+        def _():
+            @pl.when(i >= 3)
             def _():
-                finish_groups()
+                for store in group_stores(i - 2):
+                    store.wait()
+
+            group_chunk(slot, i - 1)
+            for store in group_stores(i):
+                store.start()
+
+        @pl.when(i == n_in - 1)
+        def _():
+            finish_groups()
 
         @pl.when(i >= n_in)
         def _():
-            out_chunk(i)
+            out_chunk_second(i)
 
     def tick(t, carry):
-        @pl.when(t < n)
-        def _():
-            for half in range(2):
-                copy(0, t, half).start()
+        @pl.when(t < 2 * n)
+        def _():
+            copy(0, t).start()
 
         for stage in range(5):
-            i = t - stage - 1
-
-            @pl.when(i == 0)
+            u = t - GATHER_WAITS[stage]
+
+            @pl.when(u == 0)
             def _(stage=stage):
                 tile_copy(stage).wait()
                 if stage < 4:
                     tile_copy(stage + 1).start()
 
-            @pl.when((i >= 0) & (i < n))
-            def _(stage=stage, i=i):
-                for half in range(2):
-                    copy(stage, i, half).wait()
-                    if stage < 4:
-                        copy(stage + 1, i, half).start()
-                if stage == 4:
-                    consume(i)
+            @pl.when((u >= 0) & (u < 2 * n))
+            def _(stage=stage, u=u):
+                copy(stage, u).wait()
+                if stage < 4:
+                    copy(stage + 1, u).start()
+
+        u = t - GATHER_WAITS[4]
+
+        @pl.when((u >= 1) & (lax.rem(u, 2) == 1))
+        def _():
+            consume_first(u // 2)
+
+        @pl.when((u >= 2) & (lax.rem(u, 2) == 0))
+        def _():
+            consume_second(u // 2 - 1)
 
         return carry
 
-    lax.fori_loop(0, n + 5, tick, 0)
+    lax.fori_loop(0, 2 * n + GATHER_WAITS[4] + 1, tick, 0)
     whole = pltpu.make_async_copy(big, gg_out, out_sem.at[6, 0])
     whole.start()
     pull = jnp.sum(dots[...], axis=1, keepdims=True) / wide
@@ -771,9 +851,10 @@
     whole.wait()
 
 
-def gather_forward(hidden, cotangent, live, shard, out_shard, tile, skip_rows, ph):
+def gather_forward(lengths, hidden, cotangent, shard, dt_shard, out_shard, *vectors):
     length, width = hidden.shape
-    rb, columns = shard.shape
+    rb = shard.shape[0]
+    columns = shard.shape[1] + 2 * KEY
     wide = out_shard.shape[0] * 32
     n_in, n_out = columns // (2 * HALF), width // HALF
     blocks = length // BLK
@@ -792,16 +873,18 @@
             struct((length, wide), f32),
             struct((length, width), bf16),
             struct((width, length), bf16),
+            struct((length, KEY), f32),
+            struct((8, KEY), f32),
             struct((8, wide + 2 * KEY), f32),
             struct((8, width), f32),
             struct((length, KEY), f32),
             struct((length, KEY), f32),
         ]
         + shared,
-        in_specs=[vmem] * 8,
-        out_specs=[anywhere] * 6 + [vmem] * (6 + len(shared)),
+        in_specs=[pl.BlockSpec(memory_space=pltpu.SMEM)] + [vmem] * (5 + len(vectors)),
+        out_specs=[anywhere] * 6 + [vmem] * (8 + len(shared)),
         scratch_shapes=[
-            pltpu.VMEM((n_in + n_out, 2, 32, rb, HALF), bf16),
+            pltpu.VMEM((2 * (n_in + n_out), 32, rb, HALF), bf16),
             pltpu.VMEM((32, 8, KEY), f32),
             pltpu.VMEM((2, width, 2 * HALF), bf16),
             pltpu.VMEM((wide, HALF), bf16),
@@ -818,8 +901,8 @@
             pltpu.VMEM((KEY, GC), f32),
             pltpu.VMEM((length, KEY), f32),
             pltpu.VMEM((length, HALF), f32),
-            pltpu.SemaphoreType.DMA((n_in + n_out, 2, 5)),
-            pltpu.SemaphoreType.DMA((n_in + n_out, 2, 5)),
+            pltpu.SemaphoreType.DMA((2 * (n_in + n_out), 5)),
+            pltpu.SemaphoreType.DMA((2 * (n_in + n_out), 5)),
             pltpu.SemaphoreType.DMA((2, 5)),
             pltpu.SemaphoreType.DMA((7, 2)),
         ],
@@ -827,10 +910,10 @@
             collective_id=2, has_side_effects=True, vmem_limit_bytes=63 << 20
         ),
         name="gather_forward",
-    )(hidden, cotangent, live, shard, out_shard, tile, skip_rows, ph)
-
-
-EARLY = 6
+    )(lengths, hidden, cotangent, shard, dt_shard, out_shard, *vectors)
+
+
+EARLY = 7
 
 
 def gather_lanes(row_tiles, width, lane, i):
@@ -860,10 +943,10 @@
     groups = n_in - 1
     keys_tick = n - 2
     shared = (s_ref, st_ref, hl_ref, ehl_ref, kb_ref, kt_ref, sc_ref)
-    peers, own = places()
+    place = places()
     held = (r0, r1, r2, r3, r4)
     tile_source = (tiles, t0, t1, t2, t3, t4)
-    greet(peers[0])
+    greet([exchange(place, 0, stage)[1] for stage in range(5)])
 
     def is_out(t):
         return ((t < 3 * n_out - 3) & (lax.rem(t, 3) == 0)) | (t == n - 1)
@@ -911,36 +994,37 @@
             dst_ref=sums_in.at[stage],
             send_sem=sums_sem.at[0, stage],
             recv_sem=sums_sem.at[1, stage],
-            device_id=peers[0][stage],
+            device_id=exchange(place, 0, stage)[1],
             device_id_type=MESH,
         )
 
     def tile_copy(stage):
         count = 16 >> stage
         return pltpu.make_async_remote_copy(
-            src_ref=tile_source[stage].at[pl.ds((1 - own[0][stage]) * count, count)],
+            src_ref=tile_source[stage].at[pl.ds((1 - exchange(place, 0, stage)[0]) * count, count)],
             dst_ref=tile_source[stage + 1],
             send_sem=tile_sem.at[0, stage],
             recv_sem=tile_sem.at[1, stage],
-            device_id=peers[0][stage],
+            device_id=exchange(place, 0, stage)[1],
             device_id_type=MESH,
         )
 
-    def place(stage, i):
-        return lax.rem(i, EARLY) if stage == 0 else i
-
-    def copy(stage, i, half):
+    def spot(stage, u):
+        return lax.rem(u, 2 * EARLY) if stage == 0 else u
+
+    def copy(stage, u):
         count = 16 >> stage
+        side, partner = exchange(place, kind_of(u), stage)
         if stage == 0:
-            src = parts.at[lax.rem(i, 2), 1 - own[half][0], half]
+            src = parts.at[lax.rem(u // 2, 2), 1 - side, lax.rem(u, 2)]
         else:
-            src = held[stage - 1].at[place(stage - 1, i), half, pl.ds((1 - own[half][stage]) * count, count)]
+            src = held[stage - 1].at[spot(stage - 1, u), pl.ds((1 - side) * count, count)]
         return pltpu.make_async_remote_copy(
             src_ref=src,
-            dst_ref=held[stage].at[place(stage, i), half],
-            send_sem=send.at[i, half, stage],
-            recv_sem=recv.at[i, half, stage],
-            device_id=peers[half][stage],
+            dst_ref=held[stage].at[spot(stage, u)],
+            send_sem=send.at[u, stage],
+            recv_sem=recv.at[u, stage],
+            device_id=partner,
             device_id_type=MESH,
         )
 
@@ -948,7 +1032,9 @@
     skip_sum[...] = jnp.zeros_like(skip_sum)
     rows_grad[...] = jnp.zeros_like(rows_grad)
 
-    def out_chunk(slot, j):
+    def out_chunk(slot, t):
+        j = out_index(t)
+        where = [all_positions(kind_of(2 * t + half)) for half in range(2)]
         cols = pl.ds(pl.multiple_of(j * HALF, HALF), HALF)
         live = jnp.concatenate([live_ref[...]] * (HALF // KEY), axis=1)
         upstream = (cot_ref[:, cols].astype(f32) * live).astype(bf16)
@@ -956,25 +1042,28 @@
             res = mm(gated_ref[z * 16 * rb : (z + 1) * 16 * rb], upstream)
             for b in range(8):
                 for half in range(2):
-                    c, at = block_order(half, z * 8 + b)
+                    c, at = where[half][z * 8 + b]
                     at_row = (2 * b + half) * rb
                     parts[slot, c, half, at] = res[at_row : at_row + rb].astype(bf16)
 
-    def weight_chunk(slot, g):
+    def weight_chunk(slot, t, g):
         for load in weight_loads(g):
             load.wait()
         at = lax.rem(g, 2)
         for half in range(2):
             right = dchunk[:, half * HALF : (half + 1) * HALF]
+            where = all_positions(kind_of(2 * t + half))
             for z in range(4):
                 res = mm(flipped_ref[z * 8 * rb : (z + 1) * 8 * rb], right)
                 for b in range(8):
-                    c, where = block_order(half, z * 8 + b)
-                    parts[slot, c, half, where] = res[b * rb : (b + 1) * rb].astype(bf16)
+                    c, to = where[z * 8 + b]
+                    parts[slot, c, half, to] = res[b * rb : (b + 1) * rb].astype(bf16)
         for k in range(0, width, 512):
             rows_grad[:, k : k + 512] += mm_nt(dchunk[...], w_stage[at, k : k + 512])
 
-    def group_chunk(slot, g):
+    def group_chunk(t):
+        g = group_index(t)
+
         for load in weight_loads(g + 1):
             load.start()
 
@@ -991,11 +1080,14 @@
             r_ref, c_ref, pv_ref, shared, dchunk.at[:, 0:HALF], dchunk.at[:, HALF : 2 * HALF], sv,
             pad, dpad, sg, dhcar, dsc, dkb, dsrow, dscol, ddt,
         )
+
+    def group_chunk_end(slot, t):
+        g = group_index(t)
         sv_all[:, pl.ds(pl.multiple_of(g * HALF, HALF), HALF)] = sv[...]
         skip_sum[...] += mm_hi(sv[...], reducer(g).astype(f32))
-        weight_chunk(slot, g)
-
-    def keys_chunk(slot):
+        weight_chunk(slot, t, g)
+
+    def keys_chunk():
         keys_load.wait()
         dchunk[:, 3 * KEY :] = jnp.zeros((length, KEY), bf16)
         backward_shared(
@@ -1003,9 +1095,11 @@
             dchunk.at[:, 0:HALF], dchunk.at[:, HALF : HALF + KEY], sk, sh,
             padk, dpadk, dsc, dkb, dsrow, dscol, ddt,
         )
-        weight_chunk(slot, groups)
+
+    def keys_chunk_end(slot):
+        weight_chunk(slot, keys_tick, groups)
         for half in range(2):
-            copy(0, keys_tick, half).start()
+            copy(0, 2 * keys_tick + half).start()
         gain = gain_ref[6:7]
         gain_sum[...] = jnp.zeros_like(gain_sum)
         for k in range(0, length, KEY):
@@ -1024,8 +1118,7 @@
         gate = conv
         conv = conv + [sk[:, 0:KEY], sk[:, KEY : 2 * KEY]]
         pre = [jnp.broadcast_to(gain_sum[0:1, k * KEY : (k + 1) * KEY], (8, KEY)) for k in range(width // KEY)]
-        for i in range(32):
-            c, at = block_order(0, i)
+        for i, (c, at) in enumerate(all_positions(0)):
             tile = gather_lanes(conv, (wide + 2 * KEY) // 32, lane, i)
             tile = jnp.where(row == 5, gather_lanes(gate, wide // 32, lane, i), tile)
             tiles[c * 16 + at] = jnp.where(row == 6, gather_lanes(pre, width // 32, lane, i), tile)
@@ -1033,60 +1126,83 @@
         sums[0] = jnp.where(row == 2, skip_sum[6:7], sh[...])
         sums_copy(0).start()
 
-    def write_out(i, half, value):
+    def write_out(u, value):
+        i, half = u // 2, lax.rem(u, 2)
+
         @pl.when(is_out(i))
         def _():
             cols = pl.ds(pl.multiple_of(out_index(i) * HALF, HALF), HALF)
-            out_ref[half * rb : (half + 1) * rb, cols] = value
+            out_ref[pl.ds(pl.multiple_of(half * rb, 16), rb), cols] = value
 
         @pl.when(jnp.logical_not(is_out(i)) & (i != keys_tick))
         def _():
             cols = pl.ds(pl.multiple_of(half * wide + group_index(i) * HALF, HALF), HALF)
             in_ref[:, cols] = value
 
-        @pl.when(i == keys_tick)
-        def _():
-            if half == 0:
-                in_ref[:, 2 * wide : 2 * wide + HALF] = value
-            else:
-                dt_ref[...] = value[:, :KEY]
-
-    def tick(t, carry):
-        @pl.when(t < n)
-        def _():
-            slot = lax.rem(t, 2)
-
-            @pl.when(t >= 2)
-            def _():
-                for half in range(2):
-                    copy(0, t - 2, half).wait_send()
-
-            @pl.when(is_out(t))
-            def _():
-                out_chunk(slot, out_index(t))
-
-            @pl.when(jnp.logical_not(is_out(t)) & (t != keys_tick))
-            def _():
-                group_chunk(slot, group_index(t))
-
-            @pl.when(t == keys_tick)
-            def _():
-                keys_chunk(slot)
-
-            @pl.when(t != keys_tick)
-            def _():
-                for half in range(2):
-                    copy(0, t, half).start()
+        @pl.when(u == 2 * keys_tick)
+        def _():
+            in_ref[:, 2 * wide : 2 * wide + HALF] = value
+
+        @pl.when(u == 2 * keys_tick + 1)
+        def _():
+            dt_ref[...] = value[:, :KEY]
+
+    def first_step(t):
+        @pl.when(jnp.logical_not(is_out(t)) & (t != keys_tick))
+        def _():
+            group_chunk(t)
+
+        @pl.when(t == keys_tick)
+        def _():
+            keys_chunk()
+
+    def second_step(t):
+        slot = lax.rem(t, 2)
+
+        @pl.when(t >= 2)
+        def _():
+            for half in range(2):
+                copy(0, 2 * (t - 2) + half).wait_send()
+
+        @pl.when(is_out(t))
+        def _():
+            out_chunk(slot, t)
+
+        @pl.when(jnp.logical_not(is_out(t)) & (t != keys_tick))
+        def _():
+            group_chunk_end(slot, t)
+
+        @pl.when(t == keys_tick)
+        def _():
+            keys_chunk_end(slot)
+
+        @pl.when(t != keys_tick)
+        def _():
+            for half in range(2):
+                copy(0, 2 * t + half).start()
+
+    def tick(step, carry):
+        t = step // 2
+
+        @pl.when((t < n) & (lax.rem(step, 2) == 0))
+        def _():
+            first_step(t)
+
+        @pl.when((t < n) & (lax.rem(step, 2) == 1))
+        def _():
+            second_step(t)
 
         for stage in range(5):
-            i = t - stage - 1
+            u = step - SCATTER_WAITS[stage]
             count = 16 >> stage
 
-            @pl.when(i == keys_tick)
+            @pl.when(u == 2 * keys_tick)
             def _(stage=stage, count=count):
                 sums_copy(stage).wait()
                 tile_copy(stage).wait()
-                total = tile_source[stage + 1][...] + tile_source[stage][pl.ds(own[0][stage] * count, count)]
+                total = tile_source[stage + 1][...] + tile_source[stage][
+                    pl.ds(exchange(place, 0, stage)[0] * count, count)
+                ]
                 if stage < 4:
                     sums[stage + 1] = sums[stage] + sums_in[stage]
                     sums_copy(stage + 1).start()
@@ -1096,31 +1212,28 @@
                     sums_ref[...] = sums[stage] + sums_in[stage]
                     tile_out[...] = total[0]
 
-            @pl.when((i >= 0) & (i < n))
-            def _(stage=stage, i=i, count=count):
-                for half in range(2):
-                    done = copy(stage, i, half)
-                    if stage == 0:
-                        done.wait_recv()
-                        mine = parts[lax.rem(i, 2), own[half][0], half]
-                    else:
-                        done.wait()
-                        mine = held[stage - 1][place(stage - 1, i), half, pl.ds(own[half][stage] * count, count)]
-                    if stage < 4:
-                        at = place(stage, i)
-                        held[stage][at, half] = (
-                            held[stage][at, half].astype(f32) + mine.astype(f32)
-                        ).astype(bf16)
-                        copy(stage + 1, i, half).start()
-                    else:
-                        write_out(i, half, held[stage][i, half, 0].astype(f32) + mine[0].astype(f32))
+            @pl.when((u >= 0) & (u < 2 * n))
+            def _(stage=stage, u=u, count=count):
+                done = copy(stage, u)
+                side, _ = exchange(place, kind_of(u), stage)
+                if stage == 0:
+                    done.wait_recv()
+                    mine = parts[lax.rem(u // 2, 2), side, lax.rem(u, 2)]
+                else:
+                    done.wait()
+                    mine = held[stage - 1][spot(stage - 1, u), pl.ds(side * count, count)]
+                if stage < 4:
+                    at = spot(stage, u)
+                    held[stage][at] = (held[stage][at].astype(f32) + mine.astype(f32)).astype(bf16)
+                    copy(stage + 1, u).start()
+                else:
+                    write_out(u, held[stage][u, 0].astype(f32) + mine[0].astype(f32))
 
         return carry
 
-    lax.fori_loop(0, n + 5, tick, 0)
-    for i in (n - 2, n - 1):
-        for half in range(2):
-            copy(0, i, half).wait_send()
+    lax.fori_loop(0, 2 * n + SCATTER_WAITS[4], tick, 0)
+    for u in range(2 * n - 4, 2 * n):
+        copy(0, u).wait_send()
     rows_store.wait()
 
 
@@ -1150,7 +1263,7 @@
         in_specs=[vmem] * 17 + [anywhere] * 5,
         out_specs=[anywhere] + [vmem] * 5,
         scratch_shapes=[pltpu.VMEM((2, 2, 2, 16, rb, HALF), bf16)]
-        + [pltpu.VMEM((n if stage else EARLY, 2, 16 >> stage, rb, HALF), bf16) for stage in range(5)]
+        + [pltpu.VMEM((2 * (n if stage else EARLY), 16 >> stage, rb, HALF), bf16) for stage in range(5)]
         + [pltpu.VMEM((32 >> stage, 8, KEY), f32) for stage in range(6)]
         + [pltpu.VMEM((5, 8, KEY), f32)] * 2
         + [
@@ -1168,7 +1281,7 @@
             pltpu.VMEM((8, width), f32),
         ]
         + backward_scratch(length)
-        + [pltpu.SemaphoreType.DMA((n, 2, 5))] * 2
+        + [pltpu.SemaphoreType.DMA((2 * n, 5))] * 2
         + [pltpu.SemaphoreType.DMA((2, 5))] * 2
         + [pltpu.SemaphoreType.DMA((8, 2)), pltpu.SemaphoreType.DMA((1,))],
         compiler_params=pltpu.CompilerParams(
@@ -1179,6 +1292,42 @@
         hidden, cotangent, live, flipped, gated_flipped, pv, gains, ph, inverse, pull, *shared,
         projected, mixed, grad_gated, states, w_in,
     )
+
+
+def finish_kernel(tile_ref, sums_ref, dt_in, *refs):
+    big_in, refs = refs[:4], refs[4:]
+    big_out, (pre_ref, dt_ref, conv_ref, shift_ref, bias_ref, log_ref, skip_ref, gate_ref) = refs[:4], refs[4:12]
+    stages, (sem,) = refs[12:16], refs[16:]
+    reads = [pltpu.make_async_copy(a, s, sem.at[0, k]) for k, (a, s) in enumerate(zip(big_in, stages))]
+    writes = [pltpu.make_async_copy(s, b, sem.at[1, k]) for k, (s, b) in enumerate(zip(stages, big_out))]
+    for read in reads:
+        read.start()
+    pre_ref[...] = tile_ref[6:7, 0 : pre_ref.shape[1]]
+    dt_ref[...] = dt_in[:, 0 : dt_ref.shape[1]]
+    conv_ref[...] = tile_ref[0:4, 0 : conv_ref.shape[1]]
+    shift_ref[...] = tile_ref[4:5, 0 : shift_ref.shape[1]]
+    gate_ref[...] = tile_ref[5:6, 0 : gate_ref.shape[1]]
+    for k, ref in enumerate((bias_ref, log_ref, skip_ref)):
+        ref[...] = sums_ref[k : k + 1, 0 : ref.shape[1]]
+    for read, write in zip(reads, writes):
+        read.wait()
+        write.start()
+    for write in writes:
+        write.wait()
+
+
+def finish(tile, sums, grad_dt, arrays, small_shapes):
+    vmem = pl.BlockSpec(memory_space=pltpu.VMEM)
+    anywhere = pl.BlockSpec(memory_space=pl.ANY)
+    return pl.pallas_call(
+        finish_kernel,
+        out_shape=[jax.ShapeDtypeStruct(a.shape, a.dtype) for a in arrays]
+        + [jax.ShapeDtypeStruct(shape, f32) for shape in small_shapes],
+        in_specs=[vmem] * 3 + [anywhere] * 4,
+        out_specs=[anywhere] * 4 + [vmem] * 8,
+        scratch_shapes=[pltpu.VMEM(a.shape, a.dtype) for a in arrays] + [pltpu.SemaphoreType.DMA((2, 4))],
+        name="finish",
+    )(tile, sums, grad_dt, *arrays)
 
 
 def pre_norm_inverse(rows):
@@ -1225,67 +1374,77 @@
     wide = gate_part * parts
     total = columns + 2 * KEY
 
+    if kernels:
+        rows = lambda *vectors: [v.reshape(1, -1) for v in vectors]
+        (
+            w_in, projected, mixed, states, gated_flipped, grad_gated, output, flipped, live, ph, pv, gains, inverse_two,
+            pull, *shared,
+        ) = gather_forward(
+            lengths, hidden, cotangent, in_proj, dt_proj, out_proj, conv_weight,
+            *rows(conv_bias, gate_gain, norm_gain, dt_bias, a_log, skip_gain),
+        )
+        input_grad, grad_in, grad_dt, grad_out, small_sum, head_sums = backward_scatter(
+            hidden, cotangent, live, flipped, gated_flipped, pv, gains, ph,
+            inverse_two, pull, shared, projected, mixed, grad_gated, states, w_in, rows_in,
+        )
+        output, input_grad, grad_in, grad_out, *small = finish(
+            small_sum, head_sums, grad_dt, (output, input_grad, grad_in, grad_out),
+            ((1, rows_in), (rows_in, heads), (taps, conv_part), (1, conv_part))
+            + ((1, heads),) * 3 + ((1, gate_part),),
+        )
+        pre, dt, conv, shift, bias, log, skip, gate = small
+        return (
+            output, input_grad, pre[0], grad_in, dt, conv, shift[0], bias[0], log[0], skip[0], gate[0], grad_out
+        )
+
     fill = jnp.zeros((rows_in, total - columns - heads), bf16)
     packed = jnp.concatenate([in_proj, dt_proj, fill], axis=1)
     tile = vector_tile(conv_weight, conv_bias, gate_gain, norm_gain)
     ph = jnp.pad(jnp.stack([dt_bias, a_log]).astype(f32), ((0, 6), (0, KEY - heads)))
     skip_wide = jnp.repeat(skip_gain.astype(f32), HD)[None]
     live = (jnp.arange(length) < lengths[0]).astype(f32)[:, None]
-    if kernels:
-        skip_rows = jnp.broadcast_to(skip_wide, (8, wide))
-        (
-            w_in, projected, mixed, states, gated_flipped, grad_gated, output, flipped, pv, gains, inverse_two, pull,
-            *shared,
-        ) = gather_forward(
-            hidden, cotangent, jnp.broadcast_to(live, (length, KEY)), packed, out_proj, tile, skip_rows, ph
-        )
-        input_grad, grad_in, grad_dt, grad_out, small_sum, head_sums = backward_scatter(
-            hidden, cotangent, jnp.broadcast_to(live, (length, KEY)), flipped, gated_flipped, pv, gains, ph,
-            inverse_two, pull, shared, projected, mixed, grad_gated, states, w_in, rows_in,
-        )
-    else:
-        rows_wide = hidden.astype(f32)
-        cot_wide = cotangent.astype(f32)
-        upstream = (cot_wide * live).astype(bf16)
-        inverse_one = pre_norm_inverse(rows_wide)
-        w_in, w_out = gather_rows(packed), gather_rows(out_proj)
-        tiles = gather_rows(tile[None])
-        whole = lambda rows, part: jnp.transpose(tiles[:, rows, :part], (1, 0, 2)).reshape(-1, parts * part)
-        conv_all = whole(slice(0, 5), conv_part)
-        gain_two = whole(slice(5, 6), gate_part)
-        gain_one = whole(slice(6, 7), rows_in)[0]
-        rest = jnp.concatenate([gain_two, skip_wide, jnp.zeros((1, wide), f32)], axis=0)
-        pv = jnp.concatenate([conv_all, jnp.pad(rest, ((0, 0), (0, 2 * KEY)))], axis=0)
-        normed = (rows_wide * inverse_one * gain_one[None, :]).astype(bf16)
-        projected = mm(normed, w_in)
-        mixed, product, states, inverse_two, *shared = mixer_forward(projected, pv, ph)
-        inv = inverse_two[:, :1]
-        gated = (product * inv * gain_two).astype(bf16)
-        output = (rows_wide + live * mm(gated, w_out)).astype(bf16)
-        grad_gated = mm_nt(upstream, w_out)
-        pull = jnp.sum(grad_gated * gain_two * product, axis=1, keepdims=True)
-        pull = jnp.broadcast_to(inv * inv * inv * pull / wide, inverse_two.shape)
-        grad_out = mm_tn(gated, upstream)
-        grad_proj, sums_v, sums_k, sums_h = mixer_backward(
-            projected, pv, ph, mixed, grad_gated, states, inverse_two, pull, shared
-        )
-        skip_grad = jnp.pad(jnp.sum(sums_v[6].reshape(heads, HD), axis=1), (0, KEY - heads))[None]
-        head_grads = jnp.concatenate([sums_h[:2], skip_grad, jnp.zeros((5, KEY), f32)], axis=0)
-
-        grad_normed = mm_nt(grad_proj, w_in)
-        scaled = grad_normed * gain_one[None, :]
-        row_sums = jnp.sum(scaled * rows_wide, axis=1, keepdims=True) / width
-        grad_rows = inverse_one * scaled - rows_wide * (inverse_one * inverse_one * inverse_one * row_sums)
-        input_grad = cot_wide + grad_rows
-        grad_gain_one = jnp.sum(grad_normed * rows_wide * inverse_one, axis=0, keepdims=True)
-
-        conv_grad = jnp.concatenate([sums_v[:5], sums_k[:5]], axis=1)
-        small = vector_tiles(conv_grad, sums_v[5:6], grad_gain_one, parts)
-        grad_out = scatter_rows(grad_out.astype(bf16)).astype(f32)
-        head_sums = lax.psum(head_grads, AXES)
-        grad_all = scatter_rows(mm_tn(normed, grad_proj).astype(bf16)).astype(f32)
-        grad_in, grad_dt = grad_all[:, :columns], grad_all[:, columns:]
-        small_sum = scatter_rows(small)[0]
+    rows_wide = hidden.astype(f32)
+    cot_wide = cotangent.astype(f32)
+    upstream = (cot_wide * live).astype(bf16)
+    inverse_one = pre_norm_inverse(rows_wide)
+    w_in, w_out = gather_rows(packed), gather_rows(out_proj)
+    tiles = gather_rows(tile[None])
+    whole = lambda rows, part: jnp.transpose(tiles[:, rows, :part], (1, 0, 2)).reshape(-1, parts * part)
+    conv_all = whole(slice(0, 5), conv_part)
+    gain_two = whole(slice(5, 6), gate_part)
+    gain_one = whole(slice(6, 7), rows_in)[0]
+    rest = jnp.concatenate([gain_two, skip_wide, jnp.zeros((1, wide), f32)], axis=0)
+    pv = jnp.concatenate([conv_all, jnp.pad(rest, ((0, 0), (0, 2 * KEY)))], axis=0)
+    normed = (rows_wide * inverse_one * gain_one[None, :]).astype(bf16)
+    projected = mm(normed, w_in)
+    mixed, product, states, inverse_two, *shared = mixer_forward(projected, pv, ph)
+    inv = inverse_two[:, :1]
+    gated = (product * inv * gain_two).astype(bf16)
+    output = (rows_wide + live * mm(gated, w_out)).astype(bf16)
+    grad_gated = mm_nt(upstream, w_out)
+    pull = jnp.sum(grad_gated * gain_two * product, axis=1, keepdims=True)
+    pull = jnp.broadcast_to(inv * inv * inv * pull / wide, inverse_two.shape)
+    grad_out = mm_tn(gated, upstream)
+    grad_proj, sums_v, sums_k, sums_h = mixer_backward(
+        projected, pv, ph, mixed, grad_gated, states, inverse_two, pull, shared
+    )
+    skip_grad = jnp.pad(jnp.sum(sums_v[6].reshape(heads, HD), axis=1), (0, KEY - heads))[None]
+    head_grads = jnp.concatenate([sums_h[:2], skip_grad, jnp.zeros((5, KEY), f32)], axis=0)
+
+    grad_normed = mm_nt(grad_proj, w_in)
+    scaled = grad_normed * gain_one[None, :]
+    row_sums = jnp.sum(scaled * rows_wide, axis=1, keepdims=True) / width
+    grad_rows = inverse_one * scaled - rows_wide * (inverse_one * inverse_one * inverse_one * row_sums)
+    input_grad = cot_wide + grad_rows
+    grad_gain_one = jnp.sum(grad_normed * rows_wide * inverse_one, axis=0, keepdims=True)
+
+    conv_grad = jnp.concatenate([sums_v[:5], sums_k[:5]], axis=1)
+    small = vector_tiles(conv_grad, sums_v[5:6], grad_gain_one, parts)
+    grad_out = scatter_rows(grad_out.astype(bf16)).astype(f32)
+    head_sums = lax.psum(head_grads, AXES)
+    grad_all = scatter_rows(mm_tn(normed, grad_proj).astype(bf16)).astype(f32)
+    grad_in, grad_dt = grad_all[:, :columns], grad_all[:, columns:]
+    small_sum = scatter_rows(small)[0]
     return (
         output,
         input_grad,

time: 342 us -> 295 us (0.86)
  Pallas kernels: 319 us -> 294 us
  local copies, waits for them, and re-layouts: 18.3 us -> 0 us
    pallas_call x1, Pallas kernels: 156 us -> 139 us  [backward_scatter(): pl.pallas_call(partial(backward_kernel, n_in, n_out), out_shape=[struct((...]
    pallas_call x1, Pallas kernels: 163 us -> 148 us  [gather_forward(): pl.pallas_call(partial(forward_kernel, n_in, n_out), out_shape=[struct((w...]
    unnamed x13 -> x0, local copies, waits for them, and re-layouts: 7.25 us -> none
    pallas_call x0 -> x1, Pallas kernels: none -> 6.03 us  [finish(): pl.pallas_call(finish_kernel, out_shape=[jax.ShapeDtypeStruct(a.shape, a....]
    squeeze x4 -> x0, local copies, waits for them, and re-layouts: 5.03 us -> none  [the longest x1 1.34 us: shards(): small_sum[5, :gate_part]]
where the time goes in v5:
time: 295 us
  Pallas kernels  294 us (100%)
    pallas_call x1, Pallas kernels, gather_forward(): pl.pallas_call(partial(forward_kernel, n_in, n_out), out_shape=[struct((w...  148 us
    pallas_call x1, Pallas kernels, backward_scatter(): pl.pallas_call(partial(backward_kernel, n_in, n_out), out_shape=[struct((...  139 us
    pallas_call x1, Pallas kernels, finish(): pl.pallas_call(finish_kernel, out_shape=[jax.ShapeDtypeStruct(a.shape, a....  6.03 us

profile of v5, /device:TPU:0, one launch (start us, length us, event | category | flops | bytes accessed | tf_op | source)
XLA Modules:
  0.0 295.2 jit_solution(12152019331616272536)
XLA Ops:
  1.3 148.4 %gather_forward.1 = (bf16[1536,6656]{1,0:T(8,128)(2,1)}, f32[512,6656]{1,0:T(8,128)}, f32[512,3072]{1,0:T(8,128)}, bf16[4,128,3072]{2,1,0:T(8,128)(2,1)}, bf16[3...) custom-call(s32[1]{0:T(128)S(6)} %copy.25.lengths_ref, ...), custom_call_target="tpu_custom_call" | custom-call | tf_op jit(solution)/shard_map/gather_forward/pallas_call | solution.py:865
  149.7 139.3 %backward_scatter.1 = (f32[512,1536]{1,0:T(8,128)}, f32[48,6400]{1,0:T(8,128)}, f32[48,128]{1,0:T(8,128)}, f32[96,1536]{1,0:T(8,128)}, f32[8,128]{1,0:T(8,128)}, /*index=5*/f32[8,128]{1,0:T(8,128)}) custom-call(bf16[512,1536]{1,0:T(8,128)(2,1)} %hidden_ref.3, bf16[512,1536]{1,0:T(8,128)(2,1)} %cot_ref.3, f32[512,128]{1,0:T(8,128)} %get-tuple-element.51.live_ref, ...), custom_call_target="tpu_custom_call" | custom-call | tf_op jit(solution)/shard_map/backward_scatter/pallas_call | solution.py:1253
  289.0 6.0 %finish.1 = (bf16[512,1536]{1,0:T(8,128)(2,1)}, f32[512,1536]{1,0:T(8,128)}, f32[48,6400]{1,0:T(8,128)}, f32[96,1536]{1,0:T(8,128)}, f32[1,48]{1,0:T(1,128)}, /*...) custom-call(f32[8,128]{1,0:T(8,128)} %get-tuple-element.71.tile_ref,, ...), custom_call_target="tpu_custom_call" | custom-call | tf_op jit(solution)/shard_map/finish/pallas_call | solution.py:1322

commit v6 on v5

--- a/solution.py
+++ b/solution.py
@@ -244,7 +244,7 @@
             zero = jnp.zeros_like(dyb)
             dy2 = jnp.concatenate([jnp.where(low, dyb, zero), jnp.where(low, zero, dyb)], axis=0)
             dm2 = mm_nt(dy2, xb)
-            ms = []
+            ms, scored = [], []
             for side in range(2):
                 j = 2 * q + side
                 spread = sg[rows, j : j + 1] - across[j : j + 1]
@@ -252,10 +252,12 @@
                 m = decay * sc_ref[k]
                 ms.append(m.astype(bf16))
                 dm = dm2[side * BLK : (side + 1) * BLK]
-                dsc[k] += decay * dm
-                e = jnp.where(strict, m * dm, 0.0)
+                part = decay * dm
+                scored.append(part)
+                e = jnp.where(strict, part * sc_ref[k], 0.0)
                 dsrow_k = jnp.where(col == g * GH + j, jnp.sum(e, axis=1, keepdims=True), dsrow_k)
                 ecols.append(jnp.sum(e, axis=0, keepdims=True))
+            dsc[k] += scored[0] + scored[1]
             dx = mm_tn(jnp.concatenate(ms, axis=0), dy2) + qq[:, cols] * txx[:, cols]
             dv = dx * dtx[:, cols] + par[6:7] * dy
             ddts.append((dx * v).astype(bf16))
@@ -489,7 +491,7 @@
 
 
 ORDERS = ("xylh", "yxlh", "lhxy")
-GATHER_WAITS = (2, 4, 8, 13, 15)
+GATHER_WAITS = (3, 6, 10, 14, 16)
 SCATTER_WAITS = (2, 6, 10, 14, 18)
 
 
@@ -566,7 +568,7 @@
     out_ref, flipped_ref, live_ref, ph_ref, pv_ref, gain, r_ref, c_ref, s_ref, st_ref, hl_ref, ehl_ref, kb_ref, kt_ref, sc_ref,
     held, tiles, w_stage, wo_stage, proj_stage, mixed_stage, states_stage, flip_stage, normed, gated, big,
     pad, padk, sg, hcar, ssq, dots,
-    send, recv, tile_sem, out_sem,
+    send, recv, tile_sem, out_sem, gg_sem,
 ):
     rb = w_ref.shape[0]
     length, width = hidden_ref.shape
@@ -728,31 +730,44 @@
 
     def out_chunk_first(i):
         j = i - n_in
+        side = pl.ds(pl.multiple_of(lax.rem(j, 2) * HALF, HALF), HALF)
         for half in range(2):
             for b, (c, at) in enumerate(all_positions(kind_of(2 * i + half))):
-                wo_stage[(2 * b + half) * rb : (2 * b + half + 1) * rb] = held[2 * i + half, c * 16 + at]
+                wo_stage[(2 * b + half) * rb : (2 * b + half + 1) * rb, side] = held[2 * i + half, c * 16 + at]
         cols = pl.ds(pl.multiple_of(j * HALF, HALF), HALF)
-        branch = mm(gated[...], wo_stage[...])
+        branch = mm(gated[...], wo_stage[:, side])
         live = jnp.concatenate([live_ref[...]] * (HALF // KEY), axis=1)
         out_ref[:, cols] = (hidden_ref[:, cols].astype(f32) + live * branch).astype(bf16)
         upstream = (cot_ref[:, cols].astype(f32) * live).astype(bf16)
-        dots[...] += upstream.astype(f32) * branch
+        pull = upstream.astype(f32) * branch
+        dots[...] += pull[:, :KEY] + pull[:, KEY:]
+
+    def gg_store(q):
+        cols = slice(q, q + 2 * HALF)
+        return pltpu.make_async_copy(big.at[:, cols], gg_out.at[:, cols], gg_sem.at[q // (2 * HALF)])
 
     def out_chunk_second(i):
         j = i - n_in
-        cols = pl.ds(pl.multiple_of(j * HALF, HALF), HALF)
-        live = jnp.concatenate([live_ref[...]] * (HALF // KEY), axis=1)
-        upstream = (cot_ref[:, cols].astype(f32) * live).astype(bf16)
-        for q in range(0, wide, 512):
-            more = mm_nt(upstream, wo_stage[q : q + 512])
-
-            @pl.when(j == 0)
-            def _():
-                big[:, q : q + 512] = more
-
-            @pl.when(j > 0)
-            def _():
-                big[:, q : q + 512] += more
+
+        @pl.when(lax.rem(j, 2) == 1)
+        def _():
+            cols = pl.ds(pl.multiple_of((j - 1) * HALF, 2 * HALF), 2 * HALF)
+            live = jnp.concatenate([live_ref[...]] * (2 * HALF // KEY), axis=1)
+            upstream = (cot_ref[:, cols].astype(f32) * live).astype(bf16)
+            for q in range(0, wide, 2 * HALF):
+                more = mm_nt(upstream, wo_stage[q : q + 2 * HALF])
+
+                @pl.when(j == 1)
+                def _():
+                    big[:, q : q + 2 * HALF] = more
+
+                @pl.when(j > 1)
+                def _():
+                    big[:, q : q + 2 * HALF] += more
+
+                @pl.when(j == n_out - 1)
+                def _():
+                    gg_store(q).start()
 
     def consume_first(i):
         slot = lax.rem(i, 2)
@@ -841,14 +856,13 @@
         return carry
 
     lax.fori_loop(0, 2 * n + GATHER_WAITS[4] + 1, tick, 0)
-    whole = pltpu.make_async_copy(big, gg_out, out_sem.at[6, 0])
-    whole.start()
     pull = jnp.sum(dots[...], axis=1, keepdims=True) / wide
     c_ref[...] = r_ref[...] * r_ref[...] * pull
     for i in (n_in - 2, n_in - 1):
         for store in weight_stores(i) + list(group_stores(i)):
             store.wait()
-    whole.wait()
+    for q in range(0, wide, 2 * HALF):
+        gg_store(q).wait()
 
 
 def gather_forward(lengths, hidden, cotangent, shard, dt_shard, out_shard, *vectors):
@@ -887,7 +901,7 @@
             pltpu.VMEM((2 * (n_in + n_out), 32, rb, HALF), bf16),
             pltpu.VMEM((32, 8, KEY), f32),
             pltpu.VMEM((2, width, 2 * HALF), bf16),
-            pltpu.VMEM((wide, HALF), bf16),
+            pltpu.VMEM((wide, 2 * HALF), bf16),
             pltpu.VMEM((2, length, 2 * HALF), f32),
             pltpu.VMEM((2, length, HALF), f32),
             pltpu.VMEM((2, blocks, KEY, HALF), bf16),
@@ -900,14 +914,15 @@
             pltpu.VMEM((length, KEY), f32),
             pltpu.VMEM((KEY, GC), f32),
             pltpu.VMEM((length, KEY), f32),
-            pltpu.VMEM((length, HALF), f32),
+            pltpu.VMEM((length, KEY), f32),
             pltpu.SemaphoreType.DMA((2 * (n_in + n_out), 5)),
             pltpu.SemaphoreType.DMA((2 * (n_in + n_out), 5)),
             pltpu.SemaphoreType.DMA((2, 5)),
             pltpu.SemaphoreType.DMA((7, 2)),
+            pltpu.SemaphoreType.DMA((wide // (2 * HALF),)),
         ],
         compiler_params=pltpu.CompilerParams(
-            collective_id=2, has_side_effects=True, vmem_limit_bytes=63 << 20
+            collective_id=2, has_side_effects=True, vmem_limit_bytes=67043328
         ),
         name="gather_forward",
     )(lengths, hidden, cotangent, shard, dt_shard, out_shard, *vectors)
@@ -1294,12 +1309,20 @@
     )
 
 
+PIECE = 128
+
+
 def finish_kernel(tile_ref, sums_ref, dt_in, *refs):
     big_in, refs = refs[:4], refs[4:]
     big_out, (pre_ref, dt_ref, conv_ref, shift_ref, bias_ref, log_ref, skip_ref, gate_ref) = refs[:4], refs[4:12]
     stages, (sem,) = refs[12:16], refs[16:]
-    reads = [pltpu.make_async_copy(a, s, sem.at[0, k]) for k, (a, s) in enumerate(zip(big_in, stages))]
-    writes = [pltpu.make_async_copy(s, b, sem.at[1, k]) for k, (s, b) in enumerate(zip(stages, big_out))]
+    reads, writes = [], []
+    for a, s, b in zip(big_in, stages, big_out):
+        for at in range(0, a.shape[0], PIECE):
+            rows = slice(at, min(at + PIECE, a.shape[0]))
+            k = len(reads)
+            reads.append(pltpu.make_async_copy(a.at[rows], s.at[rows], sem.at[0, k]))
+            writes.append(pltpu.make_async_copy(s.at[rows], b.at[rows], sem.at[1, k]))
     for read in reads:
         read.start()
     pre_ref[...] = tile_ref[6:7, 0 : pre_ref.shape[1]]
@@ -1325,7 +1348,9 @@
         + [jax.ShapeDtypeStruct(shape, f32) for shape in small_shapes],
         in_specs=[vmem] * 3 + [anywhere] * 4,
         out_specs=[anywhere] * 4 + [vmem] * 8,
-        scratch_shapes=[pltpu.VMEM(a.shape, a.dtype) for a in arrays] + [pltpu.SemaphoreType.DMA((2, 4))],
+        scratch_shapes=[pltpu.VMEM(a.shape, a.dtype) for a in arrays] + [
+            pltpu.SemaphoreType.DMA((2, sum(-(-a.shape[0] // PIECE) for a in arrays)))
+        ],
         name="finish",
     )(tile, sums, grad_dt, *arrays)
 

time: 295 us -> 286 us (0.969)
  Pallas kernels: 294 us -> 285 us
    pallas_call x1, Pallas kernels: 148 us -> 141 us  [gather_forward(): pl.pallas_call(partial(forward_kernel, n_in, n_out), out_shape=[struct((w...]
where the time goes in v6:
time: 286 us
  Pallas kernels  285 us (100%)
    pallas_call x1, Pallas kernels, gather_forward(): pl.pallas_call(partial(forward_kernel, n_in, n_out), out_shape=[struct((w...  141 us
    pallas_call x1, Pallas kernels, backward_scatter(): pl.pallas_call(partial(backward_kernel, n_in, n_out), out_shape=[struct((...  137 us
    pallas_call x1, Pallas kernels, finish(): pl.pallas_call(finish_kernel, out_shape=[jax.ShapeDtypeStruct(a.shape, a....  6.87 us

profile of v6, /device:TPU:0, one launch (start us, length us, event | category | flops | bytes accessed | tf_op | source)
XLA Modules:
  0.0 286.0 jit_solution(14540352499351753360)
XLA Ops:
  1.3 140.5 %gather_forward.1 = (bf16[1536,6656]{1,0:T(8,128)(2,1)}, f32[512,6656]{1,0:T(8,128)}, f32[512,3072]{1,0:T(8,128)}, bf16[4,128,3072]{2,1,0:T(8,128)(2,1)}, bf16[3...) custom-call(s32[1]{0:T(128)S(6)} %copy.25.lengths_ref, ...), custom_call_target="tpu_custom_call" | custom-call | tf_op jit(solution)/shard_map/gather_forward/pallas_call | solution.py:879
  141.8 137.1 %backward_scatter.1 = (f32[512,1536]{1,0:T(8,128)}, f32[48,6400]{1,0:T(8,128)}, f32[48,128]{1,0:T(8,128)}, f32[96,1536]{1,0:T(8,128)}, f32[8,128]{1,0:T(8,128)}, /*index=5*/f32[8,128]{1,0:T(8,128)}) custom-call(bf16[512,1536]{1,0:T(8,128)(2,1)} %hidden_ref.3, bf16[512,1536]{1,0:T(8,128)(2,1)} %cot_ref.3, f32[512,128]{1,0:T(8,128)} %get-tuple-element.51.live_ref, ...), custom_call_target="tpu_custom_call" | custom-call | tf_op jit(solution)/shard_map/backward_scatter/pallas_call | solution.py:1268
  279.0 6.9 %finish.1 = (bf16[512,1536]{1,0:T(8,128)(2,1)}, f32[512,1536]{1,0:T(8,128)}, f32[48,6400]{1,0:T(8,128)}, f32[96,1536]{1,0:T(8,128)}, f32[1,48]{1,0:T(1,128)}, /*...) custom-call(f32[8,128]{1,0:T(8,128)} %get-tuple-element.71.tile_ref,, ...), custom_call_target="tpu_custom_call" | custom-call | tf_op jit(solution)/shard_map/finish/pallas_call | solution.py:1345

commit v7 on v6

--- a/solution.py
+++ b/solution.py
@@ -562,18 +562,23 @@
 
 
 def forward_kernel(
-    n_in, n_out, lengths_ref, hidden_ref, cot_ref, w_ref, wd_ref, wo_ref, conv_ref, shift_ref, gate_ref, pre_ref,
+    n_in, n_out, lengths_ref, hidden_in, cot_in, w_ref, wd_ref, wo_ref, conv_ref, shift_ref, gate_ref, pre_ref,
     dt_ref, log_ref, skip_ref,
-    w_out, proj_out, mixed_out, states_out, flipped_gated_out, gg_out,
-    out_ref, flipped_ref, live_ref, ph_ref, pv_ref, gain, r_ref, c_ref, s_ref, st_ref, hl_ref, ehl_ref, kb_ref, kt_ref, sc_ref,
+    w_out, proj_out, mixed_out, states_out, flipped_gated_out, gg_out, out_out, flipped_out,
+    live_ref, ph_ref, pv_ref, gain, r_ref, c_ref, s_ref, st_ref, hl_ref, ehl_ref, kb_ref, kt_ref, sc_ref,
     held, tiles, w_stage, wo_stage, proj_stage, mixed_stage, states_stage, flip_stage, normed, gated, big,
-    pad, padk, sg, hcar, ssq, dots,
-    send, recv, tile_sem, out_sem, gg_sem,
+    pad, padk, sg, hcar, ssq, dots, hidden_ref, cot_ref, out_ref, flipped_ref,
+    send, recv, tile_sem, out_sem, gg_sem, row_sem,
 ):
     rb = w_ref.shape[0]
     length, width = hidden_ref.shape
     wide = big.shape[1]
     n = n_in + n_out
+    hidden_load = pltpu.make_async_copy(hidden_in, hidden_ref, row_sem.at[0])
+    cot_load = pltpu.make_async_copy(cot_in, cot_ref, row_sem.at[1])
+    flipped_store = pltpu.make_async_copy(flipped_ref, flipped_out, row_sem.at[2])
+    hidden_load.start()
+    cot_load.start()
     place = places()
     greet([exchange(place, 0, stage)[1] for stage in range(5)])
     count = (1, 2, 4, 8, 16)
@@ -685,12 +690,14 @@
             pv_ref[:, cols] = tile
         for k, tile in enumerate(pre):
             gain[:, k * KEY : (k + 1) * KEY] = tile
+        hidden_load.wait()
         for k in range(0, length, KEY):
             values = hidden_ref[k : k + KEY].astype(f32)
             mean = jnp.mean(values * values, axis=1, keepdims=True)
             rows = (values * lax.rsqrt(mean + epsilon) * gain[6:7]).astype(bf16)
             normed[k : k + KEY] = rows
             flipped_ref[:, k : k + KEY] = rows.T
+        flipped_store.start()
 
     def keys_chunk(slot):
         forward_shared(
@@ -728,8 +735,17 @@
         for k in range(wide // HALF - 2, wide // HALF):
             flip_store(k).wait()
 
+    def out_store(j):
+        cols = pl.ds(pl.multiple_of(j * HALF, HALF), HALF)
+        return pltpu.make_async_copy(out_ref.at[:, cols], out_out.at[:, cols], row_sem.at[3 + j])
+
     def out_chunk_first(i):
         j = i - n_in
+
+        @pl.when(j == 0)
+        def _():
+            cot_load.wait()
+
         side = pl.ds(pl.multiple_of(lax.rem(j, 2) * HALF, HALF), HALF)
         for half in range(2):
             for b, (c, at) in enumerate(all_positions(kind_of(2 * i + half))):
@@ -738,6 +754,7 @@
         branch = mm(gated[...], wo_stage[:, side])
         live = jnp.concatenate([live_ref[...]] * (HALF // KEY), axis=1)
         out_ref[:, cols] = (hidden_ref[:, cols].astype(f32) + live * branch).astype(bf16)
+        out_store(j).start()
         upstream = (cot_ref[:, cols].astype(f32) * live).astype(bf16)
         pull = upstream.astype(f32) * branch
         dots[...] += pull[:, :KEY] + pull[:, KEY:]
@@ -863,6 +880,9 @@
             store.wait()
     for q in range(0, wide, 2 * HALF):
         gg_store(q).wait()
+    flipped_store.wait()
+    for j in range(n_out):
+        out_store(j).wait()
 
 
 def gather_forward(lengths, hidden, cotangent, shard, dt_shard, out_shard, *vectors):
@@ -895,8 +915,8 @@
             struct((length, KEY), f32),
         ]
         + shared,
-        in_specs=[pl.BlockSpec(memory_space=pltpu.SMEM)] + [vmem] * (5 + len(vectors)),
-        out_specs=[anywhere] * 6 + [vmem] * (8 + len(shared)),
+        in_specs=[pl.BlockSpec(memory_space=pltpu.SMEM)] + [anywhere] * 2 + [vmem] * (3 + len(vectors)),
+        out_specs=[anywhere] * 8 + [vmem] * (6 + len(shared)),
         scratch_shapes=[
             pltpu.VMEM((2 * (n_in + n_out), 32, rb, HALF), bf16),
             pltpu.VMEM((32, 8, KEY), f32),
@@ -915,11 +935,16 @@
             pltpu.VMEM((KEY, GC), f32),
             pltpu.VMEM((length, KEY), f32),
             pltpu.VMEM((length, KEY), f32),
+            pltpu.VMEM((length, width), bf16),
+            pltpu.VMEM((length, width), bf16),
+            pltpu.VMEM((length, width), bf16),
+            pltpu.VMEM((width, length), bf16),
             pltpu.SemaphoreType.DMA((2 * (n_in + n_out), 5)),
             pltpu.SemaphoreType.DMA((2 * (n_in + n_out), 5)),
             pltpu.SemaphoreType.DMA((2, 5)),
             pltpu.SemaphoreType.DMA((7, 2)),
             pltpu.SemaphoreType.DMA((wide // (2 * HALF),)),
+            pltpu.SemaphoreType.DMA((3 + n_out,)),
         ],
         compiler_params=pltpu.CompilerParams(
             collective_id=2, has_side_effects=True, vmem_limit_bytes=67043328
@@ -942,14 +967,15 @@
 
 
 def backward_kernel(
-    n_in, n_out, hidden_ref, cot_ref, live_ref, flipped_ref, gated_ref, pv_ref, gain_ref, ph_ref, r_ref, c_ref,
+    n_in, n_out, live_ref, pv_ref, gain_ref, ph_ref, r_ref, c_ref,
     s_ref, st_ref, hl_ref, ehl_ref, kb_ref, kt_ref, sc_ref,
-    proj_in, mixed_in, gg_in, states_in, w_in,
+    hidden_in, cot_in, flipped_in, gated_in, proj_in, mixed_in, gg_in, states_in, w_in,
     rows_out, in_ref, dt_ref, out_ref, tile_out, sums_ref,
     parts, r0, r1, r2, r3, r4, tiles, t0, t1, t2, t3, t4, sums, sums_in,
     stage_in, states_stage, w_stage, keys_stage, dchunk, rows_grad, sv, sv_all, sk, sh, skip_sum, gain_sum,
     pad, padk, dpad, dpadk, sg, dhcar, dsc, dkb, dsrow, dscol, ddt,
-    send, recv, tile_sem, sums_sem, in_sem, out_sem,
+    hidden_ref, cot_ref, flipped_ref, gated_ref,
+    send, recv, tile_sem, sums_sem, in_sem, out_sem, row_sem,
 ):
     length, width = hidden_ref.shape
     wide = mixed_in.shape[1]
@@ -958,6 +984,12 @@
     groups = n_in - 1
     keys_tick = n - 2
     shared = (s_ref, st_ref, hl_ref, ehl_ref, kb_ref, kt_ref, sc_ref)
+    gated_load = pltpu.make_async_copy(gated_in, gated_ref, row_sem.at[0])
+    cot_load = pltpu.make_async_copy(cot_in, cot_ref, row_sem.at[1])
+    flipped_load = pltpu.make_async_copy(flipped_in, flipped_ref, row_sem.at[2])
+    hidden_load = pltpu.make_async_copy(hidden_in, hidden_ref, row_sem.at[3])
+    for load in (gated_load, cot_load, flipped_load, hidden_load):
+        load.start()
     place = places()
     held = (r0, r1, r2, r3, r4)
     tile_source = (tiles, t0, t1, t2, t3, t4)
@@ -1115,6 +1147,7 @@
         weight_chunk(slot, keys_tick, groups)
         for half in range(2):
             copy(0, 2 * keys_tick + half).start()
+        hidden_load.wait()
         gain = gain_ref[6:7]
         gain_sum[...] = jnp.zeros_like(gain_sum)
         for k in range(0, length, KEY):
@@ -1179,6 +1212,15 @@
             for half in range(2):
                 copy(0, 2 * (t - 2) + half).wait_send()
 
+        @pl.when(t == 0)
+        def _():
+            gated_load.wait()
+            cot_load.wait()
+
+        @pl.when(t == 1)
+        def _():
+            flipped_load.wait()
+
         @pl.when(is_out(t))
         def _():
             out_chunk(slot, t)
@@ -1275,7 +1317,7 @@
             struct((8, KEY), f32),
             struct((8, KEY), f32),
         ],
-        in_specs=[vmem] * 17 + [anywhere] * 5,
+        in_specs=[vmem] * 13 + [anywhere] * 9,
         out_specs=[anywhere] + [vmem] * 5,
         scratch_shapes=[pltpu.VMEM((2, 2, 2, 16, rb, HALF), bf16)]
         + [pltpu.VMEM((2 * (n if stage else EARLY), 16 >> stage, rb, HALF), bf16) for stage in range(5)]
@@ -1296,20 +1338,26 @@
             pltpu.VMEM((8, width), f32),
         ]
         + backward_scratch(length)
+        + [
+            pltpu.VMEM((length, width), bf16),
+            pltpu.VMEM((length, width), bf16),
+            pltpu.VMEM((width, length), bf16),
+            pltpu.VMEM((wide, length), bf16),
+        ]
         + [pltpu.SemaphoreType.DMA((2 * n, 5))] * 2
         + [pltpu.SemaphoreType.DMA((2, 5))] * 2
-        + [pltpu.SemaphoreType.DMA((8, 2)), pltpu.SemaphoreType.DMA((1,))],
+        + [pltpu.SemaphoreType.DMA((8, 2)), pltpu.SemaphoreType.DMA((1,)), pltpu.SemaphoreType.DMA((4,))],
         compiler_params=pltpu.CompilerParams(
             collective_id=1, has_side_effects=True, vmem_limit_bytes=67043328
         ),
         name="backward_scatter",
     )(
-        hidden, cotangent, live, flipped, gated_flipped, pv, gains, ph, inverse, pull, *shared,
-        projected, mixed, grad_gated, states, w_in,
+        live, pv, gains, ph, inverse, pull, *shared,
+        hidden, cotangent, flipped, gated_flipped, projected, mixed, grad_gated, states, w_in,
     )
 
 
-PIECE = 128
+PIECE = 512
 
 
 def finish_kernel(tile_ref, sums_ref, dt_in, *refs):

time: 286 us -> 283 us (0.990)
  Pallas kernels: 285 us -> 281 us
where the time goes in v7:
time: 283 us; the launch traced here: 282 us
  Pallas kernels  281 us (99%)
    pallas_call x1, Pallas kernels, gather_forward(): pl.pallas_call(partial(forward_kernel, n_in, n_out), out_shape=[struct((w...  139 us
    pallas_call x1, Pallas kernels, backward_scatter(): pl.pallas_call(partial(backward_kernel, n_in, n_out), out_shape=[struct((...  136 us
    pallas_call x1, Pallas kernels, finish(): pl.pallas_call(finish_kernel, out_shape=[jax.ShapeDtypeStruct(a.shape, a....  6.03 us

profile of v7, /device:TPU:0, one launch (start us, length us, event | category | flops | bytes accessed | tf_op | source)
XLA Modules:
  0.0 282.5 jit_solution(8479984298175355716)
XLA Ops:
  1.3 138.7 %gather_forward.1 = (bf16[1536,6656]{1,0:T(8,128)(2,1)}, f32[512,6656]{1,0:T(8,128)}, f32[512,3072]{1,0:T(8,128)}, bf16[4,128,3072]{2,1,0:T(8,128)(2,1)}, bf16[3...) custom-call(s32[1]{0:T(128)S(6)} %copy.25.lengths_ref, ...), custom_call_target="tpu_custom_call" | custom-call | tf_op jit(solution)/shard_map/gather_forward/pallas_call | solution.py:899
  140.0 136.3 %backward_scatter.1 = (f32[512,1536]{1,0:T(8,128)}, f32[48,6400]{1,0:T(8,128)}, f32[48,128]{1,0:T(8,128)}, f32[96,1536]{1,0:T(8,128)}, f32[8,128]{1,0:T(8,128)}, /*index=5*/f32[8,128]{1,0:T(8,128)}) custom-call(f32[512,128]{1,0:T(8,128)} %get-tuple-element.51.live_ref, f32[8,3328]{1,0:T(8,128)} %get-tuple-element.52.pv_ref, ...), custom_call_target="tpu_custom_call" | custom-call | tf_op jit(solution)/shard_map/backward_scatter/pallas_call | solution.py:1310
  276.3 6.0 %finish.1 = (bf16[512,1536]{1,0:T(8,128)(2,1)}, f32[512,1536]{1,0:T(8,128)}, f32[48,6400]{1,0:T(8,128)}, f32[96,1536]{1,0:T(8,128)}, f32[1,48]{1,0:T(1,128)}, /*...) custom-call(f32[8,128]{1,0:T(8,128)} %get-tuple-element.71.tile_ref,, ...), custom_call_target="tpu_custom_call" | custom-call | tf_op jit(solution)/shard_map/finish/pallas_call | solution.py:1393
